TPU v7x, 8 devices: a whole 2x2x1 slice. The times are simulated.
8 devices in a mesh: dp: 1 (over z), tp: 8 (over y, x, core).
Axes of the slice: x: 2, y: 2, z: 1, core: 2. Of those that a mesh axis runs over, the one named last changes fastest.
Arguments:
- tokens: int32 [512, 5], P('dp')
- start_pos: int32 [512], P('dp')
- kv_cache: bfloat16 [2, 2, 512, 128, 8, 64], P(None, None, 'dp', None, 'tp')
- expert_ids: int32 [4, 2, 512, 8], P(None, None, 'dp')
- embed: bfloat16 [49152, 1536], P('tp')
- norm_gain: float32 [5, 1536], replicated
- w_query: bfloat16 [2, 1536, 1536], P(None, None, 'tp')
- w_key: bfloat16 [2, 1536, 512], P(None, None, 'tp')
- w_value: bfloat16 [2, 1536, 512], P(None, None, 'tp')
- w_out: bfloat16 [2, 1536, 1536], P(None, 'tp')
- w_router: bfloat16 [2, 1536, 40], replicated
- w_gate: bfloat16 [2, 40, 1536, 512], P(None, 'tp')
- w_up: bfloat16 [2, 40, 1536, 512], P(None, 'tp')
- w_down: bfloat16 [2, 40, 512, 1536], P(None, 'tp')
Outputs:
- output 1: float32 [512, 4], P('dp')
- output 2: float32 [512, 49152], P('dp', 'tp')
- output 3: bfloat16 [2, 2, 512, 128, 8, 64], P(None, None, 'dp', None, 'tp')
All inputs are finite; a program needn't handle non-finite values.
Results may differ from a plain program's by a relative error of at most 0.0112274.
Values are sent between devices in bfloat16 or wider.
A program may use at most 1 GiB of HBM per device.

v0:
```python
import jax
import jax.numpy as jnp
from jax import lax
from jax.sharding import PartitionSpec as P

EMBED_MULT = 12.0
ATT_SCALE = 0.015625
RESID_MULT = 0.22
LOGIT_DIV = 6.0
NORM_EPS = 1e-6
ROPE_THETA = 10000.0


def rms_norm(hidden, gain):
    mean_sq = jnp.mean(hidden * hidden, axis=-1, keepdims=True)
    return (hidden * lax.rsqrt(mean_sq + NORM_EPS) * gain).astype(jnp.bfloat16)


def rotary(values, positions):
    head_dim = values.shape[-1]
    half_dim = head_dim // 2
    inv_freq = ROPE_THETA ** (-2.0 * jnp.arange(half_dim, dtype=jnp.float32) / head_dim)
    angles = positions.astype(jnp.float32)[:, None, None] * inv_freq
    cos_part = jnp.cos(angles)
    sin_part = jnp.sin(angles)
    first_half = values[..., :half_dim]
    second_half = values[..., half_dim:]
    return jnp.concatenate([first_half * cos_part - second_half * sin_part, second_half * cos_part + first_half * sin_part], axis=-1)


def attend(query, cache_keys, cache_vals, fresh_keys, fresh_vals, old_mask):
    old_scores = jnp.einsum('bkgh,bskh->bkgs', query, cache_keys, preferred_element_type=jnp.float32) * ATT_SCALE
    old_scores = jnp.where(old_mask[:, None, None, :], old_scores, -jnp.inf)
    new_scores = jnp.einsum('bkgh,jbkh->bkgj', query, fresh_keys, preferred_element_type=jnp.float32) * ATT_SCALE
    peak = jnp.maximum(jnp.max(old_scores, axis=-1, keepdims=True), jnp.max(new_scores, axis=-1, keepdims=True))
    old_weights = jnp.exp(old_scores - peak)
    new_weights = jnp.exp(new_scores - peak)
    total = jnp.sum(old_weights, axis=-1, keepdims=True) + jnp.sum(new_weights, axis=-1, keepdims=True)
    old_probs = (old_weights / total).astype(jnp.bfloat16)
    new_probs = (new_weights / total).astype(jnp.bfloat16)
    mixed = jnp.einsum('bkgs,bskh->bkgh', old_probs, cache_vals, preferred_element_type=jnp.float32) + jnp.einsum('bkgj,jbkh->bkgh', new_probs, fresh_vals, preferred_element_type=jnp.float32)
    return mixed.astype(jnp.bfloat16).reshape(mixed.shape[0], -1)


def expert_gates(normed, router_w, chosen_ids):
    num_experts = router_w.shape[1]
    router = jnp.dot(normed, router_w, preferred_element_type=jnp.float32)
    chosen = jnp.any(chosen_ids[:, :, None] == jnp.arange(num_experts)[None, None, :], axis=1)
    masked = jnp.where(chosen, router, -jnp.inf)
    weights = jnp.exp(masked - jnp.max(masked, axis=-1, keepdims=True))
    return weights / jnp.sum(weights, axis=-1, keepdims=True)


def expert_partial(normed, gates, gate_w, up_w, down_w):
    gate_act = jnp.einsum('bd,edf->ebf', normed, gate_w, preferred_element_type=jnp.float32)
    up_act = jnp.einsum('bd,edf->ebf', normed, up_w, preferred_element_type=jnp.float32)
    gated_hidden = (jax.nn.silu(gate_act) * up_act * gates.T[:, :, None]).astype(jnp.bfloat16)
    return jnp.einsum('ebf,efd->bd', gated_hidden, down_w, preferred_element_type=jnp.float32)


def write_cache(kv_cache, fresh_keys, fresh_vals, positions, start_pos):
    offset = positions[None, :] - start_pos[:, None]
    new_cache = kv_cache
    for step in range(len(fresh_keys[0])):
        entry = jnp.stack([jnp.stack([layer_keys[step], layer_vals[step]]) for layer_keys, layer_vals in zip(fresh_keys, fresh_vals)])
        new_cache = jnp.where((offset == step)[None, None, :, :, None, None], entry[:, :, :, None], new_cache)
    return new_cache


def solution(mesh):
    cache_spec = P(None, None, 'dp', None, 'tp', None)
    expert_spec = P(None, 'tp', None, None)
    in_specs = (P('dp', None), P('dp'), cache_spec, P(None, None, 'dp', None), P('tp', None), P(None, None), P(None, None, 'tp'), P(None, None, 'tp'), P(None, None, 'tp'), P(None, 'tp', None), P(None, None, None), expert_spec, expert_spec, expert_spec)
    out_specs = (P('dp', None), P('dp', 'tp'), cache_spec)

    def decode_local(tokens, start_pos, kv_cache, expert_ids, embed, norm_gain, w_query, w_key, w_value, w_out, w_router, w_gate, w_up, w_down):
        batch = tokens.shape[0]
        steps = tokens.shape[1] - 1
        layers = kv_cache.shape[0]
        cache_len = kv_cache.shape[3]
        kv_local = kv_cache.shape[4]
        head_dim = kv_cache.shape[5]
        heads_local = w_query.shape[2] // head_dim
        groups = heads_local // kv_local
        vocab_local = embed.shape[0]
        experts_local = w_gate.shape[1]
        shard = lax.axis_index('tp')
        vocab_start = shard * vocab_local
        expert_start = shard * experts_local
        positions = jnp.arange(cache_len)
        old_mask = positions[None, :] < start_pos[:, None]
        fresh_keys = [[] for index in range(layers)]
        fresh_vals = [[] for index in range(layers)]
        log_list = []
        logits = None
        for step in range(steps):
            local_ids = tokens[:, step] - vocab_start
            inside = (local_ids >= 0) & (local_ids < vocab_local)
            rows = jnp.take(embed, jnp.clip(local_ids, 0, vocab_local - 1), axis=0)
            rows = jnp.where(inside[:, None], rows, jnp.zeros_like(rows))
            hidden = EMBED_MULT * lax.psum(rows, 'tp').astype(jnp.float32)
            rot_pos = start_pos + step
            for layer in range(layers):
                normed = rms_norm(hidden, norm_gain[2 * layer])
                query = rotary(jnp.dot(normed, w_query[layer], preferred_element_type=jnp.float32).reshape(batch, heads_local, head_dim), rot_pos)
                key_new = rotary(jnp.dot(normed, w_key[layer], preferred_element_type=jnp.float32).reshape(batch, kv_local, head_dim), rot_pos)
                val_new = jnp.dot(normed, w_value[layer], preferred_element_type=jnp.float32).reshape(batch, kv_local, head_dim)
                fresh_keys[layer].append(key_new.astype(jnp.bfloat16))
                fresh_vals[layer].append(val_new.astype(jnp.bfloat16))
                mixed = attend(query.astype(jnp.bfloat16).reshape(batch, kv_local, groups, head_dim), kv_cache[layer, 0], kv_cache[layer, 1], jnp.stack(fresh_keys[layer]), jnp.stack(fresh_vals[layer]), old_mask)
                attn_part = jnp.dot(mixed, w_out[layer], preferred_element_type=jnp.float32).astype(jnp.bfloat16)
                hidden = hidden + RESID_MULT * lax.psum(attn_part, 'tp').astype(jnp.float32)
                normed = rms_norm(hidden, norm_gain[2 * layer + 1])
                gates = expert_gates(normed, w_router[layer], expert_ids[step, layer])
                gates_local = lax.dynamic_slice_in_dim(gates, expert_start, experts_local, axis=1)
                moe_part = expert_partial(normed, gates_local, w_gate[layer], w_up[layer], w_down[layer]).astype(jnp.bfloat16)
                hidden = hidden + RESID_MULT * lax.psum(moe_part, 'tp').astype(jnp.float32)
            final_norm = rms_norm(hidden, norm_gain[2 * layers])
            logits = jnp.einsum('bd,vd->bv', final_norm, embed, preferred_element_type=jnp.float32) / LOGIT_DIV
            peak = lax.pmax(jnp.max(logits, axis=1), 'tp')
            exp_sum = jnp.sum(jnp.exp(logits - peak[:, None]), axis=1)
            target_ids = tokens[:, step + 1] - vocab_start
            owned = (target_ids >= 0) & (target_ids < vocab_local)
            picked = jnp.take_along_axis(logits, jnp.clip(target_ids, 0, vocab_local - 1)[:, None], axis=1)[:, 0]
            picked = jnp.where(owned, picked, 0.0)
            totals = lax.psum(jnp.stack([exp_sum, picked], axis=1), 'tp')
            log_list.append(totals[:, 1] - peak - jnp.log(totals[:, 0]))
        new_cache = write_cache(kv_cache, fresh_keys, fresh_vals, positions, start_pos)
        return jnp.stack(log_list, axis=1), logits, new_cache

    return jax.shard_map(decode_local, mesh=mesh, in_specs=in_specs, out_specs=out_specs, check_vma=False)
```

profile of v0, /device:TPU:0, one launch (start us, length us, event | category | flops | bytes accessed | tf_op | source)
XLA Modules:
  0.0 1295.9 jit_solution(16173396930948129656)
XLA Ops:
  9.8 13.5 %gather_fusion.6 = bf16[512,1536]{1,0:T(8,128)(2,1)} fusion(bf16[6144,1536]{1,0:T(8,128)(2,1)} %param.22, s32[1024]{0:T(1024)S(1)} %pad_clamp_fusion), kind=kCustom, calls=%fused_computation.4.clone | custom fusion | bytes 3147776 | tf_op jit(solution)/shard_map/jit(_take)/gather | solution.py:99
  23.3 12.4 gather_fusion.4
  35.7 13.7 %gather_fusion.2 = bf16[512,1536]{1,0:T(8,128)(2,1)} fusion(bf16[6144,1536]{1,0:T(8,128)(2,1)} %param.22, s32[1024]{0:T(1024)S(1)} %pad_clamp_fusion.2), kind=kCustom, calls=%fused_computation.2.clone | custom fusion | bytes 3147776 | tf_op jit(solution)/shard_map/jit(_take)/gather | solution.py:99
  49.4 12.4 gather_fusion
  74.6 89.9 %all-reduce.21.cloned.1.call-done = (bf16[512,1536]{1,0:T(8,128)(2,1)}, bf16[512,1536]{1,0:T(8,128)(2,1)}, bf16[512,1536]{1,0:T(8,128)(2,1)}, bf16[512,1536]{1,0:T(8,128)(2,1)}) async-done(((bf16[512,1536]{1,0:T(8,128)(2,1)}, bf16[512,1536]{1,0:T(8,128)(2,1)}, bf16[512,1536]{1,0:T(8,128)(2,1)}, bf16[512,1536]{1,0:T(8,128)(2,1)}), (bf16[512,1536]{1,0:T(8,128)(2,1)}, bf16[512,1536]{1,0:T(8,128)(2,1)}, ...) | async-done | bytes 6291472 | tf_op jit(solution)/shard_map/psum | solution.py:101
  193.9 6.4 fusion.610
  204.3 7.7 fusion.52
  219.7 3.9 fusion.320
  227.8 7.4 fusion.612
  243.1 8.1 fusion.53
  253.2 3.6 fusion.318
  265.1 7.5 fusion.614
  279.4 8.0 fusion.54
  300.5 7.6 fusion.616
  315.5 7.9 fusion.314
  331.5 88.8 %all-reduce.19.cloned.1.call-done = (bf16[512,1536]{1,0:T(8,128)(2,1)}, bf16[512,1536]{1,0:T(8,128)(2,1)}, bf16[512,1536]{1,0:T(8,128)(2,1)}, bf16[512,1536]{1,0:T(8,128)(2,1)}) async-done(((bf16[512,1536]{1,0:T(8,128)(2,1)}, bf16[512,1536]{1,0:T(8,128)(2,1)}, bf16[512,1536]{1,0:T(8,128)(2,1)}, bf16[512,1536]{1,0:T(8,128)(2,1)}), (bf16[512,1536]{1,0:T(8,128)(2,1)}, bf16[512,1536]{1,0:T(8,128)(2,1)}, ...) | async-done | bytes 6291472 | tf_op jit(solution)/shard_map/psum | solution.py:112
  426.0 4.0 multiply_convert_fusion.15
  430.0 11.4 fusion.32
  441.4 5.9 fusion.34
  448.6 6.1 fusion.36
  455.3 6.5 fusion.38
  462.5 17.1 %fusion.184 = bf16[512,1536]{1,0:T(8,128)(2,1)} fusion(bf16[2,5,512,1536]{3,2,1,0:T(8,128)(2,1)} %param.31, f32[512,5,512]{2,0,1:T(8,128)} %fusion.32, f32[5,512]{1,0:T(8,128)S(1)} %fusion.535, bf16[2,5,1536,512]{3,2,1,0:T(8,128)(2,1)} %param.29, bf16[512,1536]{1,0:T(8,128)(2,1)S(1)} %copy-done.51), kind=kOutput, calls=%fused_computation.257 | convolution fusion | flops 8063025152 | bytes 24127488 | tf_op jit(solution)/shard_map/ebf,efd->bd/dot_general | solution.py:58
  479.6 17.1 %fusion.187 = bf16[512,1536]{1,0:T(8,128)(2,1)} fusion(bf16[2,5,512,1536]{3,2,1,0:T(8,128)(2,1)} %param.31, f32[512,5,512]{2,0,1:T(8,128)} %fusion.34, f32[5,512]{1,0:T(8,128)S(1)} %fusion.537, bf16[2,5,1536,512]{3,2,1,0:T(8,128)(2,1)} %param.29, bf16[512,1536]{1,0:T(8,128)(2,1)S(1)} %copy-done.49), kind=kOutput, calls=%fused_computation.258 | convolution fusion | flops 8063025152 | bytes 24127488 | tf_op jit(solution)/shard_map/ebf,efd->bd/dot_general | solution.py:58
  496.8 17.3 %fusion.190 = bf16[512,1536]{1,0:T(8,128)(2,1)} fusion(bf16[2,5,512,1536]{3,2,1,0:T(8,128)(2,1)} %param.31, f32[512,5,512]{2,0,1:T(8,128)} %fusion.36, f32[5,512]{1,0:T(8,128)S(1)} %fusion.539, bf16[2,5,1536,512]{3,2,1,0:T(8,128)(2,1)} %param.29, bf16[512,1536]{1,0:T(8,128)(2,1)S(1)} %copy-done.46), kind=kOutput, calls=%fused_computation.259 | convolution fusion | flops 8063025152 | bytes 24127488 | tf_op jit(solution)/shard_map/ebf,efd->bd/dot_general | solution.py:58
  514.1 17.1 %fusion.193 = bf16[512,1536]{1,0:T(8,128)(2,1)} fusion(bf16[2,5,512,1536]{3,2,1,0:T(8,128)(2,1)} %param.31, f32[512,5,512]{2,0,1:T(8,128)} %fusion.38, f32[5,512]{1,0:T(8,128)S(1)} %fusion.541, bf16[2,5,1536,512]{3,2,1,0:T(8,128)(2,1)} %param.29, bf16[512,1536]{1,0:T(8,128)(2,1)S(1)} %copy-done.44), kind=kOutput, calls=%fused_computation.260 | convolution fusion | flops 8063025152 | bytes 24127488 | tf_op jit(solution)/shard_map/ebf,efd->bd/dot_general | solution.py:58
  531.3 92.7 %all-reduce.17.cloned.1.call-done = (bf16[512,1536]{1,0:T(8,128)(2,1)}, bf16[512,1536]{1,0:T(8,128)(2,1)}, bf16[512,1536]{1,0:T(8,128)(2,1)}, bf16[512,1536]{1,0:T(8,128)(2,1)}) async-done(((bf16[512,1536]{1,0:T(8,128)(2,1)}, bf16[512,1536]{1,0:T(8,128)(2,1)}, bf16[512,1536]{1,0:T(8,128)(2,1)}, bf16[512,1536]{1,0:T(8,128)(2,1)}), (bf16[512,1536]{1,0:T(8,128)(2,1)}, bf16[512,1536]{1,0:T(8,128)(2,1)}, ...) | async-done | bytes 6291472 | tf_op jit(solution)/shard_map/psum | solution.py:117
  633.0 6.5 multiply_convert_fusion.14
  656.3 7.4 fusion.621
  674.0 8.1 fusion.60
  688.1 3.9 fusion.321
  698.3 7.6 fusion.623
  713.8 7.8 fusion.61
  723.6 3.6 fusion.319
  733.5 7.6 fusion.625
  748.0 8.0 fusion.62
  758.7 3.4 fusion.317
  769.9 7.6 fusion.627
  785.0 7.9 fusion.315
  810.6 79.3 %all-reduce.15.cloned.1.call-done = (bf16[512,1536]{1,0:T(8,128)(2,1)}, bf16[512,1536]{1,0:T(8,128)(2,1)}, bf16[512,1536]{1,0:T(8,128)(2,1)}, bf16[512,1536]{1,0:T(8,128)(2,1)}) async-done(((bf16[512,1536]{1,0:T(8,128)(2,1)}, bf16[512,1536]{1,0:T(8,128)(2,1)}, bf16[512,1536]{1,0:T(8,128)(2,1)}, bf16[512,1536]{1,0:T(8,128)(2,1)}), (bf16[512,1536]{1,0:T(8,128)(2,1)}, bf16[512,1536]{1,0:T(8,128)(2,1)}, ...) | async-done | bytes 6291472 | tf_op jit(solution)/shard_map/psum | solution.py:112
  889.9 4.4 multiply_reduce_fusion.13
  904.6 10.4 fusion.8
  915.6 9.3 fusion.10
  925.6 9.3 fusion.12
  935.6 6.2 fusion.14
  942.5 17.4 %fusion.172 = bf16[512,1536]{1,0:T(8,128)(2,1)} fusion(bf16[2,5,512,1536]{3,2,1,0:T(8,128)(2,1)} %param.31, f32[512,5,512]{2,0,1:T(8,128)} %fusion.8, f32[5,512]{1,0:T(8,128)S(1)} %fusion.534, bf16[2,5,1536,512]{3,2,1,0:T(8,128)(2,1)} %param.29, bf16[512,1536]{1,0:T(8,128)(2,1)} %copy-done.52), kind=kOutput, calls=%fused_computation.253 | convolution fusion | flops 8063025152 | bytes 24127488 | tf_op jit(solution)/shard_map/ebf,efd->bd/dot_general | solution.py:58
  959.9 17.4 %fusion.175 = bf16[512,1536]{1,0:T(8,128)(2,1)} fusion(bf16[2,5,512,1536]{3,2,1,0:T(8,128)(2,1)} %param.31, f32[512,5,512]{2,0,1:T(8,128)} %fusion.10, f32[5,512]{1,0:T(8,128)S(1)} %fusion.536, bf16[2,5,1536,512]{3,2,1,0:T(8,128)(2,1)} %param.29, bf16[512,1536]{1,0:T(8,128)(2,1)} %copy-done.47), kind=kOutput, calls=%fused_computation.254 | convolution fusion | flops 8063025152 | bytes 24127488 | tf_op jit(solution)/shard_map/ebf,efd->bd/dot_general | solution.py:58
  977.4 17.2 %fusion.178 = bf16[512,1536]{1,0:T(8,128)(2,1)} fusion(bf16[2,5,512,1536]{3,2,1,0:T(8,128)(2,1)} %param.31, f32[512,5,512]{2,0,1:T(8,128)} %fusion.12, f32[5,512]{1,0:T(8,128)S(1)} %fusion.538, bf16[2,5,1536,512]{3,2,1,0:T(8,128)(2,1)} %param.29, bf16[512,1536]{1,0:T(8,128)(2,1)S(1)} %get-tuple-element.135), kind=kOutput, calls=%fused_computation.255 | convolution fusion | flops 8063025152 | bytes 24127488 | tf_op jit(solution)/shard_map/ebf,efd->bd/dot_general | solution.py:58
  994.7 17.0 %fusion.181 = bf16[512,1536]{1,0:T(8,128)(2,1)} fusion(bf16[2,5,512,1536]{3,2,1,0:T(8,128)(2,1)} %param.31, f32[512,5,512]{2,0,1:T(8,128)} %fusion.14, f32[5,512]{1,0:T(8,128)S(1)} %fusion.540, bf16[2,5,1536,512]{3,2,1,0:T(8,128)(2,1)} %param.29, bf16[512,1536]{1,0:T(8,128)(2,1)S(1)} %get-tuple-element.134), kind=kOutput, calls=%fused_computation.256 | convolution fusion | flops 8063025152 | bytes 24127488 | tf_op jit(solution)/shard_map/ebf,efd->bd/dot_general | solution.py:58
  1012.6 78.6 %select_select_fusion = bf16[2,2,512,128,1,64]{3,5,4,2,1,0:T(8,128)(2,1)} fusion(bf16[2,2,512,128,1,64]{3,5,4,2,1,0:T(8,128)(2,1)} %param.20, pred[512,128]{1,0:T(8,128)(4,1)S(1)} %copy-done.128, pred[512,128]{1,0:T(8,128)(4,1)S(1)} %copy-done.129, pred[512,128]{1,0:T(8,128)(4,1)S(1)} %copy-done.130, pred[512,128]{1,0:T(8,128)(4,1)S(1)} %copy-done.127, ...), kind=kLoop, calls=%fused_computation.8 | loop fusion | flops 67108864 | bytes 68419584 | tf_op jit(solution)/shard_map/jit(_where)/select_n | solution.py:66
  1091.3 13.2 %all-reduce.13.cloned.1.call-done = (bf16[512,1536]{1,0:T(8,128)(2,1)}, bf16[512,1536]{1,0:T(8,128)(2,1)}, bf16[512,1536]{1,0:T(8,128)(2,1)}, bf16[512,1536]{1,0:T(8,128)(2,1)}) async-done(((bf16[512,1536]{1,0:T(8,128)(2,1)}, bf16[512,1536]{1,0:T(8,128)(2,1)}, bf16[512,1536]{1,0:T(8,128)(2,1)}, bf16[512,1536]{1,0:T(8,128)(2,1)}), (bf16[512,1536]{1,0:T(8,128)(2,1)}, bf16[512,1536]{1,0:T(8,128)(2,1)}, ...) | async-done | bytes 6291472 | tf_op jit(solution)/shard_map/psum | solution.py:117
  1107.9 17.8 %fusion.635 = (f32[512]{0:T(512)S(1)}, f32[512,6144]{1,0:T(8,128)}) fusion(bf16[6144,1536]{1,0:T(8,128)(2,1)} %param.22, f32[512,1536]{1,0:T(8,128)S(1)} %copy-done.31, bf16[512,1536]{1,0:T(8,128)(2,1)} %get-tuple-element.25, f32[1536]{0:T(1024)S(1)} %copy-done.163, f32[512]{0:T(512)S(1)} %add_rsqrt_fusion.12), kind=kOutput, calls=%fused_computation.919 | convolution fusion | flops 9674686464 | bytes 36186112 | tf_op jit(solution)/shard_map/bd,vd->bv/dot_general | solution.py:119
  1125.7 18.4 %fusion.632 = (f32[512]{0:T(512)S(1)}, f32[512,6144]{1,0:T(8,128)}) fusion(bf16[6144,1536]{1,0:T(8,128)(2,1)} %param.22, f32[512,1536]{1,0:T(8,128)} %copy-done.34, bf16[512,1536]{1,0:T(8,128)(2,1)} %get-tuple-element.22, f32[512]{0:T(512)S(1)} %add_rsqrt_fusion, f32[1536]{0:T(1024)S(1)} %copy-done.163), kind=kOutput, calls=%fused_computation.916 | convolution fusion | flops 9674686464 | bytes 36186112 | tf_op jit(solution)/shard_map/bd,vd->bv/dot_general | solution.py:119
  1146.1 18.3 %fusion.633 = (f32[512]{0:T(512)S(1)}, f32[512,6144]{1,0:T(8,128)}) fusion(bf16[6144,1536]{1,0:T(8,128)(2,1)} %param.22, f32[512,1536]{1,0:T(8,128)} %copy-done.32, bf16[512,1536]{1,0:T(8,128)(2,1)} %get-tuple-element.23, f32[512]{0:T(512)S(1)} %add_rsqrt_fusion.4, f32[1536]{0:T(1024)S(1)} %copy-done.163), kind=kOutput, calls=%fused_computation.917 | convolution fusion | flops 9674686464 | bytes 36186112 | tf_op jit(solution)/shard_map/bd,vd->bv/dot_general | solution.py:119
  1166.5 17.6 %fusion.634 = (f32[512]{0:T(512)S(1)}, f32[512,6144]{1,0:T(8,128)}) fusion(bf16[6144,1536]{1,0:T(8,128)(2,1)} %param.22, f32[512,1536]{1,0:T(8,128)S(1)} %copy-done.29, bf16[512,1536]{1,0:T(8,128)(2,1)} %get-tuple-element.24, f32[512]{0:T(512)S(1)} %add_rsqrt_fusion.8, f32[1536]{0:T(1024)S(1)} %copy-done.163), kind=kOutput, calls=%fused_computation.918 | convolution fusion | flops 9674686464 | bytes 36186112 | tf_op jit(solution)/shard_map/bd,vd->bv/dot_general | solution.py:119
  1184.1 8.4 gather_fusion.7
  1192.5 22.3 %all-reduce.1 = (f32[512]{0:T(512)S(1)}, f32[512]{0:T(512)S(1)}, f32[512]{0:T(512)S(1)}, f32[512]{0:T(512)S(1)}) all-reduce(f32[512]{0:T(512)S(1)} %get-tuple-element.233, f32[512]{0:T(512)S(1)} %get-tuple-element.235, f32[512]{0:T(512)S(1)} %get-tuple-element.237, ...), channel_id=1, replica_groups=mesh['dp'=1,'tp'=8] {'tp'}, use_global_device_ids=true, to_apply=%region_105.108 | all-reduce | flops 2048 | bytes 16384 | tf_op jit(solution)/shard_map/pmax | solution.py:120
  1214.8 6.4 exponential_reduce_fusion
  1221.2 8.5 gather_fusion.5
  1229.8 6.4 exponential_reduce_fusion.1
  1236.1 8.4 gather_fusion.3
  1244.5 6.4 exponential_reduce_fusion.2
  1250.9 8.5 gather_fusion.1
  1259.4 6.4 exponential_reduce_fusion.3
  1266.0 22.5 %all-reduce = (f32[512,2]{0,1:T(2,128)S(1)}, f32[512,2]{0,1:T(2,128)S(1)}, f32[512,2]{0,1:T(2,128)S(1)}, f32[512,2]{0,1:T(2,128)S(1)}) all-reduce(f32[512,2]{0,1:T(2,128)S(1)} %pad_maximum_fusion.16, f32[512,2]{0,1:T(2,128)S(1)} %pad_maximum_fusion.15, ...), channel_id=1, replica_groups=mesh['dp'=1,'tp'=8] {'tp'}, use_global_device_ids=true, to_apply=%region_107.110 | all-reduce | flops 4096 | bytes 32768 | tf_op jit(solution)/shard_map/psum | solution.py:126
  (637 shorter events, 250.4 us)
Async XLA Ops:
  7.2 157.4 %all-reduce.21.cloned.1.call-start = ((), (), s32[]{:S(2)}) async-start(), calls=%async_computation.4 | async-start | bytes 12582912 | tf_op jit(solution)/shard_map/psum | solution.py:101
  69.1 351.2 %all-reduce.19.cloned.1.call-start = ((), (), s32[]{:S(2)}) async-start(), calls=%async_computation.3 | async-start | bytes 12582912 | tf_op jit(solution)/shard_map/psum | solution.py:112
  70.6 116.2 %copy-start.147 = (f32[512]{0:T(512)}, f32[512]{0:T(512)S(1)}, u32[]{:S(2)}) copy-start(f32[512]{0:T(512)S(1)} %get-tuple-element.174) | copy-start | bytes 6148
  70.6 117.5 %copy-start.141 = (f32[512]{0:T(512)}, f32[512]{0:T(512)S(1)}, u32[]{:S(2)}) copy-start(f32[512]{0:T(512)S(1)} %get-tuple-element.173) | copy-start | bytes 6148
  70.6 117.5 %copy-start.143 = (f32[512]{0:T(512)}, f32[512]{0:T(512)S(1)}, u32[]{:S(2)}) copy-start(f32[512]{0:T(512)S(1)} %get-tuple-element.171) | copy-start | bytes 6148
  70.6 117.5 %copy-start.145 = (f32[512]{0:T(512)}, f32[512]{0:T(512)S(1)}, u32[]{:S(2)}) copy-start(f32[512]{0:T(512)S(1)} %get-tuple-element.172) | copy-start | bytes 6148
  70.6 97.9 %copy-start.60 = (bf16[2,1536,64]{1,2,0:T(8,128)(2,1)S(1)}, bf16[2,1536,64]{1,2,0:T(8,128)(2,1)}, u32[]{:S(2)}) copy-start(bf16[2,1536,64]{1,2,0:T(8,128)(2,1)} %param.25) | copy-start | bytes 1179652
  180.2 35.8 %copy-start.55 = (bf16[512,64]{0,1:T(8,128)(2,1)}, bf16[512,64]{0,1:T(8,128)(2,1)S(1)}, u32[]{:S(2)}) copy-start(bf16[512,64]{0,1:T(8,128)(2,1)S(1)} %convolution_convert_fusion.15) | copy-start | bytes 196612
  189.9 119.2 %copy-start.79 = (bf16[512,1,32]{0,2,1:T(8,128)(2,1)}, bf16[512,1,32]{0,2,1:T(8,128)(2,1)S(1)}, u32[]{:S(2)}) copy-start(bf16[512,1,32]{0,2,1:T(8,128)(2,1)S(1)} %get-tuple-element.98) | copy-start | bytes 98308
  189.9 119.2 %copy-start.81 = (bf16[512,1,32]{0,2,1:T(8,128)(2,1)}, bf16[512,1,32]{0,2,1:T(8,128)(2,1)S(1)}, u32[]{:S(2)}) copy-start(bf16[512,1,32]{0,2,1:T(8,128)(2,1)S(1)} %get-tuple-element.99) | copy-start | bytes 98308
  193.9 8.0 copy-start.66
  265.1 7.5 copy-start.100
  275.6 11.8 copy-start.103
  279.4 8.0 copy-start.122
  289.2 7.5 copy-start.91
  292.5 8.0 copy-start.136
  327.6 296.4 %all-reduce.17.cloned.1.call-start = ((), (), s32[]{:S(2)}) async-start(), calls=%async_computation.2 | async-start | bytes 12582912 | tf_op jit(solution)/shard_map/psum | solution.py:117
  426.0 15.4 %slice-start = ((s8[15728640]{0:T(1024)(128)(4,1)}), s8[4194304]{0:T(1024)(128)(4,1)S(1)}, s32[]{:S(2)}) async-start(s8[15728640]{0:T(1024)(128)(4,1)} %bitcast.945), calls=%async_computation.5 | async-start | bytes 8388608
  426.0 15.4 %slice-start.1 = ((s8[15728640]{0:T(1024)(128)(4,1)}), s8[4194304]{0:T(1024)(128)(4,1)S(1)}, s32[]{:S(2)}) async-start(s8[15728640]{0:T(1024)(128)(4,1)} %bitcast.945), calls=%async_computation.6 | async-start | bytes 8388608
  429.9 17.4 %copy-start.50 = (bf16[512,1536]{1,0:T(8,128)(2,1)}, bf16[512,1536]{1,0:T(8,128)(2,1)S(1)}, u32[]{:S(2)}) copy-start(bf16[512,1536]{1,0:T(8,128)(2,1)S(1)} %get-tuple-element.145) | copy-start | bytes 4718596
  429.9 18.0 %copy-start.48 = (bf16[512,1536]{1,0:T(8,128)(2,1)}, bf16[512,1536]{1,0:T(8,128)(2,1)S(1)}, u32[]{:S(2)}) copy-start(bf16[512,1536]{1,0:T(8,128)(2,1)S(1)} %get-tuple-element.144) | copy-start | bytes 4718596
  430.0 24.7 %copy-start.45 = (bf16[512,1536]{1,0:T(8,128)(2,1)}, bf16[512,1536]{1,0:T(8,128)(2,1)S(1)}, u32[]{:S(2)}) copy-start(bf16[512,1536]{1,0:T(8,128)(2,1)S(1)} %get-tuple-element.143) | copy-start | bytes 4718596
  430.0 31.8 %copy-start.43 = (bf16[512,1536]{1,0:T(8,128)(2,1)}, bf16[512,1536]{1,0:T(8,128)(2,1)S(1)}, u32[]{:S(2)}) copy-start(bf16[512,1536]{1,0:T(8,128)(2,1)S(1)} %get-tuple-element.142) | copy-start | bytes 4718596
  430.0 11.4 slice-start.2
  430.0 11.4 slice-start.3
  462.5 17.2 %copy-start.49 = (bf16[512,1536]{1,0:T(8,128)(2,1)S(1)}, bf16[512,1536]{1,0:T(8,128)(2,1)}, u32[]{:S(2)}) copy-start(bf16[512,1536]{1,0:T(8,128)(2,1)} %copy-done.48) | copy-start | bytes 4718596
  479.6 17.2 %copy-start.46 = (bf16[512,1536]{1,0:T(8,128)(2,1)S(1)}, bf16[512,1536]{1,0:T(8,128)(2,1)}, u32[]{:S(2)}) copy-start(bf16[512,1536]{1,0:T(8,128)(2,1)} %copy-done.45) | copy-start | bytes 4718596
  496.8 17.3 %copy-start.44 = (bf16[512,1536]{1,0:T(8,128)(2,1)S(1)}, bf16[512,1536]{1,0:T(8,128)(2,1)}, u32[]{:S(2)}) copy-start(bf16[512,1536]{1,0:T(8,128)(2,1)} %copy-done.43) | copy-start | bytes 4718596
  531.2 92.7 %copy-start.11 = (bf16[512,1536]{1,0:T(8,128)(2,1)S(1)}, bf16[512,1536]{1,0:T(8,128)(2,1)}, u32[]{:S(2)}) copy-start(bf16[512,1536]{1,0:T(8,128)(2,1)} %get-tuple-element.41) | copy-start | bytes 4718596
  531.2 95.9 %copy-start.6 = (bf16[512,1536]{1,0:T(8,128)(2,1)S(1)}, bf16[512,1536]{1,0:T(8,128)(2,1)}, u32[]{:S(2)}) copy-start(bf16[512,1536]{1,0:T(8,128)(2,1)} %get-tuple-element.40) | copy-start | bytes 4718596
  531.3 358.6 %all-reduce.15.cloned.1.call-start = ((), (), s32[]{:S(2)}) async-start(), calls=%async_computation.1 | async-start | bytes 12582912 | tf_op jit(solution)/shard_map/psum | solution.py:112
  633.0 7.7 copy-start.63
  651.8 12.3 copy-start.77
  651.8 12.3 copy-start.78
  656.3 7.5 copy-start.142
  656.3 7.8 copy-start.104
  656.3 7.8 copy-start.105
  698.3 7.6 copy-start.83
  733.5 7.6 copy-start.101
  744.2 11.9 copy-start.102
  748.0 8.1 copy-start.119
  748.0 8.1 copy-start.75
  748.0 8.1 copy-start.124
  748.0 8.1 copy-start.125
  758.7 7.5 copy-start.92
  762.0 7.9 copy-start.139
  797.2 8.8 copy-start.76
  797.2 11.5 copy-start.87
  797.2 307.3 %all-reduce.13.cloned.1.call-start = ((), (), s32[]{:S(2)}) async-start(), calls=%async_computation | async-start | bytes 12582912 | tf_op jit(solution)/shard_map/psum | solution.py:117
  894.3 8.6 copy-start.30
  904.6 10.4 copy-start.52
  904.6 20.4 %copy-start.47 = (bf16[512,1536]{1,0:T(8,128)(2,1)}, bf16[512,1536]{1,0:T(8,128)(2,1)S(1)}, u32[]{:S(2)}) copy-start(bf16[512,1536]{1,0:T(8,128)(2,1)S(1)} %get-tuple-element.136) | copy-start | bytes 4718596
  904.6 10.4 copy-start.54
  904.6 10.4 copy-start.135
  915.6 9.4 copy-start.134
  915.6 19.9 %slice-start.4 = ((s8[15728640]{0:T(1024)(128)(4,1)}), s8[4194304]{0:T(1024)(128)(4,1)S(1)}, s32[]{:S(2)}) async-start(s8[15728640]{0:T(1024)(128)(4,1)} %bitcast.947), calls=%async_computation.9 | async-start | bytes 8388608
  915.6 19.9 %slice-start.5 = ((s8[15728640]{0:T(1024)(128)(4,1)}), s8[4194304]{0:T(1024)(128)(4,1)S(1)}, s32[]{:S(2)}) async-start(s8[15728640]{0:T(1024)(128)(4,1)} %bitcast.947), calls=%async_computation.10 | async-start | bytes 8388608
  925.6 9.3 copy-start.133
  925.6 9.9 slice-start.6
  925.6 9.9 slice-start.7
  1012.6 91.8 %copy-start.31 = (f32[512,1536]{1,0:T(8,128)S(1)}, f32[512,1536]{1,0:T(8,128)}, u32[]{:S(2)}) copy-start(f32[512,1536]{1,0:T(8,128)} %copy-done.30) | copy-start | bytes 9437188
  1125.7 18.4 %copy-start.33 = (f32[512,1536]{1,0:T(8,128)S(1)}, f32[512,1536]{1,0:T(8,128)}, u32[]{:S(2)}) copy-start(f32[512,1536]{1,0:T(8,128)} %copy-done.32) | copy-start | bytes 9437188
  1146.1 18.3 %copy-start.29 = (f32[512,1536]{1,0:T(8,128)S(1)}, f32[512,1536]{1,0:T(8,128)}, u32[]{:S(2)}) copy-start(f32[512,1536]{1,0:T(8,128)} %copy-done.28) | copy-start | bytes 9437188
  1166.5 17.6 %copy-start.27 = (s32[512,1]{0,1:T(1,128)S(1)}, s32[512,1]{0,1:T(1,128)}, u32[]{:S(2)}) copy-start(s32[512,1]{0,1:T(1,128)} %get-tuple-element.245) | copy-start | bytes 6148
  (118 other events, 377.8 us)
Sparse Core Ops, SparseCore 0:
  69.2 95.2 all-reduce.20
  327.7 92.5 all-reduce.18
  531.4 92.5 all-reduce.16
  797.3 92.5 all-reduce.14
  1011.8 92.5 all-reduce.12
where the time goes:
time: 1300 us
  matrix products  488 us (38%)
  waiting for transfers between devices  364 us (28%)
  other arithmetic  229 us (18%)
  local copies, waits for them, and re-layouts  153 us (12%)
  blocking collectives  44.8 us (3%)
  between operations  16.4 us (1%)
    psum x2, waiting for transfers between devices, decode_local(): hidden = hidden + RESID_MULT * lax.psum(attn_part, 'tp').astype(jnp.float32)  168 us
    dot_general x8, matrix products, expert_partial(): jnp.einsum('ebf,efd->bd', gated_hidden, down_w, preferred_element_type=jn...  138 us
    psum x2, waiting for transfers between devices, decode_local(): hidden = hidden + RESID_MULT * lax.psum(moe_part, 'tp').astype(jnp.float32)  106 us
    psum x1, waiting for transfers between devices, decode_local(): hidden = EMBED_MULT * lax.psum(rows, 'tp').astype(jnp.float32)  89.9 us
    select_n x1, other arithmetic, write_cache(): jnp.where((offset == step)[None, None, :, :, None, None], entry[:, :, :,...  78.6 us
    dot_general x4, matrix products, decode_local(): jnp.einsum('bd,vd->bv', final_norm, embed, preferred_element_type=jnp.flo...  72.1 us
    dot_general x8, matrix products, expert_partial(): jnp.einsum('bd,edf->ebf', normed, up_w, preferred_element_type=jnp.float32)  65.1 us
    dot_general x8, matrix products, attend(): jnp.einsum('bkgs,bskh->bkgh', old_probs, cache_vals, preferred_element_ty...  63.4 us
  transfers between devices with their start and end apart: 5, of which 5 were waited for; matrix products, arithmetic and copies ran while one was open for 8% of the time, Pallas kernels for 0%

commit v1 on v0

v1 whole, which is shorter than its diff:
```python
import functools

import jax
import jax.numpy as jnp
from jax import lax
from jax.experimental import pallas as pl
from jax.experimental.pallas import tpu as pltpu
from jax.sharding import PartitionSpec as P

EMBED_MULT = 12.0
ATT_SCALE = 0.015625
RESID_MULT = 0.22
LOGIT_DIV = 6.0
NORM_EPS = 1e-6
ROPE_THETA = 10000.0

D = 1536
HEAD = 64
BATCH = 512
STEPS = 4
LAYERS = 2
CACHE = 128
EXPERTS = 40
LOCAL_EXPERTS = 5
FF = 512
VOCAB = 6144
N = 8
SEQS = BATCH // N
ROWS = SEQS * STEPS
MESH = pl.DeviceIdType.MESH
F32 = jnp.float32
BF16 = jnp.bfloat16
VMEM_LIMIT = 60 * 1024 * 1024

ORDER_RS = ("me", "sib", "bs", "a", "ds", "dg", "as", "b")
ORDER_AG = ("me", "sib", "bs", "a", "as", "b", "ds", "dg")


def places():
    me = lax.axis_index("tp")
    k = lax.rem(me, 2)
    x = lax.rem(lax.div(me, 2), 2)
    y = lax.div(me, 4)
    step_x = 2 - 4 * x
    step_y = 4 - 8 * y
    a = me + step_x + k * (step_y - step_x)
    b = me + step_y + k * (step_x - step_y)
    dg = me + step_x + step_y
    s = 1 - 2 * k
    return {"me": me, "sib": me + s, "a": a, "as": a + s, "b": b, "bs": b + s, "dg": dg, "ds": dg + s}


def entry_barrier(at):
    barrier = pltpu.get_barrier_semaphore()
    for name in ("sib", "a", "b"):
        pl.semaphore_signal(barrier, inc=1, device_id={"tp": at[name]}, device_id_type=MESH)
    pl.semaphore_wait(barrier, 3)


def pick(pos, order, at):
    total = jnp.int32(0)
    for i, name in enumerate(order):
        total = total + jnp.where(pos == i, at[name], 0)
    return total


class Gather:
    def __init__(self, at, own, ubuf, send, recv):
        self.at, self.own, self.ubuf, self.send, self.recv = at, own, ubuf, send, recv

    def copy(self, src, origin, target, slot):
        return pltpu.make_async_remote_copy(
            src_ref=src, dst_ref=self.ubuf.at[origin], send_sem=self.send.at[slot], recv_sem=self.recv.at[origin],
            device_id={"tp": target}, device_id_type=MESH)

    def item(self, slot):
        at = self.at
        if slot < 3:
            return self.copy(self.own, at["me"], at[("a", "b", "sib")[slot]], slot)
        name, target = (("a", "b"), ("a", "sib"), ("b", "sib"), ("dg", "sib"))[slot - 3]
        return self.copy(self.ubuf.at[at[name]], at[name], at[target], slot)

    def start(self, *slots):
        for slot in slots:
            self.item(slot).start()

    def arrive(self, name):
        origin = self.at[name]
        self.copy(self.own, origin, self.at["sib"], 0).wait_recv()

    def before(self, pos, rs):
        @pl.when(pos == 1)
        def _():
            self.start(1)
            self.arrive("sib")

        @pl.when(pos == 2)
        def _():
            self.arrive("a")
            self.start(3, 4)
            self.arrive("bs")

        @pl.when(pos == 4)
        def _():
            self.arrive("b")
            self.start(5)
            if rs:
                self.arrive("dg")
                self.start(6)
                self.arrive("ds")
            else:
                self.arrive("as")

        @pl.when(pos == 6)
        def _():
            if rs:
                self.arrive("as")
            else:
                self.arrive("dg")
                self.start(6)
                self.arrive("ds")

    def finish(self):
        for slot in range(7):
            self.item(slot).wait_send()


class Scatter:
    def __init__(self, at, tbuf, rbuf, send, recv):
        self.at, self.tbuf, self.rbuf, self.send, self.recv = at, tbuf, rbuf, send, recv

    def copy(self, slot, target):
        return pltpu.make_async_remote_copy(
            src_ref=self.tbuf.at[slot], dst_ref=self.rbuf.at[slot], send_sem=self.send.at[slot],
            recv_sem=self.recv.at[slot], device_id={"tp": target}, device_id_type=MESH)

    def arrive(self, slot):
        self.copy(slot, self.at["sib"]).wait_recv()

    def after(self, pos, acc, fin):
        at = self.at

        @pl.when(pos == 0)
        def _():
            fin[...] = acc[...]

        @pl.when((pos == 1) | (pos == 2) | (pos == 4) | (pos == 6))
        def _():
            slot = lax.div(pos, 2)
            self.tbuf[slot] = acc[...].astype(BF16)
            self.copy(slot, at["sib"]).start()

        @pl.when((pos == 3) | (pos == 5))
        def _():
            slot = lax.div(pos, 2)
            out = slot + 3
            self.arrive(slot)
            self.tbuf[out] = (acc[...] + self.rbuf[slot].astype(F32)).astype(BF16)
            self.copy(out, at["a"]).start()

        @pl.when(pos == 7)
        def _():
            self.arrive(3)
            self.arrive(5)
            self.tbuf[6] = (acc[...] + self.rbuf[3].astype(F32) + self.rbuf[5].astype(F32)).astype(BF16)
            self.copy(6, at["b"]).start()

    def finish(self, fin, out_ref):
        self.arrive(0)
        self.arrive(4)
        self.arrive(6)
        total = fin[...] + self.rbuf[0].astype(F32) + self.rbuf[4].astype(F32) + self.rbuf[6].astype(F32)
        out_ref[...] = total.astype(BF16)
        for slot in range(7):
            self.copy(slot, self.at["sib"]).wait_send()


def gather_scratch():
    return [pltpu.VMEM((N, ROWS, D), BF16), pltpu.SemaphoreType.DMA((7,)), pltpu.SemaphoreType.DMA((N,))]


def scatter_scratch():
    return [pltpu.VMEM((ROWS, D), F32), pltpu.VMEM((ROWS, D), F32), pltpu.VMEM((7, ROWS, D), BF16),
            pltpu.VMEM((7, ROWS, D), BF16), pltpu.SemaphoreType.DMA((7,)), pltpu.SemaphoreType.DMA((7,))]


VM = pl.BlockSpec(memory_space=pltpu.VMEM)
ANY = pl.BlockSpec(memory_space=pl.ANY)


def comm_params(ident):
    return pltpu.CompilerParams(collective_id=ident, has_side_effects=True, vmem_limit_bytes=VMEM_LIMIT)


def rows_kernel(count_ref, token_ref, row_ref, embed_ref, out_ref, buf, wide, sem):
    wide[...] = jnp.zeros_like(wide)
    count = count_ref[0]
    slots = buf.shape[0]

    def chunk(c, carry):
        base = c * slots
        width = jnp.minimum(slots, count - base)

        def issue(j, carry):
            pltpu.make_async_copy(embed_ref.at[lax.div(row_ref[base + j], 8)], buf.at[j], sem).start()
            return carry

        def place(j, carry):
            pltpu.make_async_copy(embed_ref.at[0], buf.at[j], sem).wait()
            return carry

        def move(j, carry):
            sub = lax.rem(row_ref[base + j], 8)
            block = buf[j].astype(F32)
            keep = lax.broadcasted_iota(jnp.int32, block.shape, 0) == sub
            line = jnp.sum(jnp.where(keep, block, 0.0), axis=0, keepdims=True)
            wide[pl.ds(token_ref[base + j], 1), :] = line
            return carry

        lax.fori_loop(0, width, issue, 0)
        lax.fori_loop(0, width, place, 0)
        lax.fori_loop(0, width, move, 0)
        return carry

    lax.fori_loop(0, lax.div(count + slots - 1, slots), chunk, 0)
    out_ref[...] = wide[...].astype(BF16)


def local_rows(ids, shard, embed):
    total = N * ROWS
    local = ids - shard * VOCAB
    inside = (local >= 0) & (local < VOCAB)
    rank = jnp.cumsum(inside.astype(jnp.int32)) - 1
    rank = jnp.where(inside, rank, -1)
    hit = rank[None, :] == jnp.arange(total)[:, None]
    token = jnp.sum(jnp.where(hit, jnp.arange(total)[None, :], 0), axis=1)
    row = jnp.sum(jnp.where(hit, local[None, :], 0), axis=1)
    count = jnp.sum(inside.astype(jnp.int32)).reshape(1)
    return pl.pallas_call(
        rows_kernel,
        out_shape=jax.ShapeDtypeStruct((total, D), BF16),
        grid_spec=pltpu.PrefetchScalarGridSpec(
            num_scalar_prefetch=3, grid=(1,),
            in_specs=[ANY],
            out_specs=pl.BlockSpec((total, D), lambda i, *_: (0, 0)),
            scratch_shapes=[pltpu.VMEM((256, 8, D), BF16), pltpu.VMEM((total, D), F32), pltpu.SemaphoreType.DMA]),
        compiler_params=pltpu.CompilerParams(vmem_limit_bytes=VMEM_LIMIT),
    )(count, token, row, embed.reshape(VOCAB // 8, 8, D))


def embed_kernel(rows_ref, out_ref, acc, fin, tbuf, rbuf, send, recv):
    at = places()
    entry_barrier(at)
    scatter = Scatter(at, tbuf, rbuf, send, recv)

    def body(pos, carry):
        acc[...] = rows_ref[pick(pos, ORDER_RS, at)].astype(F32)
        scatter.after(pos, acc, fin)
        return carry

    lax.fori_loop(0, N, body, 0)
    scatter.finish(fin, out_ref)


def embed_sum(rows, ident):
    return pl.pallas_call(
        embed_kernel,
        out_shape=jax.ShapeDtypeStruct((ROWS, D), BF16),
        in_specs=[VM], out_specs=VM,
        scratch_shapes=scatter_scratch(),
        compiler_params=comm_params(ident),
    )(rows.reshape(N, ROWS, D))


def qkv_kernel(u_ref, w_ref, cos_ref, sin_ref, qk_ref, v_ref, ubuf, send, recv):
    at = places()
    entry_barrier(at)
    gather = Gather(at, u_ref, ubuf, send, recv)
    gather.start(0, 2)
    ubuf[at["me"]] = u_ref[...]
    weights = w_ref[...]

    def body(pos, carry):
        gather.before(pos, False)
        blk = pick(pos, ORDER_AG, at)
        out = lax.dot_general(ubuf[blk], weights, (((1,), (1,)), ((), ())), preferred_element_type=F32)
        cos = cos_ref[blk]
        sin = sin_ref[blk]
        low = lax.rem(lax.broadcasted_iota(jnp.int32, (ROWS, 128), 1), HEAD) < HEAD // 2
        for half in range(2):
            part = out[:, half * 128:(half + 1) * 128]
            swapped = jnp.where(low, pltpu.roll(part, 128 - HEAD // 2, 1), pltpu.roll(part, HEAD // 2, 1))
            qk_ref[blk, :, half * 128:(half + 1) * 128] = (part * cos + swapped * sin).astype(BF16)
        v_ref[blk] = out[:, 256:384].astype(BF16)
        return carry

    lax.fori_loop(0, N, body, 0)
    gather.finish()


def project(u, weights, cos, sin, ident):
    return pl.pallas_call(
        qkv_kernel,
        out_shape=(jax.ShapeDtypeStruct((N, ROWS, 256), BF16), jax.ShapeDtypeStruct((N, ROWS, 128), BF16)),
        in_specs=[VM] * 4, out_specs=(VM, VM),
        scratch_shapes=gather_scratch(),
        compiler_params=comm_params(ident),
    )(u, weights, cos, sin)


ATT_SEQS = 32


def attend_kernel(qk_ref, v_ref, start_ref, cache_ref, *rest):
    o_ref, new_ref, wide = rest[-3:]
    lane = lax.broadcasted_iota(jnp.int32, (8, 128), 1)
    row = lax.broadcasted_iota(jnp.int32, (8, 128), 0)
    first = lane < HEAD
    own = [(2 * j + lax.div(lane, HEAD)) == row for j in range(4)]

    def spread(twice):
        return jnp.concatenate([jnp.where(own[j], twice, 0.0) for j in range(4)], axis=1)

    for g in range(ATT_SEQS // 8):
        span = slice(8 * g, 8 * g + 8)
        start = start_ref[span, :]
        queries, keys, vals, hot = [], [], [], []
        for s in range(STEPS):
            qk = qk_ref[0, s].astype(F32)[span, :]
            left, right = qk[:, :128], qk[:, 128:]
            left_r, right_r = pltpu.roll(left, HEAD, 1), pltpu.roll(right, HEAD, 1)
            queries += [spread(jnp.where(first, left, left_r)), spread(jnp.where(first, left_r, left)),
                        spread(jnp.where(first, right, right_r))]
            keys.append(spread(jnp.where(first, right_r, right)))
            vals.append(spread(v_ref[0, s].astype(F32)[span, :]))
            hot.append(jnp.where(lane == start + s, 1.0, 0.0))
        query = jnp.concatenate(queries, axis=0).astype(BF16)
        hot_all = jnp.concatenate(hot, axis=0).astype(BF16)
        fresh = jnp.where((lane >= start) & (lane < start + STEPS), 1.0, 0.0)
        fresh = jnp.broadcast_to(fresh[:, None, :], (8, HEAD, 128)) > 0.5
        planes = []
        for kind, entry in enumerate((keys, vals)):
            entry_all = jnp.concatenate(entry, axis=0).astype(BF16)
            update = lax.dot_general(entry_all, hot_all, (((0,), (0,)), ((), ())), preferred_element_type=F32)
            old = cache_ref[0, kind, span].astype(F32)
            plane = jnp.where(fresh, update.reshape(8, HEAD, 128), old).astype(BF16)
            new_ref[0, kind, span] = plane
            planes.append(plane.reshape(8 * HEAD, 128))
        score = jnp.dot(query, planes[0], preferred_element_type=F32) * ATT_SCALE
        valid = jnp.concatenate([jnp.where(lane <= start + s, 0.0, -jnp.inf) for s in range(STEPS) for h in range(3)], axis=0)
        score = score + valid
        weight = jnp.exp(score - jnp.max(score, axis=1, keepdims=True))
        prob = (weight / jnp.sum(weight, axis=1, keepdims=True)).astype(BF16)
        mixed = lax.dot_general(prob, planes[1], (((1,), (1,)), ((), ())), preferred_element_type=F32)
        for s in range(STEPS):
            heads = []
            for h in range(3):
                part = mixed[8 * (3 * s + h):8 * (3 * s + h) + 8, :]
                total = sum(jnp.where(own[j], part[:, 128 * j:128 * j + 128], 0.0) for j in range(4))
                heads.append(total + pltpu.roll(total, HEAD, 1))
            wide[s, span, 0:128] = jnp.where(first, heads[0], heads[1])
            wide[s, span, 128:256] = heads[2]
    o_ref[0] = wide[...].astype(BF16)


def attention(layer, qk, v, start_wide, cache, new_cache):
    per = SEQS // ATT_SEQS
    token_map = lambda i: (lax.div(i, per), 0, lax.rem(i, per), 0)
    plane_map = lambda i: (layer, 0, i, 0, 0)
    plane_spec = pl.BlockSpec((1, 2, ATT_SEQS, HEAD, CACHE), plane_map)
    args = [qk.reshape(N, STEPS, SEQS, 256), v.reshape(N, STEPS, SEQS, 128), start_wide, cache]
    in_specs = [pl.BlockSpec((1, STEPS, ATT_SEQS, 256), token_map), pl.BlockSpec((1, STEPS, ATT_SEQS, 128), token_map),
                pl.BlockSpec((ATT_SEQS, 128), lambda i: (i, 0)), plane_spec]
    aliases = {}
    if new_cache is not None:
        args.append(new_cache)
        in_specs.append(ANY)
        aliases = {4: 1}
    return pl.pallas_call(
        attend_kernel,
        out_shape=(jax.ShapeDtypeStruct((N, STEPS, SEQS, 256), BF16), jax.ShapeDtypeStruct(cache.shape, BF16)),
        grid=(BATCH // ATT_SEQS,),
        in_specs=in_specs,
        out_specs=(pl.BlockSpec((1, STEPS, ATT_SEQS, 256), token_map), plane_spec),
        scratch_shapes=[pltpu.VMEM((STEPS, ATT_SEQS, 256), F32)],
        input_output_aliases=aliases,
        compiler_params=pltpu.CompilerParams(dimension_semantics=("arbitrary",), vmem_limit_bytes=VMEM_LIMIT),
    )(*args)


def out_kernel(o_ref, w_ref, out_ref, acc, fin, tbuf, rbuf, send, recv):
    at = places()
    entry_barrier(at)
    scatter = Scatter(at, tbuf, rbuf, send, recv)

    def body(pos, carry):
        acc[...] = jnp.dot(o_ref[pick(pos, ORDER_RS, at)], w_ref[...], preferred_element_type=F32)
        scatter.after(pos, acc, fin)
        return carry

    lax.fori_loop(0, N, body, 0)
    scatter.finish(fin, out_ref)


def out_project(mixed, weights, ident):
    return pl.pallas_call(
        out_kernel,
        out_shape=jax.ShapeDtypeStruct((ROWS, D), BF16),
        in_specs=[VM, VM], out_specs=VM,
        scratch_shapes=scatter_scratch(),
        compiler_params=comm_params(ident),
    )(mixed.reshape(N, ROWS, 256), weights)


def moe_kernel(layer, u_ref, router_ref, chosen_ref, gate_hbm, up_hbm, down_hbm, out_ref, ubuf, ag_send, ag_recv,
               acc, fin, tbuf, rbuf, rs_send, rs_recv, gate_v, up_v, down_v, hidden, gates, w_sem):
    down_load = pltpu.make_async_copy(down_hbm.at[layer], down_v, w_sem.at[2, 0])
    for e in range(LOCAL_EXPERTS):
        pltpu.make_async_copy(gate_hbm.at[layer, e], gate_v.at[e], w_sem.at[0, e]).start()
        pltpu.make_async_copy(up_hbm.at[layer, e], up_v.at[e], w_sem.at[1, e]).start()
    down_load.start()
    at = places()
    entry_barrier(at)
    gather = Gather(at, u_ref, ubuf, ag_send, ag_recv)
    scatter = Scatter(at, tbuf, rbuf, rs_send, rs_recv)
    gather.start(0, 2)
    ubuf[at["me"]] = u_ref[...]

    def body(pos, carry):
        gather.before(pos, True)
        blk = pick(pos, ORDER_RS, at)
        route = jnp.dot(ubuf[blk], router_ref[...], preferred_element_type=F32)
        masked = jnp.where(chosen_ref[blk] > 0.5, route, -jnp.inf)
        weight = jnp.exp(masked - jnp.max(masked, axis=1, keepdims=True))
        gates[...] = weight / jnp.sum(weight, axis=1, keepdims=True)

        def expert(e, carry):
            @pl.when(pos == 0)
            def _():
                pltpu.make_async_copy(gate_hbm.at[layer, e], gate_v.at[e], w_sem.at[0, e]).wait()
                pltpu.make_async_copy(up_hbm.at[layer, e], up_v.at[e], w_sem.at[1, e]).wait()
            lane = lax.broadcasted_iota(jnp.int32, (ROWS, 128), 1)
            share = jnp.sum(jnp.where(lane == e, gates[...], 0.0), axis=1, keepdims=True)
            gate_act = jnp.dot(ubuf[blk], gate_v[e], preferred_element_type=F32)
            up_act = jnp.dot(ubuf[blk], up_v[e], preferred_element_type=F32)
            z = gate_act * jax.nn.sigmoid(gate_act) * up_act * share
            hidden[:, pl.ds(pl.multiple_of(e * FF, FF), FF)] = z.astype(BF16)
            return carry

        lax.fori_loop(0, LOCAL_EXPERTS, expert, 0)

        @pl.when(pos == 0)
        def _():
            down_load.wait()

        def column(c, carry):
            cols = pl.ds(pl.multiple_of(c * 512, 512), 512)
            acc[:, cols] = jnp.dot(hidden[...], down_v[:, cols], preferred_element_type=F32)
            return carry

        lax.fori_loop(0, D // 512, column, 0)
        scatter.after(pos, acc, fin)
        return carry

    lax.fori_loop(0, N, body, 0)
    gather.finish()
    scatter.finish(fin, out_ref)


def experts(layer, u, router, chosen, w_gate, w_up, w_down, ident):
    width = LOCAL_EXPERTS * FF
    return pl.pallas_call(
        functools.partial(moe_kernel, layer),
        out_shape=jax.ShapeDtypeStruct((ROWS, D), BF16),
        in_specs=[VM, VM, VM, ANY, ANY, ANY], out_specs=VM,
        scratch_shapes=gather_scratch() + scatter_scratch() + [
            pltpu.VMEM((LOCAL_EXPERTS, D, FF), BF16), pltpu.VMEM((LOCAL_EXPERTS, D, FF), BF16),
            pltpu.VMEM((width, D), BF16), pltpu.VMEM((ROWS, width), BF16), pltpu.VMEM((ROWS, 128), F32),
            pltpu.SemaphoreType.DMA((3, LOCAL_EXPERTS))],
        compiler_params=comm_params(ident),
    )(u, router, chosen, w_gate, w_up, w_down.reshape(LAYERS, width, D))


HEAD_ROWS = SEQS * (STEPS - 1)
TILE = 512
TILES = VOCAB // TILE


def fold(logits, column, target, peak, total, picked):
    parts = [logits[:, 128 * j:128 * j + 128] for j in range(TILE // 128)]
    top = functools.reduce(jnp.maximum, parts, peak)
    total = total * jnp.exp(peak - top)
    lane = lax.broadcasted_iota(jnp.int32, parts[0].shape, 1) + column
    for j, part in enumerate(parts):
        total = total + jnp.exp(part - top)
        picked = picked + jnp.where(lane + 128 * j == target, part, 0.0)
    return top, total, picked


def summary(peak, total, picked):
    top = jnp.max(peak, axis=1, keepdims=True)
    total = jnp.sum(total * jnp.exp(peak - top), axis=1, keepdims=True)
    picked = jnp.sum(picked, axis=1, keepdims=True)
    lane = lax.broadcasted_iota(jnp.int32, peak.shape, 1)
    return jnp.where(lane == 0, top, jnp.where(lane == 1, total, picked))


def head_kernel(f_ref, target_ref, embed_ref, stats_ref, last_ref, ubuf, send, recv, table, peak, total, picked, sem):
    def load(c):
        rows = pl.ds(pl.multiple_of(c * TILE, TILE), TILE)
        return pltpu.make_async_copy(embed_ref.at[rows], table.at[rows], sem.at[c])

    for c in range(TILES):
        load(c).start()
    at = places()
    entry_barrier(at)
    gather = Gather(at, f_ref, ubuf, send, recv)
    gather.start(0, 2)
    ubuf[at["me"]] = f_ref[...]

    def body(pos, carry):
        gather.before(pos, False)
        blk = pick(pos, ORDER_AG, at)
        peak[...] = jnp.full_like(peak, -1e30)
        total[...] = jnp.zeros_like(total)
        picked[...] = jnp.zeros_like(picked)

        def tile(c, carry):
            @pl.when(pos == 0)
            def _():
                load(c).wait()
            rows = pl.ds(pl.multiple_of(c * TILE, TILE), TILE)
            logits = lax.dot_general(ubuf[blk, 0:HEAD_ROWS, :], table[rows, :], (((1,), (1,)), ((), ())),
                                     preferred_element_type=F32) * (1.0 / LOGIT_DIV)
            peak[...], total[...], picked[...] = fold(logits, c * TILE, target_ref[blk], peak[...], total[...], picked[...])
            return carry

        lax.fori_loop(0, TILES, tile, 0)
        stats_ref[blk] = summary(peak[...], total[...], picked[...])
        last_ref[blk] = ubuf[blk, HEAD_ROWS:ROWS, :]
        return carry

    lax.fori_loop(0, N, body, 0)
    gather.finish()


def head_stats(f, target_wide, embed, ident):
    return pl.pallas_call(
        head_kernel,
        out_shape=(jax.ShapeDtypeStruct((N, HEAD_ROWS, 128), F32), jax.ShapeDtypeStruct((N, SEQS, D), BF16)),
        in_specs=[VM, VM, ANY], out_specs=(VM, VM),
        scratch_shapes=gather_scratch() + [pltpu.VMEM((VOCAB, D), BF16)] + [pltpu.VMEM((HEAD_ROWS, 128), F32)] * 3 + [
            pltpu.SemaphoreType.DMA((TILES,))],
        compiler_params=comm_params(ident),
    )(f, target_wide, embed)


def last_kernel(f_ref, target_ref, embed_ref, logits_ref, stats_ref, peak, total, picked):
    c = pl.program_id(0)

    @pl.when(c == 0)
    def _():
        peak[...] = jnp.full_like(peak, -1e30)
        total[...] = jnp.zeros_like(total)
        picked[...] = jnp.zeros_like(picked)

    logits = lax.dot_general(f_ref[...], embed_ref[...], (((1,), (1,)), ((), ())),
                             preferred_element_type=F32) * (1.0 / LOGIT_DIV)
    logits_ref[...] = logits
    peak[...], total[...], picked[...] = fold(logits, c * TILE, target_ref[...], peak[...], total[...], picked[...])

    @pl.when(c == TILES - 1)
    def _():
        stats_ref[...] = summary(peak[...], total[...], picked[...])


def last_step(f, target_wide, embed):
    return pl.pallas_call(
        last_kernel,
        out_shape=(jax.ShapeDtypeStruct((BATCH, VOCAB), F32), jax.ShapeDtypeStruct((BATCH, 128), F32)),
        grid=(TILES,),
        in_specs=[pl.BlockSpec((BATCH, D), lambda c: (0, 0)), pl.BlockSpec((BATCH, 128), lambda c: (0, 0)),
                  pl.BlockSpec((TILE, D), lambda c: (c, 0))],
        out_specs=(pl.BlockSpec((BATCH, TILE), lambda c: (0, c)), pl.BlockSpec((BATCH, 128), lambda c: (0, 0))),
        scratch_shapes=[pltpu.VMEM((BATCH, 128), F32)] * 3,
        compiler_params=pltpu.CompilerParams(dimension_semantics=("arbitrary",), vmem_limit_bytes=VMEM_LIMIT),
    )(f, target_wide, embed)


def share_kernel(in_ref, out_ref, send, recv):
    me = lax.axis_index("tp")
    barrier = pltpu.get_barrier_semaphore()
    for shift in range(1, N):
        pl.semaphore_signal(barrier, inc=1, device_id={"tp": lax.rem(me + shift, N)}, device_id_type=MESH)
    pl.semaphore_wait(barrier, N - 1)
    copies = [pltpu.make_async_remote_copy(
        src_ref=in_ref, dst_ref=out_ref.at[shift], send_sem=send.at[shift], recv_sem=recv.at[shift],
        device_id={"tp": lax.rem(me + shift, N)}, device_id_type=MESH) for shift in range(1, N)]
    for item in copies:
        item.start()
    out_ref[0] = in_ref[...]
    for item in copies:
        item.wait()


def share(values, ident):
    return pl.pallas_call(
        share_kernel,
        out_shape=jax.ShapeDtypeStruct((N,) + values.shape, F32),
        in_specs=[VM], out_specs=VM,
        scratch_shapes=[pltpu.SemaphoreType.DMA((N,)), pltpu.SemaphoreType.DMA((N,))],
        compiler_params=comm_params(ident),
    )(values)


def rms_norm(hidden, gain):
    mean_sq = jnp.mean(hidden * hidden, axis=-1, keepdims=True)
    return (hidden * lax.rsqrt(mean_sq + NORM_EPS) * gain).astype(BF16)


def by_block(values):
    return values.reshape(N, SEQS, values.shape[1]).transpose(0, 2, 1)


def solution(mesh):
    cache_spec = P(None, None, 'dp', None, 'tp', None)
    expert_spec = P(None, 'tp', None, None)
    in_specs = (P('dp', None), P('dp'), cache_spec, P(None, None, 'dp', None), P('tp', None), P(None, None), P(None, None, 'tp'), P(None, None, 'tp'), P(None, None, 'tp'), P(None, 'tp', None), P(None, None, None), expert_spec, expert_spec, expert_spec)
    out_specs = (P('dp', None), P('dp', 'tp'), cache_spec)

    def decode_local(tokens, start_pos, kv_cache, expert_ids, embed, norm_gain, w_query, w_key, w_value, w_out, w_router, w_gate, w_up, w_down):
        shard = lax.axis_index('tp')
        cache = kv_cache.transpose(0, 1, 2, 4, 5, 3).reshape(LAYERS, 2, BATCH, HEAD, CACHE)

        ids = by_block(tokens[:, :STEPS]).reshape(-1)
        rows = local_rows(ids, shard, embed)
        hidden = EMBED_MULT * embed_sum(rows, 0).astype(F32)

        pos = by_block(start_pos[:, None] + jnp.arange(STEPS)[None, :]).reshape(N, ROWS)
        inv_freq = ROPE_THETA ** (-2.0 * jnp.arange(HEAD // 2, dtype=F32) / HEAD)
        angles = pos.astype(F32)[:, :, None] * inv_freq
        cos, sin = jnp.cos(angles), jnp.sin(angles)
        cos = jnp.concatenate([cos] * 4, axis=-1)
        sin = jnp.concatenate([-sin, sin, -sin, sin], axis=-1)
        start_wide = jnp.broadcast_to(start_pos[:, None], (BATCH, 128))

        wq, wk, wv = (w.transpose(0, 2, 1) for w in (w_query, w_key, w_value))
        w_qkv = jnp.concatenate([wq, wk, wv, wv], axis=1)
        w_out_wide = jnp.concatenate([w_out, jnp.zeros((LAYERS, 64, D), BF16)], axis=1)

        first_expert = shard * LOCAL_EXPERTS
        turned = lax.rem(jnp.arange(EXPERTS) + first_expert, EXPERTS)
        router = jnp.take(w_router, turned, axis=2)
        router = jnp.concatenate([router, jnp.zeros((LAYERS, D, 128 - EXPERTS), BF16)], axis=2)
        lanes = jnp.concatenate([turned, jnp.full((128 - EXPERTS,), -1, turned.dtype)])
        chosen = jnp.any(expert_ids[..., None] == lanes, axis=3).astype(F32)
        chosen = chosen.reshape(STEPS, LAYERS, N, SEQS, 128).transpose(1, 2, 0, 3, 4).reshape(LAYERS, N, ROWS, 128)

        new_cache = None
        for layer in range(LAYERS):
            u = rms_norm(hidden, norm_gain[2 * layer])
            qk, v = project(u, w_qkv[layer], cos, sin, 1 + 3 * layer)
            mixed, new_cache = attention(layer, qk, v, start_wide, cache, new_cache)
            attn = out_project(mixed, w_out_wide[layer], 2 + 3 * layer)
            hidden = hidden + RESID_MULT * attn.astype(F32)
            u = rms_norm(hidden, norm_gain[2 * layer + 1])
            y = experts(layer, u, router[layer], chosen[layer], w_gate, w_up, w_down, 3 + 3 * layer)
            hidden = hidden + RESID_MULT * y.astype(F32)

        f = rms_norm(hidden, norm_gain[2 * LAYERS])
        target = tokens[:, 1:] - shard * VOCAB
        early = by_block(target[:, :STEPS - 1]).reshape(N, HEAD_ROWS, 1)
        stats, f_last = head_stats(f, jnp.broadcast_to(early, (N, HEAD_ROWS, 128)), embed, 7)
        last = jnp.broadcast_to(target[:, STEPS - 1:], (BATCH, 128))
        logits, last_stats = last_step(f_last.reshape(BATCH, D), last, embed)
        stats = stats[:, :, :8].reshape(N, STEPS - 1, SEQS, 8).transpose(3, 1, 0, 2).reshape(8, (STEPS - 1) * BATCH)
        packed = jnp.concatenate([stats, last_stats[:, :8].T], axis=1)
        shared = share(packed, 8)
        peak = jnp.max(shared[:, 0], axis=0)
        total = jnp.sum(shared[:, 1] * jnp.exp(shared[:, 0] - peak), axis=0)
        log_probs = jnp.sum(shared[:, 2], axis=0) - peak - jnp.log(total)
        log_probs = log_probs.reshape(STEPS, BATCH).T
        new_cache = new_cache.reshape(LAYERS, 2, BATCH, 1, HEAD, CACHE).transpose(0, 1, 2, 5, 3, 4)
        return log_probs, logits, new_cache

    return jax.shard_map(decode_local, mesh=mesh, in_specs=in_specs, out_specs=out_specs, check_vma=False)
```

time: 1300 us -> 671 us (0.52)
  Pallas kernels: 0 us -> 591 us
  matrix products: 488 us -> 0 us
  waiting for transfers between devices: 364 us -> 0 us
  other arithmetic: 229 us -> 55.5 us
  local copies, waits for them, and re-layouts: 153 us -> 17.3 us
  blocking collectives: 44.8 us -> 0 us
  between operations: 16.4 us -> 1.46 us
    pallas_call x0 -> x13, Pallas kernels: none -> 591 us  [the longest x2 175 us: experts(): pl.pallas_call(functools.partial(moe_kernel, layer), out_shape=jax.ShapeD...]
    dot_general x88 -> x0, matrix products: 488 us -> none  [the longest x8 138 us: expert_partial(): jnp.einsum('ebf,efd->bd', gated_hidden, down_w, preferred_element_type=jn...]
    psum x5 -> x0, waiting for transfers between devices: 364 us -> none  [the longest x2 168 us: decode_local(): hidden = hidden + RESID_MULT * lax.psum(attn_part, 'tp').astype(jnp.float32)]
    select_n x8 -> x3, other arithmetic: 85.9 us -> 0.17 us  [the longest x2 0.09 us: decode_local(): router = jnp.take(w_router, turned, axis=2)]
    gather x8 -> x2, local copies, waits for them, and re-layouts: 85.7 us -> 1.91 us  [decode_local(): router = jnp.take(w_router, turned, axis=2)]
    reduce_sum x26 -> x4, other arithmetic: 49.1 us -> 8.03 us  [the longest x1 5.67 us: local_rows(): row = jnp.sum(jnp.where(hit, local[None, :], 0), axis=1)]
    reduce_sum x20 -> x5, other arithmetic: 32.3 us -> 8.5 us  [rms_norm(): mean_sq = jnp.mean(hidden * hidden, axis=-1, keepdims=True)]
    another operation x31 -> x2, other arithmetic: 22.9 us -> 0.32 us
  transfers between devices with their start and end apart: 5 -> 0, of which waited for: 5 -> 0; matrix products, arithmetic and copies ran while one was open for 8% -> 0% of each run, Pallas kernels for 0% -> 0%
where the time goes in v1:
time: 671 us; the launch traced here: 665 us
  Pallas kernels  591 us (88%)
  other arithmetic  55.5 us (8%)
  local copies, waits for them, and re-layouts  17.3 us (3%)
    pallas_call x2, Pallas kernels, experts(): pl.pallas_call(functools.partial(moe_kernel, layer), out_shape=jax.ShapeD...  175 us
    pallas_call x2, Pallas kernels, attention(): pl.pallas_call(attend_kernel, out_shape=(jax.ShapeDtypeStruct((N, STEPS,...  87.2 us
    pallas_call x1, Pallas kernels, head_stats(): pl.pallas_call(head_kernel, out_shape=(jax.ShapeDtypeStruct((N, HEAD_ROWS...  83.9 us
    pallas_call x2, Pallas kernels, out_project(): pl.pallas_call(out_kernel, out_shape=jax.ShapeDtypeStruct((ROWS, D), BF16...  80.1 us
    pallas_call x2, Pallas kernels, project(): pl.pallas_call(qkv_kernel, out_shape=(jax.ShapeDtypeStruct((N, ROWS, 256)...  73.5 us
    pallas_call x1, Pallas kernels, embed_sum(): pl.pallas_call(embed_kernel, out_shape=jax.ShapeDtypeStruct((ROWS, D), BF...  41.6 us
    reduce_or x1, other arithmetic, decode_local(): chosen = jnp.any(expert_ids[..., None] == lanes, axis=3).astype(F32)  22.6 us
    pallas_call x1, Pallas kernels, last_step(): pl.pallas_call(last_kernel, out_shape=(jax.ShapeDtypeStruct((BATCH, VOCAB...  21.7 us

profile of v1, /device:TPU:0, one launch (start us, length us, event | category | flops | bytes accessed | tf_op | source)
XLA Modules:
  0.0 664.9 jit_solution(8228137658071150976)
XLA Ops:
  0.7 0.8 and_convert_fusion
  1.4 0.1 sub.61
  1.5 0.1 sub.63
  1.6 0.1 reshape.257
  1.7 0.1 reshape.254
  1.8 0.3 reduce-window.9
  2.0 0.1 slice.102
  2.2 0.1 slice_reduce_fusion.1
  2.3 0.1 bitcast_select_fusion
  2.3 5.7 select_reduce_fusion
  8.0 0.7 fusion.15
  8.7 16.6 %shard_map.157 = bf16[2048,1536]{1,0:T(8,128)(2,1)} custom-call(s32[1]{0:T(128)} %bitcast.count_ref, s32[2048]{0:T(1024)} %get-tuple-element.44.token_ref, s32[2048]{0:T(1024)} %get-tuple-element.43.row_ref, bf16[768,8,1536]{2,1,0:T(8,128)(2,1)} %bitcast.82), custom_call_target="tpu_custom_call" | custom-call | tf_op jit(solution)/shard_map/pallas_call | solution.py:239
  25.3 41.6 %shard_map.158 = bf16[256,1536]{1,0:T(8,128)(2,1)} custom-call(bf16[8,256,1536]{2,1,0:T(8,128)(2,1)} %bitcast.88), custom_call_target="tpu_custom_call" | custom-call | tf_op jit(solution)/shard_map/pallas_call | solution.py:266
  66.9 1.4 fusion.2
  68.3 0.1 slice_reduce_fusion.2
  68.4 2.3 fusion.4.u_ref
  70.8 0.1 add.129
  70.9 0.1 add.131
  71.0 3.7 fusion.9
  74.7 3.0 pad_maximum_fusion.1
  77.8 0.2 pad_maximum_fusion
  78.0 1.6 slice_bitcast_fusion
  79.5 36.8 %shard_map.159 = (bf16[8,256,256]{2,1,0:T(8,128)(2,1)}, bf16[8,256,128]{2,1,0:T(8,128)(2,1)}) custom-call(bf16[256,1536]{1,0:T(8,128)(2,1)} %fusion.4.u_ref, bf16[384,1536]{1,0:T(8,128)(2,1)} %get-tuple-element.50.w_ref, f32[8,256,128]{2,1,0:T(8,128)} %get-tuple-element.62.cos_ref, f32[8,256,128]{2,1,0:T(8,128)} %get-tuple-element.63.sin_ref), custom_call_target="tpu_custom_call" | custom-call | tf_op jit(solution)/shard_map/pallas_call | solution.py:302
  116.3 0.8 broadcast_in_dim.43.start_ref
  117.1 43.7 %shard_map.160 = (bf16[8,4,64,256]{3,2,1,0:T(8,128)(2,1)}, bf16[2,2,512,64,128]{4,3,2,1,0:T(8,128)(2,1)}) custom-call(bf16[8,4,64,256]{3,2,1,0:T(8,128)(2,1)} %bitcast.95, bf16[8,4,64,128]{3,2,1,0:T(8,128)(2,1)} %bitcast.100, s32[512,128]{1,0:T(8,128)} %broadcast_in_dim.43.start_ref, bf16[2,2,512,64,128]{4,3,2,1,0:T(8,128)(2,1)} %bitcast.83), custom_call_target="tpu_custom_call" | custom-call | tf_op jit(solution)/shard_map/pallas_call | solution.py:379
  160.8 1.3 fusion.6
  162.1 40.0 %shard_map.161 = bf16[256,1536]{1,0:T(8,128)(2,1)} custom-call(bf16[8,256,256]{2,1,0:T(8,128)(2,1)} %bitcast.97, bf16[256,1536]{1,0:T(8,128)(2,1)} %get-tuple-element.54.w_ref), custom_call_target="tpu_custom_call" | custom-call | tf_op jit(solution)/shard_map/pallas_call | solution.py:406
  202.1 1.6 multiply_reduce_fusion.3
  203.7 1.3 multiply_convert_fusion.3.u_ref
  205.1 1.5 gather_fusion
  206.6 0.4 copy.41
  207.0 0.1 select_bitcast_fusion
  207.1 1.1 fusion.8
  208.2 1.9 copy.42
  210.1 22.6 %compare_reduce_fusion = pred[4,2,512,128]{3,2,1,0:T(8,128)(4,1)S(1)} fusion(s32[128]{0:T(128)S(1)} %concatenate.26, s32[4,2,512,8]{3,2,1,0:T(8,128)} %copy.42), kind=kLoop, calls=%fused_computation.4 | loop fusion | flops 7864320 | bytes 655872 | tf_op jit(solution)/shard_map/reduce_or | solution.py:656
  232.7 0.1 transpose.115
  232.9 1.2 fusion.16
  234.0 1.1 copy.43
  235.1 87.7 %shard_map.162 = bf16[256,1536]{1,0:T(8,128)(2,1)} custom-call(bf16[256,1536]{1,0:T(8,128)(2,1)} %multiply_convert_fusion.3.u_ref, bf16[1536,128]{1,0:T(8,128)(2,1)} %get-tuple-element.56.router_ref, f32[8,256,128]{2,1,0:T(8,128)} %bitcast.90, bf16[2,5,1536,512]{3,2,1,0:T(8,128)(2,1)} %gate_hbm.3, bf16[2,5,1536,512]{3,2,1,0:T(8,128)(2,1)} %up_hbm.3, ...), custom_call_target="tpu_custom_call" | custom-call | tf_op jit(solution)/shard_map/pallas_call | solution.py:472
  322.7 1.8 multiply_reduce_fusion.2
  324.6 1.4 multiply_convert_fusion.2.u_ref
  326.0 36.7 %shard_map.163 = (bf16[8,256,256]{2,1,0:T(8,128)(2,1)}, bf16[8,256,128]{2,1,0:T(8,128)(2,1)}) custom-call(bf16[256,1536]{1,0:T(8,128)(2,1)} %multiply_convert_fusion.2.u_ref, bf16[384,1536]{1,0:T(8,128)(2,1)} %get-tuple-element.49.w_ref, f32[8,256,128]{2,1,0:T(8,128)} %get-tuple-element.62.cos_ref, f32[8,256,128]{2,1,0:T(8,128)} %get-tuple-element.63.sin_ref), custom_call_target="tpu_custom_call" | custom-call | tf_op jit(solution)/shard_map/pallas_call | solution.py:302
  362.7 43.6 %shard_map.164 = (bf16[8,4,64,256]{3,2,1,0:T(8,128)(2,1)}, bf16[2,2,512,64,128]{4,3,2,1,0:T(8,128)(2,1)}) custom-call(bf16[8,4,64,256]{3,2,1,0:T(8,128)(2,1)} %bitcast.94, bf16[8,4,64,128]{3,2,1,0:T(8,128)(2,1)} %bitcast.99, s32[512,128]{1,0:T(8,128)} %broadcast_in_dim.43.start_ref, ...), custom_call_target="tpu_custom_call", output_to_operand_aliasing={{1}: (4, {})} | custom-call | tf_op jit(solution)/shard_map/pallas_call | solution.py:379
  406.3 40.1 %shard_map.165 = bf16[256,1536]{1,0:T(8,128)(2,1)} custom-call(bf16[8,256,256]{2,1,0:T(8,128)(2,1)} %bitcast.96, bf16[256,1536]{1,0:T(8,128)(2,1)} %get-tuple-element.53.w_ref), custom_call_target="tpu_custom_call" | custom-call | tf_op jit(solution)/shard_map/pallas_call | solution.py:406
  446.4 2.1 multiply_reduce_fusion.1
  448.5 1.1 multiply_convert_fusion.1.u_ref
  449.6 0.3 copy-done.6
  449.9 1.1 copy.44
  451.0 87.5 %shard_map.166 = bf16[256,1536]{1,0:T(8,128)(2,1)} custom-call(bf16[256,1536]{1,0:T(8,128)(2,1)} %multiply_convert_fusion.1.u_ref, bf16[1536,128]{1,0:T(8,128)(2,1)} %get-tuple-element.55.router_ref, f32[8,256,128]{2,1,0:T(8,128)} %bitcast.91, bf16[2,5,1536,512]{3,2,1,0:T(8,128)(2,1)} %gate_hbm.3, bf16[2,5,1536,512]{3,2,1,0:T(8,128)(2,1)} %up_hbm.3, ...), custom_call_target="tpu_custom_call" | custom-call | tf_op jit(solution)/shard_map/pallas_call | solution.py:472
  538.5 1.5 multiply_reduce_fusion
  540.1 1.2 multiply_convert_fusion.f_ref
  541.3 0.1 reshape.248
  541.4 0.1 broadcast_in_dim.75
  541.5 1.2 broadcast_in_dim.76.target_ref
  542.6 83.9 %shard_map.167 = (f32[8,192,128]{2,1,0:T(8,128)}, bf16[8,64,1536]{2,1,0:T(8,128)(2,1)}) custom-call(bf16[256,1536]{1,0:T(8,128)(2,1)} %multiply_convert_fusion.f_ref, s32[8,192,128]{2,1,0:T(8,128)} %broadcast_in_dim.76.target_ref, bf16[6144,1536]{1,0:T(8,128)(2,1)} %embed_ref.3), custom_call_target="tpu_custom_call" | custom-call | tf_op jit(solution)/shard_map/pallas_call | solution.py:548
  626.5 0.8 broadcast_in_dim.78.target_ref
  627.4 21.7 %shard_map.168 = (f32[512,6144]{1,0:T(8,128)}, f32[512,128]{1,0:T(8,128)}) custom-call(bf16[512,1536]{1,0:T(8,128)(2,1)} %bitcast.92, s32[512,128]{1,0:T(8,128)} %broadcast_in_dim.78.target_ref, bf16[6144,1536]{1,0:T(8,128)(2,1)} %embed_ref.3), custom_call_target="tpu_custom_call" | custom-call | tf_op jit(solution)/shard_map/pallas_call | solution.py:578
  649.1 1.1 copy.47
  650.2 0.3 copy.46
  650.4 0.1 reshape.250
  650.5 0.6 pad_maximum_fusion.3.in_ref
  651.1 11.0 %shard_map.169 = f32[8,8,2048]{2,1,0:T(8,128)} custom-call(f32[8,2048]{1,0:T(8,128)} %pad_maximum_fusion.3.in_ref), custom_call_target="tpu_custom_call" | custom-call | tf_op jit(solution)/shard_map/pallas_call | solution.py:607
  662.1 1.6 slice_reduce_fusion
  663.8 0.6 sub.71
  (55 shorter events, 0.4 us)
Async XLA Ops:
  0.6 204.4 %copy-start = (bf16[2,1536,40]{1,2,0:T(8,128)(2,1)S(1)}, bf16[2,1536,40]{1,2,0:T(8,128)(2,1)}, u32[]{:S(2)}) copy-start(bf16[2,1536,40]{1,2,0:T(8,128)(2,1)} %param.24) | copy-start | bytes 737284
  25.3 43.0 %copy-start.13 = (f32[5,1536]{1,0:T(8,128)S(1)}, f32[5,1536]{1,0:T(8,128)}, u32[]{:S(2)}) copy-start(f32[5,1536]{1,0:T(8,128)} %param.19) | copy-start | bytes 92164
  66.9 3.8 copy-start.15
  74.7 3.1 copy-start.7
  74.7 3.1 copy-start.10
  74.7 3.0 copy-start.11
  117.1 43.7 %copy-start.8 = (bf16[2,192,1536]{2,1,0:T(8,128)(2,1)S(1)}, bf16[2,192,1536]{2,1,0:T(8,128)(2,1)}, u32[]{:S(2)}) copy-start(bf16[2,192,1536]{2,1,0:T(8,128)(2,1)} %param.23) | copy-start | bytes 3538948
  162.1 40.0 %copy-start.2 = (bf16[256,1536]{1,0:T(8,128)(2,1)S(1)}, bf16[256,1536]{1,0:T(8,128)(2,1)}, u32[]{:S(2)}) copy-start(bf16[256,1536]{1,0:T(8,128)(2,1)} %shard_map.158) | copy-start | bytes 2359300
  202.1 1.7 copy-start.3
  207.0 1.2 copy-start.12
  322.7 1.8 copy-start.4
  448.5 1.4 copy-start.6
  538.5 1.6 copy-start.5
  540.1 1.2 copy-start.14
  627.4 22.8 %copy-start.9 = (f32[8,192,128]{2,1,0:T(8,128)S(1)}, f32[8,192,128]{2,1,0:T(8,128)}, u32[]{:S(2)}) copy-start(f32[8,192,128]{2,1,0:T(8,128)} %get-tuple-element.22) | copy-start | bytes 2359300
  627.4 37.1 %copy-start.1 = (bf16[2,1536,40]{1,2,0:T(8,128)(2,1)S(1)}, bf16[2,1536,40]{1,2,0:T(8,128)(2,1)}, u32[]{:S(2)}) copy-start(bf16[2,1536,40]{1,2,0:T(8,128)(2,1)} %param.24) | copy-start | bytes 737284

commit v2 on v1

v2 whole, which is shorter than its diff:
```python
import functools

import jax
import jax.numpy as jnp
from jax import lax
from jax.experimental import pallas as pl
from jax.experimental.pallas import tpu as pltpu
from jax.sharding import PartitionSpec as P

EMBED_MULT = 12.0
ATT_SCALE = 0.015625
RESID_MULT = 0.22
LOGIT_DIV = 6.0
NORM_EPS = 1e-6
ROPE_THETA = 10000.0

D = 1536
HEAD = 64
BATCH = 512
STEPS = 4
LAYERS = 2
CACHE = 128
EXPERTS = 40
LOCAL_EXPERTS = 5
FF = 512
VOCAB = 6144
N = 8
SEQS = BATCH // N
ROWS = SEQS * STEPS
MESH = pl.DeviceIdType.MESH
F32 = jnp.float32
BF16 = jnp.bfloat16
VMEM_LIMIT = 60 * 1024 * 1024

ORDER_RS = ("me", "sib", "bs", "a", "ds", "dg", "as", "b")
ORDER_AG = ("me", "sib", "bs", "a", "as", "b", "ds", "dg")


def places():
    me = lax.axis_index("tp")
    k = lax.rem(me, 2)
    x = lax.rem(lax.div(me, 2), 2)
    y = lax.div(me, 4)
    step_x = 2 - 4 * x
    step_y = 4 - 8 * y
    a = me + step_x + k * (step_y - step_x)
    b = me + step_y + k * (step_x - step_y)
    dg = me + step_x + step_y
    s = 1 - 2 * k
    return {"me": me, "sib": me + s, "a": a, "as": a + s, "b": b, "bs": b + s, "dg": dg, "ds": dg + s}


def entry_barrier(at, names=("sib", "a", "b")):
    barrier = pltpu.get_barrier_semaphore()
    for name in names:
        pl.semaphore_signal(barrier, inc=1, device_id={"tp": at[name]}, device_id_type=MESH)
    pl.semaphore_wait(barrier, len(names))


def pick(pos, order, at):
    total = jnp.int32(0)
    for i, name in enumerate(order):
        total = total + jnp.where(pos == i, at[name], 0)
    return total


class Gather:
    def __init__(self, at, own, ubuf, send, recv):
        self.at, self.own, self.ubuf, self.send, self.recv = at, own, ubuf, send, recv

    def copy(self, src, origin, target, slot):
        return pltpu.make_async_remote_copy(
            src_ref=src, dst_ref=self.ubuf.at[origin], send_sem=self.send.at[slot], recv_sem=self.recv.at[origin],
            device_id={"tp": target}, device_id_type=MESH)

    def item(self, slot):
        at = self.at
        if slot < 3:
            return self.copy(self.own, at["me"], at[("a", "b", "sib")[slot]], slot)
        name, target = (("a", "b"), ("a", "sib"), ("b", "sib"), ("dg", "sib"))[slot - 3]
        return self.copy(self.ubuf.at[at[name]], at[name], at[target], slot)

    def start(self, *slots):
        for slot in slots:
            self.item(slot).start()

    def arrive(self, name):
        origin = self.at[name]
        self.copy(self.own, origin, self.at["sib"], 0).wait_recv()

    def before(self, pos, rs):
        @pl.when(pos == 1)
        def _():
            self.start(1)
            self.arrive("sib")

        @pl.when(pos == 2)
        def _():
            self.arrive("a")
            self.start(3, 4)
            self.arrive("bs")

        @pl.when(pos == 4)
        def _():
            self.arrive("b")
            self.start(5)
            if rs:
                self.arrive("dg")
                self.start(6)
                self.arrive("ds")
            else:
                self.arrive("as")

        @pl.when(pos == 6)
        def _():
            if rs:
                self.arrive("as")
            else:
                self.arrive("dg")
                self.start(6)
                self.arrive("ds")

    def finish(self):
        for slot in range(7):
            self.item(slot).wait_send()


class Scatter:
    def __init__(self, at, tbuf, rbuf, send, recv):
        self.at, self.tbuf, self.rbuf, self.send, self.recv = at, tbuf, rbuf, send, recv

    def copy(self, slot, target):
        return pltpu.make_async_remote_copy(
            src_ref=self.tbuf.at[slot], dst_ref=self.rbuf.at[slot], send_sem=self.send.at[slot],
            recv_sem=self.recv.at[slot], device_id={"tp": target}, device_id_type=MESH)

    def arrive(self, slot):
        self.copy(slot, self.at["sib"]).wait_recv()

    def after(self, pos, acc, fin):
        at = self.at

        @pl.when(pos == 0)
        def _():
            fin[...] = acc[...]

        @pl.when((pos == 1) | (pos == 2) | (pos == 4) | (pos == 6))
        def _():
            slot = lax.div(pos, 2)
            self.tbuf[slot] = acc[...].astype(BF16)
            self.copy(slot, at["sib"]).start()

        @pl.when((pos == 3) | (pos == 5))
        def _():
            slot = lax.div(pos, 2)
            out = slot + 3
            self.arrive(slot)
            self.tbuf[out] = (acc[...] + self.rbuf[slot].astype(F32)).astype(BF16)
            self.copy(out, at["a"]).start()

        @pl.when(pos == 7)
        def _():
            self.arrive(3)
            self.arrive(5)
            self.tbuf[6] = (acc[...] + self.rbuf[3].astype(F32) + self.rbuf[5].astype(F32)).astype(BF16)
            self.copy(6, at["b"]).start()

    def finish(self, fin, hidden_in, gain_ref, hidden_ref, normed_ref):
        self.arrive(0)
        self.arrive(4)
        self.arrive(6)

        def chunk(c, carry):
            rows = pl.ds(pl.multiple_of(c * 32, 32), 32)
            total = fin[rows, :]
            for slot in (0, 4, 6):
                total = total + self.rbuf[slot, rows, :].astype(F32)
            total = total.astype(BF16).astype(F32)
            if hidden_in is None:
                hidden = EMBED_MULT * total
            else:
                hidden = hidden_in[rows, :] + RESID_MULT * total
            hidden_ref[rows, :] = hidden
            mean_sq = jnp.mean(hidden * hidden, axis=1, keepdims=True)
            normed_ref[rows, :] = (hidden * lax.rsqrt(mean_sq + NORM_EPS) * gain_ref[...]).astype(BF16)
            return carry

        lax.fori_loop(0, ROWS // 32, chunk, 0)
        for slot in range(7):
            self.copy(slot, self.at["sib"]).wait_send()


def gather_scratch():
    return [pltpu.VMEM((N, ROWS, D), BF16), pltpu.SemaphoreType.DMA((7,)), pltpu.SemaphoreType.DMA((N,))]


def scatter_scratch():
    return [pltpu.VMEM((ROWS, D), F32), pltpu.VMEM((ROWS, D), F32), pltpu.VMEM((7, ROWS, D), BF16),
            pltpu.VMEM((7, ROWS, D), BF16), pltpu.SemaphoreType.DMA((7,)), pltpu.SemaphoreType.DMA((7,))]


VM = pl.BlockSpec(memory_space=pltpu.VMEM)
RESIDUAL = (jax.ShapeDtypeStruct((ROWS, D), F32), jax.ShapeDtypeStruct((ROWS, D), BF16))
ANY = pl.BlockSpec(memory_space=pl.ANY)


def comm_params(ident):
    return pltpu.CompilerParams(collective_id=ident, has_side_effects=True, vmem_limit_bytes=VMEM_LIMIT)


def rows_kernel(count_ref, token_ref, row_ref, embed_ref, out_ref, buf, wide, sem):
    wide[...] = jnp.zeros_like(wide)
    count = count_ref[0]
    slots = buf.shape[0]

    def chunk(c, carry):
        base = c * slots
        width = jnp.minimum(slots, count - base)

        def issue(j, carry):
            pltpu.make_async_copy(embed_ref.at[lax.div(row_ref[base + j], 8)], buf.at[j], sem).start()
            return carry

        def place(j, carry):
            pltpu.make_async_copy(embed_ref.at[0], buf.at[j], sem).wait()
            return carry

        def move(j, carry):
            sub = lax.rem(row_ref[base + j], 8)
            block = buf[j].astype(F32)
            keep = lax.broadcasted_iota(jnp.int32, block.shape, 0) == sub
            line = jnp.sum(jnp.where(keep, block, 0.0), axis=0, keepdims=True)
            wide[pl.ds(token_ref[base + j], 1), :] = line
            return carry

        lax.fori_loop(0, width, issue, 0)
        lax.fori_loop(0, width, place, 0)
        lax.fori_loop(0, width, move, 0)
        return carry

    lax.fori_loop(0, lax.div(count + slots - 1, slots), chunk, 0)
    out_ref[...] = wide[...].astype(BF16)


def local_rows(ids, shard, embed):
    total = N * ROWS
    local = ids - shard * VOCAB
    inside = (local >= 0) & (local < VOCAB)
    rank = jnp.cumsum(inside.astype(jnp.int32)) - 1
    rank = jnp.where(inside, rank, -1)
    hit = rank[None, :] == jnp.arange(total)[:, None]
    token = jnp.sum(jnp.where(hit, jnp.arange(total)[None, :], 0), axis=1)
    row = jnp.sum(jnp.where(hit, local[None, :], 0), axis=1)
    count = jnp.sum(inside.astype(jnp.int32)).reshape(1)
    return pl.pallas_call(
        rows_kernel,
        out_shape=jax.ShapeDtypeStruct((total, D), BF16),
        grid_spec=pltpu.PrefetchScalarGridSpec(
            num_scalar_prefetch=3, grid=(1,),
            in_specs=[ANY],
            out_specs=pl.BlockSpec((total, D), lambda i, *_: (0, 0)),
            scratch_shapes=[pltpu.VMEM((256, 8, D), BF16), pltpu.VMEM((total, D), F32), pltpu.SemaphoreType.DMA]),
        compiler_params=pltpu.CompilerParams(vmem_limit_bytes=VMEM_LIMIT),
    )(count, token, row, embed.reshape(VOCAB // 8, 8, D))


def embed_kernel(rows_ref, gain_ref, hidden_ref, normed_ref, acc, fin, tbuf, rbuf, send, recv):
    at = places()
    entry_barrier(at)
    scatter = Scatter(at, tbuf, rbuf, send, recv)

    def body(pos, carry):
        acc[...] = rows_ref[pick(pos, ORDER_RS, at)].astype(F32)
        scatter.after(pos, acc, fin)
        return carry

    lax.fori_loop(0, N, body, 0)
    scatter.finish(fin, None, gain_ref, hidden_ref, normed_ref)


def embed_sum(rows, gain, ident):
    return pl.pallas_call(
        embed_kernel,
        out_shape=RESIDUAL,
        in_specs=[VM, VM], out_specs=(VM, VM),
        scratch_shapes=scatter_scratch(),
        compiler_params=comm_params(ident),
    )(rows.reshape(N, ROWS, D), gain)


HALF = 32
SLOTS = 4


def attend_half(base, start_ref, first_seq, qk, vv, planes, mixed_out):
    lane = lax.broadcasted_iota(jnp.int32, (8, 128), 1)
    row = lax.broadcasted_iota(jnp.int32, (8, 128), 0)
    first = lane < HEAD
    own = [(2 * j + lax.div(lane, HEAD)) == row for j in range(4)]
    groups = range(HALF // 8)

    def spread(twice):
        return jnp.concatenate([jnp.where(own[j], twice, 0.0) for j in range(4)], axis=1)

    starts = [start_ref[pl.ds(pl.multiple_of(first_seq + base + 8 * g, 8), 8), :] for g in groups]
    query, updates = [], []
    for g in groups:
        queries, keys, vals, hot = [], [], [], []
        for s in range(STEPS):
            span = pl.ds(pl.multiple_of(s * SEQS + base + 8 * g, 8), 8)
            left, right = qk[span, 0:128], qk[span, 128:256]
            left_r, right_r = pltpu.roll(left, HEAD, 1), pltpu.roll(right, HEAD, 1)
            queries += [spread(jnp.where(first, left, left_r)), spread(jnp.where(first, left_r, left)),
                        spread(jnp.where(first, right, right_r))]
            keys.append(spread(jnp.where(first, right_r, right)))
            vals.append(spread(vv[span, :]))
            hot.append(jnp.where(lane == starts[g] + s, 1.0, 0.0))
        query.append(jnp.concatenate(queries, axis=0).astype(BF16))
        hot_all = jnp.concatenate(hot, axis=0).astype(BF16)
        updates.append([
            lax.dot_general(jnp.concatenate(entry, axis=0).astype(BF16), hot_all, (((0,), (0,)), ((), ())),
                            preferred_element_type=F32) for entry in (keys, vals)])
    for g in groups:
        span = pl.ds(base + 8 * g, 8)
        fresh = jnp.where((lane >= starts[g]) & (lane < starts[g] + STEPS), 1.0, 0.0)
        fresh = jnp.broadcast_to(fresh[:, None, :], (8, HEAD, 128)) > 0.5
        for kind in range(2):
            old = planes[kind, span].astype(F32)
            planes[kind, span] = jnp.where(fresh, updates[g][kind].reshape(8, HEAD, 128), old).astype(BF16)
    scores = [jnp.dot(query[g], planes[0, pl.ds(base + 8 * g, 8)].reshape(8 * HEAD, 128), preferred_element_type=F32)
              for g in groups]
    probs = []
    for g in groups:
        valid = [jnp.where(lane <= starts[g] + s, 0.0, -jnp.inf) for s in range(STEPS)]
        score = scores[g] * ATT_SCALE + jnp.concatenate([valid[s] for s in range(STEPS) for h in range(3)], axis=0)
        weight = jnp.exp(score - jnp.max(score, axis=1, keepdims=True))
        probs.append((weight / jnp.sum(weight, axis=1, keepdims=True)).astype(BF16))
    mixed = [lax.dot_general(probs[g], planes[1, pl.ds(base + 8 * g, 8)].reshape(8 * HEAD, 128),
                             (((1,), (1,)), ((), ())), preferred_element_type=F32) for g in groups]
    for g in groups:
        for s in range(STEPS):
            span = pl.ds(pl.multiple_of(s * SEQS + base + 8 * g, 8), 8)
            heads = []
            for h in range(3):
                part = mixed[g][8 * (3 * s + h):8 * (3 * s + h) + 8, :]
                total = sum(jnp.where(own[j], part[:, 128 * j:128 * j + 128], 0.0) for j in range(4))
                heads.append(total + pltpu.roll(total, HEAD, 1))
            mixed_out[span, 0:128] = jnp.where(first, heads[0], heads[1])
            mixed_out[span, 128:256] = heads[2]


def attn_kernel(layer, u_ref, w_ref, cos_ref, sin_ref, start_ref, w_out_ref, hidden_in, gain_ref, cache_ref, *rest):
    if layer > 0:
        rest = rest[1:]
    (hidden_ref, normed_ref, new_ref, ubuf, ag_send, ag_recv, acc, fin, tbuf, rbuf, rs_send, rs_recv,
     qk, vv, mixed, planes, in_sem, out_sem) = rest
    at = places()

    def plane_span(pos):
        return pl.ds(pick(pos, ORDER_RS, at) * SEQS, SEQS)

    def load(pos):
        slot = lax.rem(pos, SLOTS)
        return pltpu.make_async_copy(cache_ref.at[layer, :, plane_span(pos)], planes.at[slot], in_sem.at[slot])

    def store(pos):
        slot = lax.rem(pos, SLOTS)
        return pltpu.make_async_copy(planes.at[slot], new_ref.at[layer, :, plane_span(pos)], out_sem.at[slot])

    load(jnp.int32(0)).start()
    load(jnp.int32(1)).start()
    entry_barrier(at)
    gather = Gather(at, u_ref, ubuf, ag_send, ag_recv)
    scatter = Scatter(at, tbuf, rbuf, rs_send, rs_recv)
    gather.start(0, 2)
    ubuf[at["me"]] = u_ref[...]

    def body(pos, carry):
        gather.before(pos, True)
        blk = pick(pos, ORDER_RS, at)

        @pl.when(pos >= 2)
        def _():
            store(pos - 2).wait()

        @pl.when(pos < N - 2)
        def _():
            load(pos + 2).start()

        out = lax.dot_general(ubuf[blk], w_ref[...], (((1,), (1,)), ((), ())), preferred_element_type=F32)
        cos = cos_ref[blk]
        sin = sin_ref[blk]
        low = lax.rem(lax.broadcasted_iota(jnp.int32, (ROWS, 128), 1), HEAD) < HEAD // 2
        for half in range(2):
            part = out[:, half * 128:(half + 1) * 128]
            swapped = jnp.where(low, pltpu.roll(part, 128 - HEAD // 2, 1), pltpu.roll(part, HEAD // 2, 1))
            qk[:, half * 128:(half + 1) * 128] = (part * cos + swapped * sin).astype(BF16).astype(F32)
        vv[...] = out[:, 256:384].astype(BF16).astype(F32)
        load(pos).wait()

        def half_block(i, carry):
            attend_half(i * HALF, start_ref, blk * SEQS, qk, vv, planes.at[lax.rem(pos, SLOTS)], mixed)
            return carry

        lax.fori_loop(0, SEQS // HALF, half_block, 0)
        store(pos).start()
        acc[...] = jnp.dot(mixed[...].astype(BF16), w_out_ref[...], preferred_element_type=F32)
        scatter.after(pos, acc, fin)
        return carry

    lax.fori_loop(0, N, body, 0)
    store(jnp.int32(N - 2)).wait()
    store(jnp.int32(N - 1)).wait()
    gather.finish()
    scatter.finish(fin, hidden_in, gain_ref, hidden_ref, normed_ref)


def attention(layer, u, w_qkv, cos, sin, start_wide, w_out, hidden, gain, cache, new_cache, ident):
    args = [u, w_qkv, cos, sin, start_wide, w_out, hidden, gain, cache]
    in_specs = [VM] * 8 + [ANY]
    aliases = {}
    if new_cache is not None:
        args.append(new_cache)
        in_specs.append(ANY)
        aliases = {9: 2}
    return pl.pallas_call(
        functools.partial(attn_kernel, layer),
        out_shape=RESIDUAL + (jax.ShapeDtypeStruct(cache.shape, BF16),),
        in_specs=in_specs, out_specs=(VM, VM, ANY),
        scratch_shapes=gather_scratch() + scatter_scratch() + [
            pltpu.VMEM((ROWS, 256), F32), pltpu.VMEM((ROWS, 128), F32), pltpu.VMEM((ROWS, 256), F32),
            pltpu.VMEM((SLOTS, 2, SEQS, HEAD, CACHE), BF16), pltpu.SemaphoreType.DMA((SLOTS,)),
            pltpu.SemaphoreType.DMA((SLOTS,))],
        input_output_aliases=aliases,
        compiler_params=comm_params(ident),
    )(*args)


def moe_kernel(layer, u_ref, router_ref, ids_ref, hidden_in, gain_ref, gate_hbm, up_hbm, down_hbm, hidden_ref, normed_ref,
               ubuf, ag_send, ag_recv, acc, fin, tbuf, rbuf, rs_send, rs_recv, gate_v, up_v, down_v, hidden, gates, w_sem):
    def load(kind, e):
        src, dst = ((gate_hbm, gate_v), (up_hbm, up_v))[kind]
        return pltpu.make_async_copy(src.at[layer, e], dst.at[e], w_sem.at[kind, e])

    down_load = pltpu.make_async_copy(down_hbm.at[layer], down_v, w_sem.at[2, 0])
    for e in range(LOCAL_EXPERTS):
        load(0, e).start()
        load(1, e).start()
    down_load.start()
    at = places()
    entry_barrier(at)
    gather = Gather(at, u_ref, ubuf, ag_send, ag_recv)
    scatter = Scatter(at, tbuf, rbuf, rs_send, rs_recv)
    gather.start(0, 2)
    ubuf[at["me"]] = u_ref[...]
    lane = lax.broadcasted_iota(jnp.int32, (ROWS, 128), 1)

    def route(blk):
        ids = ids_ref[blk]
        chosen = lane == ids[:, 0:1]
        for j in range(1, 8):
            chosen = chosen | (lane == ids[:, j:j + 1])
        score = jnp.dot(ubuf[blk], router_ref[...], preferred_element_type=F32)
        masked = jnp.where(chosen, score, -jnp.inf)
        weight = jnp.exp(masked - jnp.max(masked, axis=1, keepdims=True))
        gates[...] = weight / jnp.sum(weight, axis=1, keepdims=True)

    def expert(blk, e):
        share = jnp.sum(jnp.where(lane == e, gates[...], 0.0), axis=1, keepdims=True)
        gate_act = jnp.dot(ubuf[blk], gate_v[e], preferred_element_type=F32)
        up_act = jnp.dot(ubuf[blk], up_v[e], preferred_element_type=F32)
        z = gate_act * jax.nn.sigmoid(gate_act) * up_act * share
        start = e * FF if isinstance(e, int) else pl.multiple_of(e * FF, FF)
        hidden[:, pl.ds(start, FF)] = z.astype(BF16)

    def down():
        for c in range(D // 512):
            cols = slice(c * 512, c * 512 + 512)
            acc[:, cols] = jnp.dot(hidden[...], down_v[:, cols], preferred_element_type=F32)

    def first_expert(e, carry):
        load(0, e).wait()
        load(1, e).wait()
        expert(at["me"], e)
        return carry

    route(at["me"])
    lax.fori_loop(0, LOCAL_EXPERTS, first_expert, 0)
    down_load.wait()
    down()
    fin[...] = acc[...]

    def body(pos, carry):
        gather.before(pos, True)
        blk = pick(pos, ORDER_RS, at)
        route(blk)
        for e in range(LOCAL_EXPERTS):
            expert(blk, e)
        down()
        scatter.after(pos, acc, fin)
        return carry

    lax.fori_loop(1, N, body, 0)
    gather.finish()
    scatter.finish(fin, hidden_in, gain_ref, hidden_ref, normed_ref)


def experts(layer, u, router, ids, hidden, gain, w_gate, w_up, w_down, ident):
    width = LOCAL_EXPERTS * FF
    return pl.pallas_call(
        functools.partial(moe_kernel, layer),
        out_shape=RESIDUAL,
        in_specs=[VM] * 5 + [ANY] * 3, out_specs=(VM, VM),
        scratch_shapes=gather_scratch() + scatter_scratch() + [
            pltpu.VMEM((LOCAL_EXPERTS, D, FF), BF16), pltpu.VMEM((LOCAL_EXPERTS, D, FF), BF16),
            pltpu.VMEM((width, D), BF16), pltpu.VMEM((ROWS, width), BF16), pltpu.VMEM((ROWS, 128), F32),
            pltpu.SemaphoreType.DMA((3, LOCAL_EXPERTS))],
        compiler_params=comm_params(ident),
    )(u, router, ids, hidden, gain, w_gate, w_up, w_down.reshape(LAYERS, width, D))


TILE = 1024
TILES = VOCAB // TILE
LAST_TILE = 512


def fold(logits, column, target, stat):
    part = (logits * (1.0 / LOGIT_DIV)).reshape(TILE // 8, 8, ROWS)
    peak = stat[0]
    top = jnp.maximum(peak, jnp.max(part, axis=0))
    row = 8 * lax.broadcasted_iota(jnp.int32, part.shape, 0) + lax.broadcasted_iota(jnp.int32, part.shape, 1)
    stat[0] = top
    stat[1] = stat[1] * jnp.exp(peak - top) + jnp.sum(jnp.exp(part - top), axis=0)
    stat[2] = stat[2] + jnp.sum(jnp.where(row == target - column, part, 0.0), axis=0)


def head_kernel(f_ref, target_ref, embed_ref, probs_ref, last_ref, ubuf, send, recv, table, even, odd, stat, mine, theirs,
                share_send, share_recv, sem):
    def load(c):
        rows = pl.ds(pl.multiple_of(c * TILE, TILE), TILE)
        return pltpu.make_async_copy(embed_ref.at[rows], table.at[rows], sem.at[c])

    for c in range(TILES):
        load(c).start()
    at = places()
    entry_barrier(at, ORDER_AG[1:])
    gather = Gather(at, f_ref, ubuf, send, recv)
    gather.start(0, 2)
    ubuf[at["me"]] = f_ref[...]

    def tile_logits(blk, start):
        return lax.dot_general(table[pl.ds(start, TILE), :], ubuf[blk], (((1,), (1,)), ((), ())), preferred_element_type=F32)

    def begin():
        stat[0] = jnp.full((8, ROWS), -1e30, F32)
        stat[1] = jnp.zeros((8, ROWS), F32)
        stat[2] = jnp.zeros((8, ROWS), F32)

    def end(blk):
        peak = stat[0]
        top = jnp.max(peak, axis=0, keepdims=True)
        mine[0, pl.ds(blk, 1), :] = top
        mine[1, pl.ds(blk, 1), :] = jnp.sum(stat[1] * jnp.exp(peak - top), axis=0, keepdims=True)
        mine[2, pl.ds(blk, 1), :] = jnp.sum(stat[2], axis=0, keepdims=True)
        last_ref[blk] = ubuf[blk, ROWS - SEQS:ROWS, :]

    def first_tile(c, carry):
        load(c).wait()
        even[...] = tile_logits(at["me"], pl.multiple_of(c * TILE, TILE))
        fold(even[...], c * TILE, target_ref[at["me"]], stat)
        return carry

    begin()
    lax.fori_loop(0, TILES, first_tile, 0)
    end(at["me"])

    def body(pos, carry):
        gather.before(pos, False)
        blk = pick(pos, ORDER_AG, at)
        target = target_ref[blk]
        begin()
        bufs = (even, odd)
        even[...] = tile_logits(blk, 0)
        for c in range(1, TILES + 1):
            if c < TILES:
                bufs[c % 2][...] = tile_logits(blk, c * TILE)
            fold(bufs[(c - 1) % 2][...], (c - 1) * TILE, target, stat)
        end(blk)
        return carry

    lax.fori_loop(1, N, body, 0)
    gather.finish()
    me = at["me"]
    copies = [pltpu.make_async_remote_copy(
        src_ref=mine, dst_ref=theirs.at[shift], send_sem=share_send.at[shift], recv_sem=share_recv.at[shift],
        device_id={"tp": lax.rem(me + shift, N)}, device_id_type=MESH) for shift in range(1, N)]
    for item in copies:
        item.start()
    theirs[0] = mine[...]
    for item in copies:
        item.wait()
    peak = functools.reduce(jnp.maximum, [theirs[i, 0] for i in range(N)])
    total = sum(theirs[i, 1] * jnp.exp(theirs[i, 0] - peak) for i in range(N))
    picked = sum(theirs[i, 2] for i in range(N))
    probs_ref[...] = picked - peak - jnp.log(total)


def head(f, target, embed, ident):
    return pl.pallas_call(
        head_kernel,
        out_shape=(jax.ShapeDtypeStruct((N, ROWS), F32), jax.ShapeDtypeStruct((N, SEQS, D), BF16)),
        in_specs=[VM, VM, ANY], out_specs=(VM, VM),
        scratch_shapes=gather_scratch() + [
            pltpu.VMEM((VOCAB, D), BF16), pltpu.VMEM((TILE, ROWS), F32), pltpu.VMEM((TILE, ROWS), F32),
            pltpu.VMEM((3, 8, ROWS), F32), pltpu.VMEM((3, N, ROWS), F32), pltpu.VMEM((N, 3, N, ROWS), F32),
            pltpu.SemaphoreType.DMA((N,)), pltpu.SemaphoreType.DMA((N,)), pltpu.SemaphoreType.DMA((TILES,))],
        compiler_params=comm_params(ident),
    )(f, target, embed)


def last_kernel(f_ref, embed_ref, logits_ref):
    logits_ref[...] = lax.dot_general(f_ref[...], embed_ref[...], (((1,), (1,)), ((), ())),
                                      preferred_element_type=F32) * (1.0 / LOGIT_DIV)


def last_step(f, embed):
    return pl.pallas_call(
        last_kernel,
        out_shape=jax.ShapeDtypeStruct((BATCH, VOCAB), F32),
        grid=(VOCAB // LAST_TILE,),
        in_specs=[pl.BlockSpec((BATCH, D), lambda c: (0, 0)), pl.BlockSpec((LAST_TILE, D), lambda c: (c, 0))],
        out_specs=pl.BlockSpec((BATCH, LAST_TILE), lambda c: (0, c)),
        compiler_params=pltpu.CompilerParams(dimension_semantics=("arbitrary",), vmem_limit_bytes=VMEM_LIMIT),
    )(f, embed)


def by_block(values):
    return values.reshape(N, SEQS, values.shape[1]).transpose(0, 2, 1)


def solution(mesh):
    cache_spec = P(None, None, 'dp', None, 'tp', None)
    expert_spec = P(None, 'tp', None, None)
    in_specs = (P('dp', None), P('dp'), cache_spec, P(None, None, 'dp', None), P('tp', None), P(None, None), P(None, None, 'tp'), P(None, None, 'tp'), P(None, None, 'tp'), P(None, 'tp', None), P(None, None, None), expert_spec, expert_spec, expert_spec)
    out_specs = (P('dp', None), P('dp', 'tp'), cache_spec)

    def decode_local(tokens, start_pos, kv_cache, expert_ids, embed, norm_gain, w_query, w_key, w_value, w_out, w_router, w_gate, w_up, w_down):
        shard = lax.axis_index('tp')
        cache = kv_cache.transpose(0, 1, 2, 4, 5, 3).reshape(LAYERS, 2, BATCH, HEAD, CACHE)

        gains = norm_gain[:, None, :]
        ids = by_block(tokens[:, :STEPS]).reshape(-1)
        rows = local_rows(ids, shard, embed)
        hidden, normed = embed_sum(rows, gains[0], 0)

        pos = by_block(start_pos[:, None] + jnp.arange(STEPS)[None, :]).reshape(N, ROWS)
        inv_freq = ROPE_THETA ** (-2.0 * jnp.arange(HEAD // 2, dtype=F32) / HEAD)
        angles = pos.astype(F32)[:, :, None] * inv_freq
        cos, sin = jnp.cos(angles), jnp.sin(angles)
        cos = jnp.concatenate([cos] * 4, axis=-1)
        sin = jnp.concatenate([-sin, sin, -sin, sin], axis=-1)
        start_wide = jnp.broadcast_to(start_pos[:, None], (BATCH, 128))

        wq, wk, wv = (w.transpose(0, 2, 1) for w in (w_query, w_key, w_value))
        w_qkv = jnp.concatenate([wq, wk, wv, wv], axis=1)
        w_out_wide = jnp.concatenate([w_out, jnp.zeros((LAYERS, 64, D), BF16)], axis=1)

        first_expert = shard * LOCAL_EXPERTS
        turned = lax.rem(jnp.arange(EXPERTS) + first_expert, EXPERTS)
        router = jnp.take(w_router, turned, axis=2)
        router = jnp.concatenate([router, jnp.zeros((LAYERS, D, 128 - EXPERTS), BF16)], axis=2)
        routed = lax.rem(expert_ids + (EXPERTS - first_expert), EXPERTS)
        routed = routed.reshape(STEPS, LAYERS, N, SEQS, 8).transpose(1, 2, 0, 3, 4).reshape(LAYERS, N, ROWS, 8)

        new_cache = None
        for layer in range(LAYERS):
            hidden, normed, new_cache = attention(layer, normed, w_qkv[layer], cos, sin, start_wide, w_out_wide[layer], hidden,
                                                  gains[2 * layer + 1], cache, new_cache, 1 + 2 * layer)
            hidden, normed = experts(layer, normed, router[layer], routed[layer], hidden, gains[2 * layer + 2],
                                     w_gate, w_up, w_down, 2 + 2 * layer)

        target = by_block(tokens[:, 1:] - shard * VOCAB).reshape(N, 1, ROWS)
        log_probs, f_last = head(normed, target, embed, 5)
        logits = last_step(f_last.reshape(BATCH, D), embed)
        log_probs = log_probs.reshape(N, STEPS, SEQS).transpose(0, 2, 1).reshape(BATCH, STEPS)
        new_cache = new_cache.reshape(LAYERS, 2, BATCH, 1, HEAD, CACHE).transpose(0, 1, 2, 5, 3, 4)
        return log_probs, logits, new_cache

    return jax.shard_map(decode_local, mesh=mesh, in_specs=in_specs, out_specs=out_specs, check_vma=False)
```

time: 671 us -> 493 us (0.73)
  Pallas kernels: 591 us -> 437 us
  other arithmetic: 55.5 us -> 14.7 us
  local copies, waits for them, and re-layouts: 17.3 us -> 34.8 us
    pallas_call x12 -> x7, Pallas kernels: 574 us -> 420 us  [the longest x2 157 us: experts(): pl.pallas_call(functools.partial(moe_kernel, layer), out_shape=RESIDUAL,...]
    reduce_or x1 -> x0, other arithmetic: 22.6 us -> none  [decode_local(): chosen = jnp.any(expert_ids[..., None] == lanes, axis=3).astype(F32)]
    unnamed x33 -> x23, local copies, waits for them, and re-layouts: 2.33 us -> 23.1 us
    reduce_sum x7 -> x0, other arithmetic: 10.2 us -> none  [the longest x5 8.5 us: rms_norm(): mean_sq = jnp.mean(hidden * hidden, axis=-1, keepdims=True)]
    convert_element_type x5 -> x0, other arithmetic: 7.26 us -> none  [rms_norm(): return (hidden * lax.rsqrt(mean_sq + NORM_EPS) * gain).astype(BF16)]
where the time goes in v2:
time: 493 us; the launch traced here: 488 us
  Pallas kernels  437 us (89%)
  local copies, waits for them, and re-layouts  34.8 us (7%)
  other arithmetic  14.7 us (3%)
    pallas_call x2, Pallas kernels, experts(): pl.pallas_call(functools.partial(moe_kernel, layer), out_shape=RESIDUAL,...  157 us
    pallas_call x2, Pallas kernels, attention(): pl.pallas_call(functools.partial(attn_kernel, layer), out_shape=RESIDUAL...  135 us
    pallas_call x1, Pallas kernels, head(): pl.pallas_call(head_kernel, out_shape=(jax.ShapeDtypeStruct((N, ROWS), F3...  66.2 us
    pallas_call x1, Pallas kernels, embed_sum(): pl.pallas_call(embed_kernel, out_shape=RESIDUAL, in_specs=[VM, VM], out_s...  43 us
    unnamed x23, local copies, waits for them, and re-layouts  23.1 us
    pallas_call x1, Pallas kernels, last_step(): pl.pallas_call(last_kernel, out_shape=jax.ShapeDtypeStruct((BATCH, VOCAB)...  19.5 us
    pallas_call x1, Pallas kernels, local_rows(): pl.pallas_call(rows_kernel, out_shape=jax.ShapeDtypeStruct((total, D), BF...  16.6 us

profile of v2, /device:TPU:0, one launch (start us, length us, event | category | flops | bytes accessed | tf_op | source)
XLA Modules:
  0.0 487.7 jit_solution(13579617029998338034)
XLA Ops:
  0.6 0.0 copy-start
  0.7 0.8 and_convert_fusion
  1.4 0.1 sub.44
  1.5 0.1 sub.46
  1.6 0.1 reshape.194
  1.7 0.1 reshape.192
  1.8 0.3 reduce-window.9
  2.0 0.1 slice.78
  2.2 0.1 slice_reduce_fusion
  2.3 0.1 bitcast_select_fusion
  2.3 5.7 %select_reduce_fusion = (s32[2048]{0:T(1024)}, s32[2048]{0:T(1024)}) fusion(s32[2048]{0:T(1024)S(1)} %sub.46, s32[2048]{0:T(1024)S(1)} %bitcast_select_fusion), kind=kLoop, calls=%fused_computation.1 | loop fusion | flops 20967424 | bytes 32768 | tf_op jit(solution)/shard_map/reduce_sum | solution.py:253
  8.0 0.7 fusion.6
  8.7 0.0 copy-start.7
  8.7 16.6 %shard_map.157 = bf16[2048,1536]{1,0:T(8,128)(2,1)} custom-call(s32[1]{0:T(128)} %bitcast.count_ref, s32[2048]{0:T(1024)} %get-tuple-element.39.token_ref, s32[2048]{0:T(1024)} %get-tuple-element.38.row_ref, bf16[768,8,1536]{2,1,0:T(8,128)(2,1)} %bitcast.59), custom_call_target="tpu_custom_call" | custom-call | tf_op jit(solution)/shard_map/pallas_call | solution.py:255
  25.3 0.0 copy-start.9
  25.3 0.0 copy-done.7
  25.3 0.6 fusion.8
  25.9 43.0 %shard_map.158 = (f32[256,1536]{1,0:T(8,128)}, bf16[256,1536]{1,0:T(8,128)(2,1)}) custom-call(bf16[8,256,1536]{2,1,0:T(8,128)(2,1)} %bitcast.65, f32[1,1536]{1,0:T(1,128)} %get-tuple-element.53.gain_ref), custom_call_target="tpu_custom_call" | custom-call | tf_op jit(solution)/shard_map/pallas_call | solution.py:282
  68.9 0.0 copy-done.9
  68.9 0.1 add.78
  69.0 0.1 add.80
  69.1 0.1 add.82
  69.2 0.0 copy-start.2
  69.2 0.0 copy-start.4
  69.2 0.0 copy-start.5
  69.3 3.7 fusion.4
  73.0 3.0 pad_maximum_fusion.1
  76.0 0.0 copy-done.2
  76.0 0.0 copy-done.4
  76.0 0.0 copy-done.5
  76.0 0.0 copy-start.3
  76.1 0.2 pad_maximum_fusion
  76.3 1.6 slice_bitcast_fusion
  77.8 0.0 copy-done.3
  77.8 1.2 fusion.1
  79.1 0.8 broadcast_in_dim.50.start_ref
  79.9 66.9 %shard_map.159 = (f32[256,1536]{1,0:T(8,128)}, bf16[256,1536]{1,0:T(8,128)(2,1)}, bf16[2,2,512,64,128]{4,3,2,1,0:T(8,128)(2,1)}) custom-call(bf16[256,1536]{1,0:T(8,128)(2,1)} %get-tuple-element.16.u_ref, bf16[384,1536]{1,0:T(8,128)(2,1)} %get-tuple-element.43.w_ref, f32[8,256,128]{2,1,0:T(8,128)} %get-tuple-element.58.cos_ref, ...), custom_call_target="tpu_custom_call" | custom-call | tf_op jit(solution)/shard_map/pallas_call | solution.py:426
  146.8 0.0 copy-done
  146.8 0.0 copy-start.6
  146.8 1.5 gather_fusion
  148.4 0.4 copy.35
  148.8 0.1 select_bitcast_fusion
  148.9 1.0 fusion.3
  149.9 0.0 copy-done.6
  149.9 0.1 add_remainder_fusion
  150.0 0.1 reshape.183
  150.1 0.6 copy.36
  150.7 1.4 fusion.7
  152.2 79.4 %shard_map.160 = (f32[256,1536]{1,0:T(8,128)}, bf16[256,1536]{1,0:T(8,128)(2,1)}) custom-call(bf16[256,1536]{1,0:T(8,128)(2,1)} %get-tuple-element.18.u_ref, bf16[1536,128]{1,0:T(8,128)(2,1)} %get-tuple-element.49.router_ref, s32[8,256,8]{2,1,0:T(8,128)} %bitcast.68, f32[256,1536]{1,0:T(8,128)} %get-tuple-element.19.hidden_in, ...), custom_call_target="tpu_custom_call" | custom-call | tf_op jit(solution)/shard_map/pallas_call | solution.py:510
  231.5 67.9 %shard_map.161 = (f32[256,1536]{1,0:T(8,128)}, bf16[256,1536]{1,0:T(8,128)(2,1)}, bf16[2,2,512,64,128]{4,3,2,1,0:T(8,128)(2,1)}) custom-call(bf16[256,1536]{1,0:T(8,128)(2,1)} %get-tuple-element.20.u_ref, bf16[384,1536]{1,0:T(8,128)(2,1)} %get-tuple-element.42.w_ref, f32[8,256,128]{2,1,0:T(8,128)} %get-tuple-element.58.cos_ref, ...), custom_call_target="tpu_custom_call", output_to_operand_aliasing={{2}: (9, {})} | custom-call | tf_op jit(solution)/shard_map/pallas_call | solution.py:426
  299.4 0.0 copy-start.8
  299.4 77.7 %shard_map.162 = (f32[256,1536]{1,0:T(8,128)}, bf16[256,1536]{1,0:T(8,128)(2,1)}) custom-call(bf16[256,1536]{1,0:T(8,128)(2,1)} %get-tuple-element.23.u_ref, bf16[1536,128]{1,0:T(8,128)(2,1)} %get-tuple-element.48.router_ref, s32[8,256,8]{2,1,0:T(8,128)} %bitcast.67, f32[256,1536]{1,0:T(8,128)} %get-tuple-element.24.hidden_in, ...), custom_call_target="tpu_custom_call" | custom-call | tf_op jit(solution)/shard_map/pallas_call | solution.py:510
  377.1 0.0 copy-done.8
  377.2 0.1 reshape.185
  377.2 0.7 reshape.186.target_ref
  377.9 66.2 %shard_map.163 = (f32[8,256]{1,0:T(8,128)}, bf16[8,64,1536]{2,1,0:T(8,128)(2,1)}) custom-call(bf16[256,1536]{1,0:T(8,128)(2,1)} %get-tuple-element.25.f_ref, s32[8,1,256]{2,1,0:T(1,128)} %reshape.186.target_ref, bf16[6144,1536]{1,0:T(8,128)(2,1)} %embed_ref.3), custom_call_target="tpu_custom_call" | custom-call | tf_op jit(solution)/shard_map/pallas_call | solution.py:609
  444.1 0.0 copy-start.10
  444.1 19.5 %shard_map.164 = f32[512,6144]{1,0:T(8,128)} custom-call(bf16[512,1536]{1,0:T(8,128)(2,1)} %bitcast.69, bf16[6144,1536]{1,0:T(8,128)(2,1)} %embed_ref.3), custom_call_target="tpu_custom_call" | custom-call | tf_op jit(solution)/shard_map/pallas_call | solution.py:627
  463.6 0.0 copy-done.10
  463.6 0.1 reshape.187
  463.7 0.7 reshape.188
  464.4 0.0 copy-start.1
  464.4 23.0 %copy.46 = bf16[2,2,512,128,1,64]{3,5,4,2,1,0:T(8,128)(2,1)} copy(bf16[2,2,512,128,1,64]{3,5,4,2,1,0:T(8,128)(2,1)} %bitcast.62) | data formatting | bytes 67108864
  487.5 0.0 copy-done.1
  (13 shorter events, 0.1 us)
Async XLA Ops:
  0.6 146.2 %copy-start = (bf16[2,1536,40]{1,2,0:T(8,128)(2,1)S(1)}, bf16[2,1536,40]{1,2,0:T(8,128)(2,1)}, u32[]{:S(2)}) copy-start(bf16[2,1536,40]{1,2,0:T(8,128)(2,1)} %param.24) | copy-start | bytes 737284
  8.7 16.6 %copy-start.7 = (f32[5,1536]{1,0:T(8,128)S(1)}, f32[5,1536]{1,0:T(8,128)}, u32[]{:S(2)}) copy-start(f32[5,1536]{1,0:T(8,128)} %param.19) | copy-start | bytes 92164
  25.3 43.6 %copy-start.9 = (s32[512]{0:T(512)S(1)}, s32[512]{0:T(512)}, u32[]{:S(2)}) copy-start(s32[512]{0:T(512)} %param.15) | copy-start | bytes 6148
  69.2 6.8 %copy-start.2 = (bf16[2,1536,192]{1,2,0:T(8,128)(2,1)S(1)}, bf16[2,1536,192]{1,2,0:T(8,128)(2,1)}, u32[]{:S(2)}) copy-start(bf16[2,1536,192]{1,2,0:T(8,128)(2,1)} %param.20) | copy-start | bytes 3538948
  69.2 6.8 %copy-start.4 = (bf16[2,1536,64]{1,2,0:T(8,128)(2,1)S(1)}, bf16[2,1536,64]{1,2,0:T(8,128)(2,1)}, u32[]{:S(2)}) copy-start(bf16[2,1536,64]{1,2,0:T(8,128)(2,1)} %param.22) | copy-start | bytes 1179652
  69.2 6.8 %copy-start.5 = (bf16[2,1536,64]{1,2,0:T(8,128)(2,1)S(1)}, bf16[2,1536,64]{1,2,0:T(8,128)(2,1)}, u32[]{:S(2)}) copy-start(bf16[2,1536,64]{1,2,0:T(8,128)(2,1)} %param.21) | copy-start | bytes 1179652
  76.0 1.8 copy-start.3
  146.8 3.1 copy-start.6
  299.4 77.7 %copy-start.8 = (s32[512,5]{0,1:T(8,128)S(1)}, s32[512,5]{0,1:T(8,128)}, u32[]{:S(2)}) copy-start(s32[512,5]{0,1:T(8,128)} %param.14) | copy-start | bytes 30724
  444.1 19.5 %copy-start.10 = (f32[8,256]{1,0:T(8,128)S(1)}, f32[8,256]{1,0:T(8,128)}, u32[]{:S(2)}) copy-start(f32[8,256]{1,0:T(8,128)} %get-tuple-element.26) | copy-start | bytes 24580
  464.4 23.0 %copy-start.1 = (bf16[2,1536,40]{1,2,0:T(8,128)(2,1)S(1)}, bf16[2,1536,40]{1,2,0:T(8,128)(2,1)}, u32[]{:S(2)}) copy-start(bf16[2,1536,40]{1,2,0:T(8,128)(2,1)} %param.24) | copy-start | bytes 737284

commit v3 on v2

--- a/solution.py
+++ b/solution.py
@@ -32,8 +32,9 @@
 BF16 = jnp.bfloat16
 VMEM_LIMIT = 60 * 1024 * 1024
 
-ORDER_RS = ("me", "sib", "bs", "a", "ds", "dg", "as", "b")
-ORDER_AG = ("me", "sib", "bs", "a", "as", "b", "ds", "dg")
+ORDER_RS = ("sib", "bs", "a", "ds", "dg", "as", "b", "me")
+ORDER_AG = ("me", "sib", "bs", "a", "ds", "dg", "as", "b")
+ORDER_EMBED = ("sib", "ds", "dg", "bs", "a", "as", "b", "me")
 
 
 def places():
@@ -88,37 +89,28 @@
         origin = self.at[name]
         self.copy(self.own, origin, self.at["sib"], 0).wait_recv()
 
-    def before(self, pos, rs):
-        @pl.when(pos == 1)
-        def _():
-            self.start(1)
+    def before(self, pos, order):
+        @pl.when(pos == order.index("sib"))
+        def _():
             self.arrive("sib")
 
-        @pl.when(pos == 2)
+        @pl.when(pos == order.index("bs"))
         def _():
             self.arrive("a")
-            self.start(3, 4)
+            self.start(3, 4, 1)
             self.arrive("bs")
 
-        @pl.when(pos == 4)
+        @pl.when(pos == order.index("ds"))
+        def _():
+            self.arrive("dg")
+            self.start(6)
+            self.arrive("ds")
+
+        @pl.when(pos == order.index("as"))
         def _():
             self.arrive("b")
             self.start(5)
-            if rs:
-                self.arrive("dg")
-                self.start(6)
-                self.arrive("ds")
-            else:
-                self.arrive("as")
-
-        @pl.when(pos == 6)
-        def _():
-            if rs:
-                self.arrive("as")
-            else:
-                self.arrive("dg")
-                self.start(6)
-                self.arrive("ds")
+            self.arrive("as")
 
     def finish(self):
         for slot in range(7):
@@ -137,42 +129,38 @@
     def arrive(self, slot):
         self.copy(slot, self.at["sib"]).wait_recv()
 
-    def after(self, pos, acc, fin):
+    def after(self, pos, acc, far_first=False):
         at = self.at
 
-        @pl.when(pos == 0)
-        def _():
-            fin[...] = acc[...]
-
-        @pl.when((pos == 1) | (pos == 2) | (pos == 4) | (pos == 6))
-        def _():
-            slot = lax.div(pos, 2)
+        @pl.when((pos == 0) | (pos == 1) | (pos == 3) | (pos == 5))
+        def _():
+            slot = lax.div(pos + 1, 2)
             self.tbuf[slot] = acc[...].astype(BF16)
             self.copy(slot, at["sib"]).start()
 
-        @pl.when((pos == 3) | (pos == 5))
+        @pl.when((pos == 2) | (pos == 4))
         def _():
             slot = lax.div(pos, 2)
-            out = slot + 3
+            out = 6 - slot if far_first else slot + 3
             self.arrive(slot)
             self.tbuf[out] = (acc[...] + self.rbuf[slot].astype(F32)).astype(BF16)
             self.copy(out, at["a"]).start()
 
-        @pl.when(pos == 7)
+        @pl.when(pos == 6)
         def _():
             self.arrive(3)
             self.arrive(5)
             self.tbuf[6] = (acc[...] + self.rbuf[3].astype(F32) + self.rbuf[5].astype(F32)).astype(BF16)
             self.copy(6, at["b"]).start()
 
-    def finish(self, fin, hidden_in, gain_ref, hidden_ref, normed_ref):
+    def finish(self, acc, hidden_in, gain, hidden_ref, normed_ref):
         self.arrive(0)
         self.arrive(4)
         self.arrive(6)
 
         def chunk(c, carry):
             rows = pl.ds(pl.multiple_of(c * 32, 32), 32)
-            total = fin[rows, :]
+            total = acc[rows, :]
             for slot in (0, 4, 6):
                 total = total + self.rbuf[slot, rows, :].astype(F32)
             total = total.astype(BF16).astype(F32)
@@ -182,7 +170,7 @@
                 hidden = hidden_in[rows, :] + RESID_MULT * total
             hidden_ref[rows, :] = hidden
             mean_sq = jnp.mean(hidden * hidden, axis=1, keepdims=True)
-            normed_ref[rows, :] = (hidden * lax.rsqrt(mean_sq + NORM_EPS) * gain_ref[...]).astype(BF16)
+            normed_ref[rows, :] = (hidden * lax.rsqrt(mean_sq + NORM_EPS) * gain).astype(BF16)
             return carry
 
         lax.fori_loop(0, ROWS // 32, chunk, 0)
@@ -195,7 +183,7 @@
 
 
 def scatter_scratch():
-    return [pltpu.VMEM((ROWS, D), F32), pltpu.VMEM((ROWS, D), F32), pltpu.VMEM((7, ROWS, D), BF16),
+    return [pltpu.VMEM((ROWS, D), F32), pltpu.VMEM((7, ROWS, D), BF16),
             pltpu.VMEM((7, ROWS, D), BF16), pltpu.SemaphoreType.DMA((7,)), pltpu.SemaphoreType.DMA((7,))]
 
 
@@ -225,21 +213,23 @@
             pltpu.make_async_copy(embed_ref.at[0], buf.at[j], sem).wait()
             return carry
 
-        def move(j, carry):
-            sub = lax.rem(row_ref[base + j], 8)
-            block = buf[j].astype(F32)
-            keep = lax.broadcasted_iota(jnp.int32, block.shape, 0) == sub
-            line = jnp.sum(jnp.where(keep, block, 0.0), axis=0, keepdims=True)
-            wide[pl.ds(token_ref[base + j], 1), :] = line
+        def move(i, carry):
+            for j in range(4):
+                spot = base + 4 * i + j
+                sub = lax.rem(row_ref[spot], 8)
+                block = buf[4 * i + j].astype(F32)
+                keep = lax.broadcasted_iota(jnp.int32, block.shape, 0) == sub
+                line = jnp.sum(jnp.where(keep, block, 0.0), axis=0, keepdims=True)
+                wide[pl.ds(token_ref[spot], 1), :] = line
             return carry
 
         lax.fori_loop(0, width, issue, 0)
         lax.fori_loop(0, width, place, 0)
-        lax.fori_loop(0, width, move, 0)
+        lax.fori_loop(0, lax.div(width + 3, 4), move, 0)
         return carry
 
     lax.fori_loop(0, lax.div(count + slots - 1, slots), chunk, 0)
-    out_ref[...] = wide[...].astype(BF16)
+    out_ref[...] = wide[0:N * ROWS, :].astype(BF16)
 
 
 def local_rows(ids, shard, embed):
@@ -249,7 +239,7 @@
     rank = jnp.cumsum(inside.astype(jnp.int32)) - 1
     rank = jnp.where(inside, rank, -1)
     hit = rank[None, :] == jnp.arange(total)[:, None]
-    token = jnp.sum(jnp.where(hit, jnp.arange(total)[None, :], 0), axis=1)
+    token = jnp.sum(jnp.where(hit, jnp.arange(total)[None, :] - total, 0), axis=1) + total
     row = jnp.sum(jnp.where(hit, local[None, :], 0), axis=1)
     count = jnp.sum(inside.astype(jnp.int32)).reshape(1)
     return pl.pallas_call(
@@ -259,33 +249,33 @@
             num_scalar_prefetch=3, grid=(1,),
             in_specs=[ANY],
             out_specs=pl.BlockSpec((total, D), lambda i, *_: (0, 0)),
-            scratch_shapes=[pltpu.VMEM((256, 8, D), BF16), pltpu.VMEM((total, D), F32), pltpu.SemaphoreType.DMA]),
+            scratch_shapes=[pltpu.VMEM((256, 8, D), BF16), pltpu.VMEM((total + 8, D), F32), pltpu.SemaphoreType.DMA]),
         compiler_params=pltpu.CompilerParams(vmem_limit_bytes=VMEM_LIMIT),
     )(count, token, row, embed.reshape(VOCAB // 8, 8, D))
 
 
-def embed_kernel(rows_ref, gain_ref, hidden_ref, normed_ref, acc, fin, tbuf, rbuf, send, recv):
+def embed_kernel(rows_ref, gains_ref, hidden_ref, normed_ref, acc, tbuf, rbuf, send, recv):
     at = places()
     entry_barrier(at)
     scatter = Scatter(at, tbuf, rbuf, send, recv)
 
     def body(pos, carry):
-        acc[...] = rows_ref[pick(pos, ORDER_RS, at)].astype(F32)
-        scatter.after(pos, acc, fin)
+        acc[...] = rows_ref[pick(pos, ORDER_EMBED, at)].astype(F32)
+        scatter.after(pos, acc, far_first=True)
         return carry
 
     lax.fori_loop(0, N, body, 0)
-    scatter.finish(fin, None, gain_ref, hidden_ref, normed_ref)
-
-
-def embed_sum(rows, gain, ident):
+    scatter.finish(acc, None, gains_ref[0:1, :], hidden_ref, normed_ref)
+
+
+def embed_sum(rows, gains, ident):
     return pl.pallas_call(
         embed_kernel,
         out_shape=RESIDUAL,
         in_specs=[VM, VM], out_specs=(VM, VM),
         scratch_shapes=scatter_scratch(),
         compiler_params=comm_params(ident),
-    )(rows.reshape(N, ROWS, D), gain)
+    )(rows.reshape(N, ROWS, D), gains)
 
 
 HALF = 32
@@ -349,12 +339,22 @@
             mixed_out[span, 128:256] = heads[2]
 
 
-def attn_kernel(layer, u_ref, w_ref, cos_ref, sin_ref, start_ref, w_out_ref, hidden_in, gain_ref, cache_ref, *rest):
+def attn_kernel(layer, u_ref, cos_ref, sin_ref, start_ref, hidden_in, gains_ref, wq_ref, wk_ref, wv_ref, wo_ref, cache_ref,
+                *rest):
     if layer > 0:
         rest = rest[1:]
-    (hidden_ref, normed_ref, new_ref, ubuf, ag_send, ag_recv, acc, fin, tbuf, rbuf, rs_send, rs_recv,
-     qk, vv, mixed, planes, in_sem, out_sem) = rest
+    (hidden_ref, normed_ref, new_ref, ubuf, ag_send, ag_recv, acc, tbuf, rbuf, rs_send, rs_recv,
+     qk, vv, mixed, planes, w_qkv, w_out, in_sem, out_sem, w_sem) = rest
     at = places()
+    weights = [
+        pltpu.make_async_copy(wq_ref.at[layer], w_qkv.at[0:192], w_sem.at[0]),
+        pltpu.make_async_copy(wk_ref.at[layer], w_qkv.at[192:256], w_sem.at[1]),
+        pltpu.make_async_copy(wv_ref.at[layer], w_qkv.at[256:320], w_sem.at[2]),
+        pltpu.make_async_copy(wv_ref.at[layer], w_qkv.at[320:384], w_sem.at[3]),
+        pltpu.make_async_copy(wo_ref.at[layer], w_out.at[0:192], w_sem.at[4])]
+    for item in weights:
+        item.start()
+    w_out[192:256, :] = jnp.zeros((64, D), BF16)
 
     def plane_span(pos):
         return pl.ds(pick(pos, ORDER_RS, at) * SEQS, SEQS)
@@ -374,9 +374,11 @@
     scatter = Scatter(at, tbuf, rbuf, rs_send, rs_recv)
     gather.start(0, 2)
     ubuf[at["me"]] = u_ref[...]
+    for item in weights:
+        item.wait()
 
     def body(pos, carry):
-        gather.before(pos, True)
+        gather.before(pos, ORDER_RS)
         blk = pick(pos, ORDER_RS, at)
 
         @pl.when(pos >= 2)
@@ -387,7 +389,7 @@
         def _():
             load(pos + 2).start()
 
-        out = lax.dot_general(ubuf[blk], w_ref[...], (((1,), (1,)), ((), ())), preferred_element_type=F32)
+        out = lax.dot_general(ubuf[blk], w_qkv[...], (((1,), (1,)), ((), ())), preferred_element_type=F32)
         cos = cos_ref[blk]
         sin = sin_ref[blk]
         low = lax.rem(lax.broadcasted_iota(jnp.int32, (ROWS, 128), 1), HEAD) < HEAD // 2
@@ -404,40 +406,40 @@
 
         lax.fori_loop(0, SEQS // HALF, half_block, 0)
         store(pos).start()
-        acc[...] = jnp.dot(mixed[...].astype(BF16), w_out_ref[...], preferred_element_type=F32)
-        scatter.after(pos, acc, fin)
+        acc[...] = jnp.dot(mixed[...].astype(BF16), w_out[...], preferred_element_type=F32)
+        scatter.after(pos, acc)
         return carry
 
     lax.fori_loop(0, N, body, 0)
     store(jnp.int32(N - 2)).wait()
     store(jnp.int32(N - 1)).wait()
     gather.finish()
-    scatter.finish(fin, hidden_in, gain_ref, hidden_ref, normed_ref)
-
-
-def attention(layer, u, w_qkv, cos, sin, start_wide, w_out, hidden, gain, cache, new_cache, ident):
-    args = [u, w_qkv, cos, sin, start_wide, w_out, hidden, gain, cache]
-    in_specs = [VM] * 8 + [ANY]
+    scatter.finish(acc, hidden_in, gains_ref[2 * layer + 1:2 * layer + 2, :], hidden_ref, normed_ref)
+
+
+def attention(layer, u, cos, sin, start_wide, hidden, gains, weights, cache, new_cache, ident):
+    args = [u, cos, sin, start_wide, hidden, gains, *weights, cache]
+    in_specs = [VM] * 6 + [ANY] * 5
     aliases = {}
     if new_cache is not None:
         args.append(new_cache)
         in_specs.append(ANY)
-        aliases = {9: 2}
+        aliases = {11: 2}
     return pl.pallas_call(
         functools.partial(attn_kernel, layer),
         out_shape=RESIDUAL + (jax.ShapeDtypeStruct(cache.shape, BF16),),
         in_specs=in_specs, out_specs=(VM, VM, ANY),
         scratch_shapes=gather_scratch() + scatter_scratch() + [
             pltpu.VMEM((ROWS, 256), F32), pltpu.VMEM((ROWS, 128), F32), pltpu.VMEM((ROWS, 256), F32),
-            pltpu.VMEM((SLOTS, 2, SEQS, HEAD, CACHE), BF16), pltpu.SemaphoreType.DMA((SLOTS,)),
-            pltpu.SemaphoreType.DMA((SLOTS,))],
+            pltpu.VMEM((SLOTS, 2, SEQS, HEAD, CACHE), BF16), pltpu.VMEM((384, D), BF16), pltpu.VMEM((256, D), BF16),
+            pltpu.SemaphoreType.DMA((SLOTS,)), pltpu.SemaphoreType.DMA((SLOTS,)), pltpu.SemaphoreType.DMA((5,))],
         input_output_aliases=aliases,
         compiler_params=comm_params(ident),
     )(*args)
 
 
-def moe_kernel(layer, u_ref, router_ref, ids_ref, hidden_in, gain_ref, gate_hbm, up_hbm, down_hbm, hidden_ref, normed_ref,
-               ubuf, ag_send, ag_recv, acc, fin, tbuf, rbuf, rs_send, rs_recv, gate_v, up_v, down_v, hidden, gates, w_sem):
+def moe_kernel(layer, u_ref, router_ref, ids_ref, hidden_in, gains_ref, gate_hbm, up_hbm, down_hbm, hidden_ref, normed_ref,
+               ubuf, ag_send, ag_recv, acc, tbuf, rbuf, rs_send, rs_recv, gate_v, up_v, down_v, hidden, gates, w_sem):
     def load(kind, e):
         src, dst = ((gate_hbm, gate_v), (up_hbm, up_v))[kind]
         return pltpu.make_async_copy(src.at[layer, e], dst.at[e], w_sem.at[kind, e])
@@ -453,22 +455,24 @@
     scatter = Scatter(at, tbuf, rbuf, rs_send, rs_recv)
     gather.start(0, 2)
     ubuf[at["me"]] = u_ref[...]
-    lane = lax.broadcasted_iota(jnp.int32, (ROWS, 128), 1)
+    lane = lax.broadcasted_iota(jnp.int32, (ROWS, EXPERTS), 1)
 
     def route(blk):
         ids = ids_ref[blk]
         chosen = lane == ids[:, 0:1]
         for j in range(1, 8):
             chosen = chosen | (lane == ids[:, j:j + 1])
-        score = jnp.dot(ubuf[blk], router_ref[...], preferred_element_type=F32)
+        score = lax.dot_general(ubuf[blk], router_ref[layer], (((1,), (1,)), ((), ())), preferred_element_type=F32)
         masked = jnp.where(chosen, score, -jnp.inf)
         weight = jnp.exp(masked - jnp.max(masked, axis=1, keepdims=True))
         gates[...] = weight / jnp.sum(weight, axis=1, keepdims=True)
 
-    def expert(blk, e):
-        share = jnp.sum(jnp.where(lane == e, gates[...], 0.0), axis=1, keepdims=True)
-        gate_act = jnp.dot(ubuf[blk], gate_v[e], preferred_element_type=F32)
-        up_act = jnp.dot(ubuf[blk], up_v[e], preferred_element_type=F32)
+    def inner(blk, e):
+        return (jnp.dot(ubuf[blk], gate_v[e], preferred_element_type=F32),
+                jnp.dot(ubuf[blk], up_v[e], preferred_element_type=F32))
+
+    def activate(e, gate_act, up_act):
+        share = jnp.sum(jnp.where(lane == at["me"] * LOCAL_EXPERTS + e, gates[...], 0.0), axis=1, keepdims=True)
         z = gate_act * jax.nn.sigmoid(gate_act) * up_act * share
         start = e * FF if isinstance(e, int) else pl.multiple_of(e * FF, FF)
         hidden[:, pl.ds(start, FF)] = z.astype(BF16)
@@ -481,31 +485,35 @@
     def first_expert(e, carry):
         load(0, e).wait()
         load(1, e).wait()
-        expert(at["me"], e)
+        activate(e, *inner(at["sib"], e))
         return carry
 
-    route(at["me"])
+    gather.before(jnp.int32(0), ORDER_RS)
+    route(at["sib"])
     lax.fori_loop(0, LOCAL_EXPERTS, first_expert, 0)
     down_load.wait()
     down()
-    fin[...] = acc[...]
+    scatter.after(jnp.int32(0), acc)
 
     def body(pos, carry):
-        gather.before(pos, True)
+        gather.before(pos, ORDER_RS)
         blk = pick(pos, ORDER_RS, at)
+        acts = inner(blk, 0)
         route(blk)
         for e in range(LOCAL_EXPERTS):
-            expert(blk, e)
+            following = inner(blk, e + 1) if e + 1 < LOCAL_EXPERTS else None
+            activate(e, *acts)
+            acts = following
         down()
-        scatter.after(pos, acc, fin)
+        scatter.after(pos, acc)
         return carry
 
     lax.fori_loop(1, N, body, 0)
     gather.finish()
-    scatter.finish(fin, hidden_in, gain_ref, hidden_ref, normed_ref)
-
-
-def experts(layer, u, router, ids, hidden, gain, w_gate, w_up, w_down, ident):
+    scatter.finish(acc, hidden_in, gains_ref[2 * layer + 2:2 * layer + 3, :], hidden_ref, normed_ref)
+
+
+def experts(layer, u, router, ids, hidden, gains, w_gate, w_up, w_down, ident):
     width = LOCAL_EXPERTS * FF
     return pl.pallas_call(
         functools.partial(moe_kernel, layer),
@@ -513,15 +521,15 @@
         in_specs=[VM] * 5 + [ANY] * 3, out_specs=(VM, VM),
         scratch_shapes=gather_scratch() + scatter_scratch() + [
             pltpu.VMEM((LOCAL_EXPERTS, D, FF), BF16), pltpu.VMEM((LOCAL_EXPERTS, D, FF), BF16),
-            pltpu.VMEM((width, D), BF16), pltpu.VMEM((ROWS, width), BF16), pltpu.VMEM((ROWS, 128), F32),
+            pltpu.VMEM((width, D), BF16), pltpu.VMEM((ROWS, width), BF16), pltpu.VMEM((ROWS, EXPERTS), F32),
             pltpu.SemaphoreType.DMA((3, LOCAL_EXPERTS))],
         compiler_params=comm_params(ident),
-    )(u, router, ids, hidden, gain, w_gate, w_up, w_down.reshape(LAYERS, width, D))
+    )(u, router, ids, hidden, gains, w_gate, w_up, w_down.reshape(LAYERS, width, D))
 
 
 TILE = 1024
 TILES = VOCAB // TILE
-LAST_TILE = 512
+LAST_TILE = 384
 
 
 def fold(logits, column, target, stat):
@@ -575,7 +583,7 @@
     end(at["me"])
 
     def body(pos, carry):
-        gather.before(pos, False)
+        gather.before(pos, ORDER_AG)
         blk = pick(pos, ORDER_AG, at)
         target = target_ref[blk]
         begin()
@@ -618,20 +626,25 @@
     )(f, target, embed)
 
 
-def last_kernel(f_ref, embed_ref, logits_ref):
+def last_kernel(f_ref, embed_ref, cache_ref, logits_ref, new_ref):
     logits_ref[...] = lax.dot_general(f_ref[...], embed_ref[...], (((1,), (1,)), ((), ())),
                                       preferred_element_type=F32) * (1.0 / LOGIT_DIV)
-
-
-def last_step(f, embed):
-    return pl.pallas_call(
+    new_ref[...] = cache_ref[...]
+
+
+def last_step(f, embed, cache):
+    steps = VOCAB // LAST_TILE
+    flat = cache.reshape(LAYERS * 2 * BATCH, HEAD, CACHE)
+    plane_spec = pl.BlockSpec((flat.shape[0] // steps, HEAD, CACHE), lambda c: (c, 0, 0))
+    logits, flat = pl.pallas_call(
         last_kernel,
-        out_shape=jax.ShapeDtypeStruct((BATCH, VOCAB), F32),
-        grid=(VOCAB // LAST_TILE,),
-        in_specs=[pl.BlockSpec((BATCH, D), lambda c: (0, 0)), pl.BlockSpec((LAST_TILE, D), lambda c: (c, 0))],
-        out_specs=pl.BlockSpec((BATCH, LAST_TILE), lambda c: (0, c)),
+        out_shape=(jax.ShapeDtypeStruct((BATCH, VOCAB), F32), jax.ShapeDtypeStruct(flat.shape, BF16)),
+        grid=(steps,),
+        in_specs=[pl.BlockSpec((BATCH, D), lambda c: (0, 0)), pl.BlockSpec((LAST_TILE, D), lambda c: (c, 0)), plane_spec],
+        out_specs=(pl.BlockSpec((BATCH, LAST_TILE), lambda c: (0, c)), plane_spec),
         compiler_params=pltpu.CompilerParams(dimension_semantics=("arbitrary",), vmem_limit_bytes=VMEM_LIMIT),
-    )(f, embed)
+    )(f, embed, flat)
+    return logits, flat.reshape(cache.shape)
 
 
 def by_block(values):
@@ -648,10 +661,9 @@
         shard = lax.axis_index('tp')
         cache = kv_cache.transpose(0, 1, 2, 4, 5, 3).reshape(LAYERS, 2, BATCH, HEAD, CACHE)
 
-        gains = norm_gain[:, None, :]
         ids = by_block(tokens[:, :STEPS]).reshape(-1)
         rows = local_rows(ids, shard, embed)
-        hidden, normed = embed_sum(rows, gains[0], 0)
+        hidden, normed = embed_sum(rows, norm_gain, 0)
 
         pos = by_block(start_pos[:, None] + jnp.arange(STEPS)[None, :]).reshape(N, ROWS)
         inv_freq = ROPE_THETA ** (-2.0 * jnp.arange(HEAD // 2, dtype=F32) / HEAD)
@@ -661,27 +673,19 @@
         sin = jnp.concatenate([-sin, sin, -sin, sin], axis=-1)
         start_wide = jnp.broadcast_to(start_pos[:, None], (BATCH, 128))
 
-        wq, wk, wv = (w.transpose(0, 2, 1) for w in (w_query, w_key, w_value))
-        w_qkv = jnp.concatenate([wq, wk, wv, wv], axis=1)
-        w_out_wide = jnp.concatenate([w_out, jnp.zeros((LAYERS, 64, D), BF16)], axis=1)
-
-        first_expert = shard * LOCAL_EXPERTS
-        turned = lax.rem(jnp.arange(EXPERTS) + first_expert, EXPERTS)
-        router = jnp.take(w_router, turned, axis=2)
-        router = jnp.concatenate([router, jnp.zeros((LAYERS, D, 128 - EXPERTS), BF16)], axis=2)
-        routed = lax.rem(expert_ids + (EXPERTS - first_expert), EXPERTS)
-        routed = routed.reshape(STEPS, LAYERS, N, SEQS, 8).transpose(1, 2, 0, 3, 4).reshape(LAYERS, N, ROWS, 8)
+        weights = [w.transpose(0, 2, 1) for w in (w_query, w_key, w_value)] + [w_out]
+        router = w_router.transpose(0, 2, 1)
+        routed = expert_ids.reshape(STEPS, LAYERS, N, SEQS, 8).transpose(1, 2, 0, 3, 4).reshape(LAYERS, N, ROWS, 8)
 
         new_cache = None
         for layer in range(LAYERS):
-            hidden, normed, new_cache = attention(layer, normed, w_qkv[layer], cos, sin, start_wide, w_out_wide[layer], hidden,
-                                                  gains[2 * layer + 1], cache, new_cache, 1 + 2 * layer)
-            hidden, normed = experts(layer, normed, router[layer], routed[layer], hidden, gains[2 * layer + 2],
-                                     w_gate, w_up, w_down, 2 + 2 * layer)
+            hidden, normed, new_cache = attention(layer, normed, cos, sin, start_wide, hidden, norm_gain, weights, cache, new_cache,
+                                                  1 + 2 * layer)
+            hidden, normed = experts(layer, normed, router, routed[layer], hidden, norm_gain, w_gate, w_up, w_down, 2 + 2 * layer)
 
         target = by_block(tokens[:, 1:] - shard * VOCAB).reshape(N, 1, ROWS)
         log_probs, f_last = head(normed, target, embed, 5)
-        logits = last_step(f_last.reshape(BATCH, D), embed)
+        logits, new_cache = last_step(f_last.reshape(BATCH, D), embed, new_cache)
         log_probs = log_probs.reshape(N, STEPS, SEQS).transpose(0, 2, 1).reshape(BATCH, STEPS)
         new_cache = new_cache.reshape(LAYERS, 2, BATCH, 1, HEAD, CACHE).transpose(0, 1, 2, 5, 3, 4)
         return log_probs, logits, new_cache

time: 493 us -> 470 us (0.953)
  local copies, waits for them, and re-layouts: 34.8 us -> 8.26 us
    unnamed x23 -> x0, local copies, waits for them, and re-layouts: 23.1 us -> none
    pallas_call x1, Pallas kernels: 19.5 us -> 42 us  [last_step(): pl.pallas_call(last_kernel, out_shape=(jax.ShapeDtypeStruct((BATCH, VOCAB...]
    pallas_call x2, Pallas kernels: 157 us -> 148 us  [experts(): pl.pallas_call(functools.partial(moe_kernel, layer), out_shape=RESIDUAL,...]
    pallas_call x2, Pallas kernels: 135 us -> 128 us  [attention(): pl.pallas_call(functools.partial(attn_kernel, layer), out_shape=RESIDUAL...]
where the time goes in v3:
time: 470 us; the launch traced here: 461 us
  Pallas kernels  437 us (93%)
  other arithmetic  14.4 us (3%)
  local copies, waits for them, and re-layouts  8.26 us (2%)
    pallas_call x2, Pallas kernels, experts(): pl.pallas_call(functools.partial(moe_kernel, layer), out_shape=RESIDUAL,...  148 us
    pallas_call x2, Pallas kernels, attention(): pl.pallas_call(functools.partial(attn_kernel, layer), out_shape=RESIDUAL...  128 us
    pallas_call x1, Pallas kernels, head(): pl.pallas_call(head_kernel, out_shape=(jax.ShapeDtypeStruct((N, ROWS), F3...  65.1 us
    pallas_call x1, Pallas kernels, last_step(): pl.pallas_call(last_kernel, out_shape=(jax.ShapeDtypeStruct((BATCH, VOCAB...  42 us
    pallas_call x1, Pallas kernels, embed_sum(): pl.pallas_call(embed_kernel, out_shape=RESIDUAL, in_specs=[VM, VM], out_s...  40.4 us
    pallas_call x1, Pallas kernels, local_rows(): pl.pallas_call(rows_kernel, out_shape=jax.ShapeDtypeStruct((total, D), BF...  13.9 us

profile of v3, /device:TPU:0, one launch (start us, length us, event | category | flops | bytes accessed | tf_op | source)
XLA Modules:
  0.0 461.2 jit_solution(7065229042799986051)
XLA Ops:
  0.7 0.1 add.50
  0.7 0.8 add.46
  1.5 0.7 slice_subtract_fusion
  2.2 0.1 reshape.156
  2.3 0.7 reshape.157.target_ref
  3.0 0.1 add.48
  3.1 0.7 and_convert_fusion
  3.8 0.6 fusion.1
  4.4 0.1 reshape.165
  4.5 0.1 reshape.163
  4.6 0.3 reduce-window.9
  4.9 0.1 slice.27
  5.0 0.1 slice_reduce_fusion
  5.1 0.1 sub.45
  5.2 0.1 sub.47
  5.3 0.1 bitcast_select_fusion
  5.3 4.6 select_reduce_fusion
  10.0 0.6 broadcast_add_fusion.token_ref
  10.6 1.5 broadcast_in_dim.37.start_ref
  12.1 1.0 reshape.154
  13.1 0.6 copy.34
  13.7 1.4 fusion.2
  15.1 3.7 fusion
  18.9 3.0 pad_maximum_fusion
  21.9 13.9 %shard_map.157 = bf16[2048,1536]{1,0:T(8,128)(2,1)} custom-call(s32[1]{0:T(128)} %bitcast.count_ref, s32[2048]{0:T(1024)} %broadcast_add_fusion.token_ref, s32[2048]{0:T(1024)} %get-tuple-element.33.row_ref, bf16[768,8,1536]{2,1,0:T(8,128)(2,1)} %bitcast.45), custom_call_target="tpu_custom_call" | custom-call | tf_op jit(solution)/shard_map/pallas_call | solution.py:245
  35.8 40.4 %shard_map.158 = (f32[256,1536]{1,0:T(8,128)}, bf16[256,1536]{1,0:T(8,128)(2,1)}) custom-call(bf16[8,256,1536]{2,1,0:T(8,128)(2,1)} %bitcast.51, f32[5,1536]{1,0:T(8,128)} %gains_ref.9), custom_call_target="tpu_custom_call" | custom-call | tf_op jit(solution)/shard_map/pallas_call | solution.py:272
  76.2 63.7 %shard_map.159 = (f32[256,1536]{1,0:T(8,128)}, bf16[256,1536]{1,0:T(8,128)(2,1)}, bf16[2,2,512,64,128]{4,3,2,1,0:T(8,128)(2,1)}) custom-call(bf16[256,1536]{1,0:T(8,128)(2,1)} %get-tuple-element.18.u_ref, f32[8,256,128]{2,1,0:T(8,128)} %get-tuple-element.44.cos_ref, f32[8,256,128]{2,1,0:T(8,128)} %get-tuple-element.45.sin_ref, ...), custom_call_target="tpu_custom_call" | custom-call | tf_op jit(solution)/shard_map/pallas_call | solution.py:428
  139.9 74.2 %shard_map.160 = (f32[256,1536]{1,0:T(8,128)}, bf16[256,1536]{1,0:T(8,128)(2,1)}) custom-call(bf16[256,1536]{1,0:T(8,128)(2,1)} %get-tuple-element.20.u_ref, bf16[2,40,1536]{2,1,0:T(8,128)(2,1)} %bitcast.62, s32[8,256,8]{2,1,0:T(8,128)} %bitcast.56, f32[256,1536]{1,0:T(8,128)} %get-tuple-element.21.hidden_in, f32[5,1536]{1,0:T(8,128)} %gains_ref.9, ...), custom_call_target="tpu_custom_call" | custom-call | tf_op jit(solution)/shard_map/pallas_call | solution.py:518
  214.1 63.8 %shard_map.161 = (f32[256,1536]{1,0:T(8,128)}, bf16[256,1536]{1,0:T(8,128)(2,1)}, bf16[2,2,512,64,128]{4,3,2,1,0:T(8,128)(2,1)}) custom-call(bf16[256,1536]{1,0:T(8,128)(2,1)} %get-tuple-element.22.u_ref, f32[8,256,128]{2,1,0:T(8,128)} %get-tuple-element.44.cos_ref, f32[8,256,128]{2,1,0:T(8,128)} %get-tuple-element.45.sin_ref, ...), custom_call_target="tpu_custom_call", output_to_operand_aliasing={{2}: (11, {})} | custom-call | tf_op jit(solution)/shard_map/pallas_call | solution.py:428
  277.9 74.2 %shard_map.162 = (f32[256,1536]{1,0:T(8,128)}, bf16[256,1536]{1,0:T(8,128)(2,1)}) custom-call(bf16[256,1536]{1,0:T(8,128)(2,1)} %get-tuple-element.25.u_ref, bf16[2,40,1536]{2,1,0:T(8,128)(2,1)} %bitcast.63, s32[8,256,8]{2,1,0:T(8,128)} %bitcast.55, f32[256,1536]{1,0:T(8,128)} %get-tuple-element.26.hidden_in, f32[5,1536]{1,0:T(8,128)} %gains_ref.9, ...), custom_call_target="tpu_custom_call" | custom-call | tf_op jit(solution)/shard_map/pallas_call | solution.py:518
  352.1 65.1 %shard_map.163 = (f32[8,256]{1,0:T(8,128)}, bf16[8,64,1536]{2,1,0:T(8,128)(2,1)}) custom-call(bf16[256,1536]{1,0:T(8,128)(2,1)} %get-tuple-element.27.f_ref, s32[8,1,256]{2,1,0:T(1,128)} %reshape.157.target_ref, bf16[6144,1536]{1,0:T(8,128)(2,1)} %embed_ref.3), custom_call_target="tpu_custom_call" | custom-call | tf_op jit(solution)/shard_map/pallas_call | solution.py:617
  417.3 0.8 reshape.158
  418.1 0.7 reshape.159
  418.7 42.0 %shard_map.164 = (f32[512,6144]{1,0:T(8,128)}, bf16[2048,64,128]{2,1,0:T(8,128)(2,1)}) custom-call(bf16[512,1536]{1,0:T(8,128)(2,1)} %bitcast.61, bf16[6144,1536]{1,0:T(8,128)(2,1)} %embed_ref.3, bf16[2048,64,128]{2,1,0:T(8,128)(2,1)} %bitcast.48), custom_call_target="tpu_custom_call" | custom-call | tf_op jit(solution)/shard_map/pallas_call | solution.py:639
  (9 shorter events, 0.1 us)

commit v4 on v3

--- a/solution.py
+++ b/solution.py
@@ -196,62 +196,102 @@
     return pltpu.CompilerParams(collective_id=ident, has_side_effects=True, vmem_limit_bytes=VMEM_LIMIT)
 
 
-def rows_kernel(count_ref, token_ref, row_ref, embed_ref, out_ref, buf, wide, sem):
-    wide[...] = jnp.zeros_like(wide)
-    count = count_ref[0]
-    slots = buf.shape[0]
+CAP = 64
+
+
+def pack_kernel(group_ref, place_ref, embed_ref, out_ref, buf, sem):
+    def issue(d, carry):
+        for j in range(CAP):
+            pltpu.make_async_copy(embed_ref.at[group_ref[d * CAP + j]], buf.at[d, j], sem.at[d]).start()
+        return carry
+
+    def place(d, carry):
+        pltpu.make_async_copy(embed_ref.at[0:CAP], buf.at[d], sem.at[d]).wait()
+        lane = lax.broadcasted_iota(jnp.int32, (CAP, 8 * CAP), 1)
+        one_hot = jnp.where(lane == place_ref[d], 1.0, 0.0).astype(BF16)
+        out_ref[d] = jnp.dot(one_hot, buf[d].reshape(8 * CAP, D), preferred_element_type=F32).astype(BF16)
+        return carry
+
+    lax.fori_loop(0, N, issue, 0)
+    lax.fori_loop(0, N, place, 0)
+
+
+def pack_rows(owned, embed):
+    group = lax.div(owned, 8).reshape(-1)
+    place = (8 * jnp.arange(CAP) + lax.rem(owned, 8)).reshape(N, CAP, 1)
+    return pl.pallas_call(
+        pack_kernel,
+        out_shape=jax.ShapeDtypeStruct((N, CAP, D), BF16),
+        grid_spec=pltpu.PrefetchScalarGridSpec(
+            num_scalar_prefetch=1, grid=(1,),
+            in_specs=[pl.BlockSpec((N, CAP, 1), lambda i, *_: (0, 0, 0)), ANY],
+            out_specs=pl.BlockSpec((N, CAP, D), lambda i, *_: (0, 0, 0)),
+            scratch_shapes=[pltpu.VMEM((N, CAP, 8, D), BF16), pltpu.SemaphoreType.DMA((N,))]),
+        compiler_params=pltpu.CompilerParams(vmem_limit_bytes=VMEM_LIMIT),
+    )(group, place, embed.reshape(VOCAB // 8, 8, D))
+
+
+def exchange_kernel(packed_ref, slot_ref, gains_ref, hidden_ref, normed_ref, held, send, recv):
+    me = lax.axis_index("tp")
+    barrier = pltpu.get_barrier_semaphore()
+    for shift in range(1, N):
+        pl.semaphore_signal(barrier, inc=1, device_id={"tp": lax.rem(me + shift, N)}, device_id_type=MESH)
+    pl.semaphore_wait(barrier, N - 1)
+
+    def copy(target, origin, shift):
+        return pltpu.make_async_remote_copy(
+            src_ref=packed_ref.at[target], dst_ref=held.at[origin], send_sem=send.at[shift], recv_sem=recv.at[shift],
+            device_id={"tp": target}, device_id_type=MESH)
+
+    for shift in range(1, N):
+        copy(lax.rem(me + shift, N), me, shift).start()
+    held[me] = packed_ref[me]
+    for shift in range(1, N):
+        copy(lax.rem(me + shift, N), lax.rem(me + N - shift, N), shift).wait()
 
     def chunk(c, carry):
-        base = c * slots
-        width = jnp.minimum(slots, count - base)
-
-        def issue(j, carry):
-            pltpu.make_async_copy(embed_ref.at[lax.div(row_ref[base + j], 8)], buf.at[j], sem).start()
-            return carry
-
-        def place(j, carry):
-            pltpu.make_async_copy(embed_ref.at[0], buf.at[j], sem).wait()
-            return carry
-
-        def move(i, carry):
-            for j in range(4):
-                spot = base + 4 * i + j
-                sub = lax.rem(row_ref[spot], 8)
-                block = buf[4 * i + j].astype(F32)
-                keep = lax.broadcasted_iota(jnp.int32, block.shape, 0) == sub
-                line = jnp.sum(jnp.where(keep, block, 0.0), axis=0, keepdims=True)
-                wide[pl.ds(token_ref[spot], 1), :] = line
-            return carry
-
-        lax.fori_loop(0, width, issue, 0)
-        lax.fori_loop(0, width, place, 0)
-        lax.fori_loop(0, lax.div(width + 3, 4), move, 0)
-        return carry
-
-    lax.fori_loop(0, lax.div(count + slots - 1, slots), chunk, 0)
-    out_ref[...] = wide[0:N * ROWS, :].astype(BF16)
-
-
-def local_rows(ids, shard, embed):
-    total = N * ROWS
+        rows = pl.ds(pl.multiple_of(c * 64, 64), 64)
+        lane = lax.broadcasted_iota(jnp.int32, (64, N * CAP), 1)
+        one_hot = jnp.where(lane == slot_ref[rows, :], 1.0, 0.0).astype(BF16)
+        hidden = EMBED_MULT * jnp.dot(one_hot, held[...].reshape(N * CAP, D), preferred_element_type=F32)
+        hidden_ref[rows, :] = hidden
+        mean_sq = jnp.mean(hidden * hidden, axis=1, keepdims=True)
+        normed_ref[rows, :] = (hidden * lax.rsqrt(mean_sq + NORM_EPS) * gains_ref[0:1, :]).astype(BF16)
+        return carry
+
+    lax.fori_loop(0, ROWS // 64, chunk, 0)
+
+
+def exchange_rows(packed, slot, gains, ident):
+    return pl.pallas_call(
+        exchange_kernel,
+        out_shape=RESIDUAL,
+        in_specs=[VM] * 3, out_specs=(VM, VM),
+        scratch_shapes=[pltpu.VMEM((N, CAP, D), BF16), pltpu.SemaphoreType.DMA((N,)), pltpu.SemaphoreType.DMA((N,))],
+        compiler_params=comm_params(ident),
+    )(packed, slot, gains)
+
+
+def embed_tokens(ids, shard, embed, gains):
+    owner = lax.div(ids, VOCAB)
+    earlier = jnp.arange(ROWS)[:, None] > jnp.arange(ROWS)[None, :]
+    rank = jnp.sum(((owner[:, :, None] == owner[:, None, :]) & earlier).astype(jnp.int32), axis=2)
     local = ids - shard * VOCAB
-    inside = (local >= 0) & (local < VOCAB)
-    rank = jnp.cumsum(inside.astype(jnp.int32)) - 1
-    rank = jnp.where(inside, rank, -1)
-    hit = rank[None, :] == jnp.arange(total)[:, None]
-    token = jnp.sum(jnp.where(hit, jnp.arange(total)[None, :] - total, 0), axis=1) + total
-    row = jnp.sum(jnp.where(hit, local[None, :], 0), axis=1)
-    count = jnp.sum(inside.astype(jnp.int32)).reshape(1)
-    return pl.pallas_call(
-        rows_kernel,
-        out_shape=jax.ShapeDtypeStruct((total, D), BF16),
-        grid_spec=pltpu.PrefetchScalarGridSpec(
-            num_scalar_prefetch=3, grid=(1,),
-            in_specs=[ANY],
-            out_specs=pl.BlockSpec((total, D), lambda i, *_: (0, 0)),
-            scratch_shapes=[pltpu.VMEM((256, 8, D), BF16), pltpu.VMEM((total + 8, D), F32), pltpu.SemaphoreType.DMA]),
-        compiler_params=pltpu.CompilerParams(vmem_limit_bytes=VMEM_LIMIT),
-    )(count, token, row, embed.reshape(VOCAB // 8, 8, D))
+
+    def packed(gains):
+        mine = jnp.where(owner == shard, rank, -1)
+        hit = mine[:, None, :] == jnp.arange(CAP)[None, :, None]
+        owned = jnp.sum(jnp.where(hit, local[:, None, :], 0), axis=2)
+        slot = lax.dynamic_index_in_dim(owner * CAP + rank, shard, 0, keepdims=False)
+        return exchange_rows(pack_rows(owned, embed), slot[:, None], gains, 0)
+
+    def general(gains):
+        flat = local.reshape(-1)
+        inside = (flat >= 0) & (flat < VOCAB)
+        rows = jnp.take(embed, jnp.clip(flat, 0, VOCAB - 1), axis=0)
+        return embed_sum(jnp.where(inside[:, None], rows, jnp.zeros_like(rows)), gains, 6)
+
+    return lax.cond(jnp.max(rank) < CAP, packed, general, gains)
 
 
 def embed_kernel(rows_ref, gains_ref, hidden_ref, normed_ref, acc, tbuf, rbuf, send, recv):
@@ -532,14 +572,21 @@
 LAST_TILE = 384
 
 
+LOG2E = 1.4426950408889634
+
+
 def fold(logits, column, target, stat):
-    part = (logits * (1.0 / LOGIT_DIV)).reshape(TILE // 8, 8, ROWS)
+    part = logits.reshape(TILE // 8, 8, ROWS)
     peak = stat[0]
     top = jnp.maximum(peak, jnp.max(part, axis=0))
-    row = 8 * lax.broadcasted_iota(jnp.int32, part.shape, 0) + lax.broadcasted_iota(jnp.int32, part.shape, 1)
     stat[0] = top
-    stat[1] = stat[1] * jnp.exp(peak - top) + jnp.sum(jnp.exp(part - top), axis=0)
-    stat[2] = stat[2] + jnp.sum(jnp.where(row == target - column, part, 0.0), axis=0)
+    stat[1] = stat[1] * jnp.exp2((peak - top) * (LOG2E / LOGIT_DIV)) + jnp.sum(
+        jnp.exp2((part - top) * (LOG2E / LOGIT_DIV)), axis=0)
+    here = target - column // 8 if isinstance(column, int) else target - lax.div(column, 8)
+    picked = stat[2]
+    for g in range(TILE // 8):
+        picked = jnp.where(here == g, part[g], picked)
+    stat[2] = picked
 
 
 def head_kernel(f_ref, target_ref, embed_ref, probs_ref, last_ref, ubuf, send, recv, table, even, odd, stat, mine, theirs,
@@ -559,6 +606,11 @@
     def tile_logits(blk, start):
         return lax.dot_general(table[pl.ds(start, TILE), :], ubuf[blk], (((1,), (1,)), ((), ())), preferred_element_type=F32)
 
+    def group_of(blk):
+        local = jnp.broadcast_to(target_ref[blk], (8, ROWS))
+        sub = lax.broadcasted_iota(jnp.int32, (8, ROWS), 0)
+        return jnp.where((local >= 0) & ((local & 7) == sub), local >> 3, -1 - VOCAB)
+
     def begin():
         stat[0] = jnp.full((8, ROWS), -1e30, F32)
         stat[1] = jnp.zeros((8, ROWS), F32)
@@ -568,14 +620,14 @@
         peak = stat[0]
         top = jnp.max(peak, axis=0, keepdims=True)
         mine[0, pl.ds(blk, 1), :] = top
-        mine[1, pl.ds(blk, 1), :] = jnp.sum(stat[1] * jnp.exp(peak - top), axis=0, keepdims=True)
+        mine[1, pl.ds(blk, 1), :] = jnp.sum(stat[1] * jnp.exp2((peak - top) * (LOG2E / LOGIT_DIV)), axis=0, keepdims=True)
         mine[2, pl.ds(blk, 1), :] = jnp.sum(stat[2], axis=0, keepdims=True)
         last_ref[blk] = ubuf[blk, ROWS - SEQS:ROWS, :]
 
     def first_tile(c, carry):
         load(c).wait()
         even[...] = tile_logits(at["me"], pl.multiple_of(c * TILE, TILE))
-        fold(even[...], c * TILE, target_ref[at["me"]], stat)
+        fold(even[...], c * TILE, group_of(at["me"]), stat)
         return carry
 
     begin()
@@ -585,7 +637,7 @@
     def body(pos, carry):
         gather.before(pos, ORDER_AG)
         blk = pick(pos, ORDER_AG, at)
-        target = target_ref[blk]
+        target = group_of(blk)
         begin()
         bufs = (even, odd)
         even[...] = tile_logits(blk, 0)
@@ -608,9 +660,9 @@
     for item in copies:
         item.wait()
     peak = functools.reduce(jnp.maximum, [theirs[i, 0] for i in range(N)])
-    total = sum(theirs[i, 1] * jnp.exp(theirs[i, 0] - peak) for i in range(N))
+    total = sum(theirs[i, 1] * jnp.exp2((theirs[i, 0] - peak) * (LOG2E / LOGIT_DIV)) for i in range(N))
     picked = sum(theirs[i, 2] for i in range(N))
-    probs_ref[...] = picked - peak - jnp.log(total)
+    probs_ref[...] = (picked - peak) * (1.0 / LOGIT_DIV) - jnp.log(total)
 
 
 def head(f, target, embed, ident):
@@ -626,22 +678,57 @@
     )(f, target, embed)
 
 
-def last_kernel(f_ref, embed_ref, cache_ref, logits_ref, new_ref):
+LAST_STEPS = VOCAB // LAST_TILE
+PLANES = LAYERS * 2 * BATCH // LAST_STEPS
+RING = 8
+AHEAD = 4
+
+
+def last_kernel(f_ref, embed_ref, cache_ref, logits_ref, new_ref, ring, in_sem, out_sem):
+    c = pl.program_id(0)
+
+    def load(i):
+        slot = lax.rem(i, RING)
+        return pltpu.make_async_copy(cache_ref.at[pl.ds(i * PLANES, PLANES)], ring.at[slot], in_sem.at[slot])
+
+    def store(i):
+        slot = lax.rem(i, RING)
+        return pltpu.make_async_copy(ring.at[slot], new_ref.at[pl.ds(i * PLANES, PLANES)], out_sem.at[slot])
+
+    @pl.when(c == 0)
+    def _():
+        for i in range(AHEAD):
+            load(jnp.int32(i)).start()
+
+    @pl.when((c >= RING - AHEAD) & (c < LAST_STEPS - AHEAD))
+    def _():
+        store(c + AHEAD - RING).wait()
+
+    @pl.when(c < LAST_STEPS - AHEAD)
+    def _():
+        load(c + AHEAD).start()
+
+    load(c).wait()
+    store(c).start()
     logits_ref[...] = lax.dot_general(f_ref[...], embed_ref[...], (((1,), (1,)), ((), ())),
                                       preferred_element_type=F32) * (1.0 / LOGIT_DIV)
-    new_ref[...] = cache_ref[...]
+
+    @pl.when(c == LAST_STEPS - 1)
+    def _():
+        for i in range(LAST_STEPS - RING, LAST_STEPS):
+            store(jnp.int32(i)).wait()
 
 
 def last_step(f, embed, cache):
-    steps = VOCAB // LAST_TILE
     flat = cache.reshape(LAYERS * 2 * BATCH, HEAD, CACHE)
-    plane_spec = pl.BlockSpec((flat.shape[0] // steps, HEAD, CACHE), lambda c: (c, 0, 0))
     logits, flat = pl.pallas_call(
         last_kernel,
         out_shape=(jax.ShapeDtypeStruct((BATCH, VOCAB), F32), jax.ShapeDtypeStruct(flat.shape, BF16)),
-        grid=(steps,),
-        in_specs=[pl.BlockSpec((BATCH, D), lambda c: (0, 0)), pl.BlockSpec((LAST_TILE, D), lambda c: (c, 0)), plane_spec],
-        out_specs=(pl.BlockSpec((BATCH, LAST_TILE), lambda c: (0, c)), plane_spec),
+        grid=(LAST_STEPS,),
+        in_specs=[pl.BlockSpec((BATCH, D), lambda c: (0, 0)), pl.BlockSpec((LAST_TILE, D), lambda c: (c, 0)), ANY],
+        out_specs=(pl.BlockSpec((BATCH, LAST_TILE), lambda c: (0, c)), ANY),
+        scratch_shapes=[pltpu.VMEM((RING, PLANES, HEAD, CACHE), BF16), pltpu.SemaphoreType.DMA((RING,)),
+                        pltpu.SemaphoreType.DMA((RING,))],
         compiler_params=pltpu.CompilerParams(dimension_semantics=("arbitrary",), vmem_limit_bytes=VMEM_LIMIT),
     )(f, embed, flat)
     return logits, flat.reshape(cache.shape)
@@ -661,16 +748,14 @@
         shard = lax.axis_index('tp')
         cache = kv_cache.transpose(0, 1, 2, 4, 5, 3).reshape(LAYERS, 2, BATCH, HEAD, CACHE)
 
-        ids = by_block(tokens[:, :STEPS]).reshape(-1)
-        rows = local_rows(ids, shard, embed)
-        hidden, normed = embed_sum(rows, norm_gain, 0)
+        ids = by_block(tokens[:, :STEPS]).reshape(N, ROWS)
+        hidden, normed = embed_tokens(ids, shard, embed, norm_gain)
 
         pos = by_block(start_pos[:, None] + jnp.arange(STEPS)[None, :]).reshape(N, ROWS)
         inv_freq = ROPE_THETA ** (-2.0 * jnp.arange(HEAD // 2, dtype=F32) / HEAD)
-        angles = pos.astype(F32)[:, :, None] * inv_freq
-        cos, sin = jnp.cos(angles), jnp.sin(angles)
-        cos = jnp.concatenate([cos] * 4, axis=-1)
-        sin = jnp.concatenate([-sin, sin, -sin, sin], axis=-1)
+        angles = pos.astype(F32)[:, :, None] * jnp.tile(inv_freq, 4)
+        cos = jnp.cos(angles)
+        sin = jnp.sin(angles) * jnp.where(jnp.arange(128) % HEAD < HEAD // 2, -1.0, 1.0)
         start_wide = jnp.broadcast_to(start_pos[:, None], (BATCH, 128))
 
         weights = [w.transpose(0, 2, 1) for w in (w_query, w_key, w_value)] + [w_out]

time: 470 us -> 436 us (0.928); the launches traced: 461 us -> 435 us
  Pallas kernels: 437 us -> 415 us
  other arithmetic: 14.4 us -> 9.38 us
    pallas_call x2, Pallas kernels: 54.3 us -> 40.6 us  [the longest x1 25.6 us: exchange_rows(): pl.pallas_call(exchange_kernel, out_shape=RESIDUAL, in_specs=[VM] * 3, ou...]
    pallas_call x1, Pallas kernels: 42 us -> 35 us  [last_step(): pl.pallas_call(last_kernel, out_shape=(jax.ShapeDtypeStruct((BATCH, VOCAB...]
    mul x0 -> x2, other arithmetic: none -> 5.51 us  [the longest x1 5.51 us: decode_local(): jnp.sin(angles) * jnp.where(jnp.arange(128) % HEAD < HEAD // 2, -1.0, 1.0)]
where the time goes in v4:
time: 436 us; the launch traced here: 435 us
  Pallas kernels  415 us (95%)
  other arithmetic  9.38 us (2%)
  local copies, waits for them, and re-layouts  9.03 us (2%)
    pallas_call x2, Pallas kernels, experts(): pl.pallas_call(functools.partial(moe_kernel, layer), out_shape=RESIDUAL,...  148 us
    pallas_call x2, Pallas kernels, attention(): pl.pallas_call(functools.partial(attn_kernel, layer), out_shape=RESIDUAL...  128 us
    pallas_call x1, Pallas kernels, head(): pl.pallas_call(head_kernel, out_shape=(jax.ShapeDtypeStruct((N, ROWS), F3...  63.1 us
    pallas_call x1, Pallas kernels, last_step(): pl.pallas_call(last_kernel, out_shape=(jax.ShapeDtypeStruct((BATCH, VOCAB...  35 us
    pallas_call x1, Pallas kernels, exchange_rows(): pl.pallas_call(exchange_kernel, out_shape=RESIDUAL, in_specs=[VM] * 3, ou...  25.6 us
    pallas_call x1, Pallas kernels, pack_rows(): pl.pallas_call(pack_kernel, out_shape=jax.ShapeDtypeStruct((N, CAP, D), B...  14.9 us

profile of v4, /device:TPU:0, one launch (start us, length us, event | category | flops | bytes accessed | tf_op | source)
XLA Modules:
  0.0 435.3 jit_solution(12621598211006361410)
XLA Ops:
  0.6 0.0 copy-start
  0.7 0.1 mul.42
  0.8 0.1 add.80
  0.9 0.8 add.76
  1.6 0.1 add.78
  1.7 0.8 slice_subtract_fusion
  2.5 0.1 reshape.218
  2.6 0.7 reshape.219.target_ref
  3.3 0.1 reshape.213
  3.4 0.1 reshape.214
  3.5 0.8 convert_reduce_fusion
  4.3 0.6 reduce_max.9
  5.6 1.5 broadcast_in_dim.67.start_ref
  7.1 1.0 reshape.216
  8.1 0.6 copy.40
  8.7 1.4 fusion.5
  10.2 5.5 %fusion.4 = (f32[8,256,128]{2,1,0:T(8,128)}, f32[8,256,128]{2,1,0:T(8,128)}) fusion(f32[128]{0:T(128)S(1)} %compare_select_fusion.3, f32[128]{0:T(128)S(1)} %mul.42, f32[8,256]{1,0:T(8,128)S(1)} %add_convert_fusion), kind=kLoop, calls=%fused_computation.26 | loop fusion | flops 524288 | bytes 2106368 | tf_op jit(solution)/shard_map/mul | solution.py:758
  15.7 0.0 copy-done
  15.7 43.4 %conditional.1 = ((f32[256,1536]{1,0:T(8,128)S(1)}, bf16[256,1536]{1,0:T(8,128)(2,1)S(1)})) conditional(s32[]{:T(128)} %convert_element_type.14, (s32[8,256]{1,0:T(8,128)S(1)}, bf16[6144,1536]{1,0:T(8,128)(2,1)}, f32[5,1536]{1,0:T(8,128)S(1)}) %tuple.27, (s32[8,256]{1,0:T(8,128)S(1)}, s32[]{:T(128)}, s32[8,256]{1,0:T(8,128)S(1)}, ...), branch_computations={%region_2.3_spmd, %region_3.0_spmd} | conditional | flops 6322176 | bytes 25255944 | solution.py:294
  15.7 0.2 select_reduce_fusion
  15.9 0.1 reduce_sum.13
  16.0 0.6 negate_select_fusion.2.group_ref
  16.6 0.8 copy.37.slot_ref
  17.4 0.1 copy.34
  17.5 0.8 fusion.1.place_ref
  18.3 14.9 %branch_1_fun.2.packed_ref = bf16[8,64,1536]{2,1,0:T(8,128)(2,1)} custom-call(s32[512]{0:T(512)} %negate_select_fusion.2.group_ref, s32[8,64,1]{2,1,0:T(8,128)} %fusion.1.place_ref, bf16[768,8,1536]{2,1,0:T(8,128)(2,1)} %bitcast.48), custom_call_target="tpu_custom_call" | custom-call | tf_op jit(solution)/shard_map/cond/branch_1_fun/pallas_call | solution.py:222
  33.3 25.6 %branch_1_fun.3 = (f32[256,1536]{1,0:T(8,128)S(1)}, bf16[256,1536]{1,0:T(8,128)(2,1)S(1)}) custom-call(bf16[8,64,1536]{2,1,0:T(8,128)(2,1)} %branch_1_fun.2.packed_ref, s32[256,1]{1,0:T(8,128)} %copy.37.slot_ref, f32[5,1536]{1,0:T(8,128)S(1)} %get-tuple-element.29.gains_ref), custom_call_target="tpu_custom_call" | custom-call | tf_op jit(solution)/shard_map/cond/branch_1_fun/pallas_call | solution.py:266
  59.1 64.1 %shard_map.157 = (f32[256,1536]{1,0:T(8,128)}, bf16[256,1536]{1,0:T(8,128)(2,1)}, bf16[2,2,512,64,128]{4,3,2,1,0:T(8,128)(2,1)}) custom-call(bf16[256,1536]{1,0:T(8,128)(2,1)S(1)} %get-tuple-element.48.u_ref, f32[8,256,128]{2,1,0:T(8,128)} %get-tuple-element.72.cos_ref, f32[8,256,128]{2,1,0:T(8,128)} %get-tuple-element.71.sin_ref, ...), custom_call_target="tpu_custom_call" | custom-call | tf_op jit(solution)/shard_map/pallas_call | solution.py:468
  123.2 74.3 %shard_map.158 = (f32[256,1536]{1,0:T(8,128)}, bf16[256,1536]{1,0:T(8,128)(2,1)}) custom-call(bf16[256,1536]{1,0:T(8,128)(2,1)} %get-tuple-element.50.u_ref, bf16[2,40,1536]{2,1,0:T(8,128)(2,1)} %bitcast.65, s32[8,256,8]{2,1,0:T(8,128)} %bitcast.59, f32[256,1536]{1,0:T(8,128)} %get-tuple-element.51.hidden_in, f32[5,1536]{1,0:T(8,128)S(1)} %copy-done, ...), custom_call_target="tpu_custom_call" | custom-call | tf_op jit(solution)/shard_map/pallas_call | solution.py:558
  197.5 63.8 %shard_map.159 = (f32[256,1536]{1,0:T(8,128)}, bf16[256,1536]{1,0:T(8,128)(2,1)}, bf16[2,2,512,64,128]{4,3,2,1,0:T(8,128)(2,1)}) custom-call(bf16[256,1536]{1,0:T(8,128)(2,1)} %get-tuple-element.52.u_ref, f32[8,256,128]{2,1,0:T(8,128)} %get-tuple-element.72.cos_ref, f32[8,256,128]{2,1,0:T(8,128)} %get-tuple-element.71.sin_ref, ...), custom_call_target="tpu_custom_call", output_to_operand_aliasing={{2}: (11, {})} | custom-call | tf_op jit(solution)/shard_map/pallas_call | solution.py:468
  261.3 74.2 %shard_map.160 = (f32[256,1536]{1,0:T(8,128)}, bf16[256,1536]{1,0:T(8,128)(2,1)}) custom-call(bf16[256,1536]{1,0:T(8,128)(2,1)} %get-tuple-element.55.u_ref, bf16[2,40,1536]{2,1,0:T(8,128)(2,1)} %bitcast.66, s32[8,256,8]{2,1,0:T(8,128)} %bitcast.58, f32[256,1536]{1,0:T(8,128)} %get-tuple-element.56.hidden_in, f32[5,1536]{1,0:T(8,128)S(1)} %copy-done, ...), custom_call_target="tpu_custom_call" | custom-call | tf_op jit(solution)/shard_map/pallas_call | solution.py:558
  335.5 63.1 %shard_map.161 = (f32[8,256]{1,0:T(8,128)}, bf16[8,64,1536]{2,1,0:T(8,128)(2,1)}) custom-call(bf16[256,1536]{1,0:T(8,128)(2,1)} %get-tuple-element.57.f_ref, s32[8,1,256]{2,1,0:T(1,128)} %reshape.219.target_ref, bf16[6144,1536]{1,0:T(8,128)(2,1)} %embed_ref.3), custom_call_target="tpu_custom_call" | custom-call | tf_op jit(solution)/shard_map/pallas_call | solution.py:669
  398.6 0.8 reshape.220
  399.4 0.7 reshape.221
  400.1 35.0 %shard_map.162 = (f32[512,6144]{1,0:T(8,128)}, bf16[2048,64,128]{2,1,0:T(8,128)(2,1)}) custom-call(bf16[512,1536]{1,0:T(8,128)(2,1)} %bitcast.64, bf16[6144,1536]{1,0:T(8,128)(2,1)} %embed_ref.3, bf16[2048,64,128]{2,1,0:T(8,128)(2,1)} %bitcast.51), custom_call_target="tpu_custom_call" | custom-call | tf_op jit(solution)/shard_map/pallas_call | solution.py:724
  (14 shorter events, 0.1 us)
Async XLA Ops:
  0.6 15.0 %copy-start = (f32[5,1536]{1,0:T(8,128)S(1)}, f32[5,1536]{1,0:T(8,128)}, u32[]{:S(2)}) copy-start(f32[5,1536]{1,0:T(8,128)} %gains_ref.7) | copy-start | bytes 92164

commit v5 on v4

--- a/solution.py
+++ b/solution.py
@@ -200,20 +200,32 @@
 
 
 def pack_kernel(group_ref, place_ref, embed_ref, out_ref, buf, sem):
-    def issue(d, carry):
+    def issue(d):
         for j in range(CAP):
             pltpu.make_async_copy(embed_ref.at[group_ref[d * CAP + j]], buf.at[d, j], sem.at[d]).start()
-        return carry
-
-    def place(d, carry):
+
+    def place(d):
         pltpu.make_async_copy(embed_ref.at[0:CAP], buf.at[d], sem.at[d]).wait()
         lane = lax.broadcasted_iota(jnp.int32, (CAP, 8 * CAP), 1)
         one_hot = jnp.where(lane == place_ref[d], 1.0, 0.0).astype(BF16)
         out_ref[d] = jnp.dot(one_hot, buf[d].reshape(8 * CAP, D), preferred_element_type=F32).astype(BF16)
-        return carry
-
-    lax.fori_loop(0, N, issue, 0)
-    lax.fori_loop(0, N, place, 0)
+
+    def body(d, carry):
+        issue(d + 2)
+        place(d)
+        return carry
+
+    def first(d, carry):
+        issue(d)
+        return carry
+
+    def last(d, carry):
+        place(d)
+        return carry
+
+    lax.fori_loop(0, 2, first, 0)
+    lax.fori_loop(0, N - 2, body, 0)
+    lax.fori_loop(N - 2, N, last, 0)
 
 
 def pack_rows(owned, embed):
@@ -379,12 +391,12 @@
             mixed_out[span, 128:256] = heads[2]
 
 
-def attn_kernel(layer, u_ref, cos_ref, sin_ref, start_ref, hidden_in, gains_ref, wq_ref, wk_ref, wv_ref, wo_ref, cache_ref,
+def attn_kernel(layer, u_ref, table_ref, start_ref, gains_ref, hidden_hbm, wq_ref, wk_ref, wv_ref, wo_ref, cache_ref,
                 *rest):
     if layer > 0:
         rest = rest[1:]
     (hidden_ref, normed_ref, new_ref, ubuf, ag_send, ag_recv, acc, tbuf, rbuf, rs_send, rs_recv,
-     qk, vv, mixed, planes, w_qkv, w_out, in_sem, out_sem, w_sem) = rest
+     qk, vv, mixed, planes, w_qkv, w_out, hidden_in, in_sem, out_sem, w_sem) = rest
     at = places()
     weights = [
         pltpu.make_async_copy(wq_ref.at[layer], w_qkv.at[0:192], w_sem.at[0]),
@@ -394,6 +406,8 @@
         pltpu.make_async_copy(wo_ref.at[layer], w_out.at[0:192], w_sem.at[4])]
     for item in weights:
         item.start()
+    residual = pltpu.make_async_copy(hidden_hbm, hidden_in, w_sem.at[5])
+    residual.start()
     w_out[192:256, :] = jnp.zeros((64, D), BF16)
 
     def plane_span(pos):
@@ -430,8 +444,12 @@
             load(pos + 2).start()
 
         out = lax.dot_general(ubuf[blk], w_qkv[...], (((1,), (1,)), ((), ())), preferred_element_type=F32)
-        cos = cos_ref[blk]
-        sin = sin_ref[blk]
+        start = start_ref[pl.ds(pl.multiple_of(blk * SEQS, SEQS), SEQS), :]
+        lane = lax.broadcasted_iota(jnp.int32, (SEQS, 128), 1)
+        hot = jnp.concatenate([jnp.where(lane == start + s, 1.0, 0.0) for s in range(STEPS)], axis=0)
+        turn = jnp.dot(hot, table_ref[...], precision=lax.Precision.HIGHEST, preferred_element_type=F32)
+        cos = turn[:, 0:128]
+        sin = turn[:, 128:256]
         low = lax.rem(lax.broadcasted_iota(jnp.int32, (ROWS, 128), 1), HEAD) < HEAD // 2
         for half in range(2):
             part = out[:, half * 128:(half + 1) * 128]
@@ -454,17 +472,18 @@
     store(jnp.int32(N - 2)).wait()
     store(jnp.int32(N - 1)).wait()
     gather.finish()
+    residual.wait()
     scatter.finish(acc, hidden_in, gains_ref[2 * layer + 1:2 * layer + 2, :], hidden_ref, normed_ref)
 
 
-def attention(layer, u, cos, sin, start_wide, hidden, gains, weights, cache, new_cache, ident):
-    args = [u, cos, sin, start_wide, hidden, gains, *weights, cache]
-    in_specs = [VM] * 6 + [ANY] * 5
+def attention(layer, u, table, start_wide, hidden, gains, weights, cache, new_cache, ident):
+    args = [u, table, start_wide, gains, hidden, *weights, cache]
+    in_specs = [VM] * 4 + [ANY] * 6
     aliases = {}
     if new_cache is not None:
         args.append(new_cache)
         in_specs.append(ANY)
-        aliases = {11: 2}
+        aliases = {10: 2}
     return pl.pallas_call(
         functools.partial(attn_kernel, layer),
         out_shape=RESIDUAL + (jax.ShapeDtypeStruct(cache.shape, BF16),),
@@ -472,14 +491,15 @@
         scratch_shapes=gather_scratch() + scatter_scratch() + [
             pltpu.VMEM((ROWS, 256), F32), pltpu.VMEM((ROWS, 128), F32), pltpu.VMEM((ROWS, 256), F32),
             pltpu.VMEM((SLOTS, 2, SEQS, HEAD, CACHE), BF16), pltpu.VMEM((384, D), BF16), pltpu.VMEM((256, D), BF16),
-            pltpu.SemaphoreType.DMA((SLOTS,)), pltpu.SemaphoreType.DMA((SLOTS,)), pltpu.SemaphoreType.DMA((5,))],
+            pltpu.VMEM((ROWS, D), F32), pltpu.SemaphoreType.DMA((SLOTS,)), pltpu.SemaphoreType.DMA((SLOTS,)),
+            pltpu.SemaphoreType.DMA((6,))],
         input_output_aliases=aliases,
         compiler_params=comm_params(ident),
     )(*args)
 
 
-def moe_kernel(layer, u_ref, router_ref, ids_ref, hidden_in, gains_ref, gate_hbm, up_hbm, down_hbm, hidden_ref, normed_ref,
-               ubuf, ag_send, ag_recv, acc, tbuf, rbuf, rs_send, rs_recv, gate_v, up_v, down_v, hidden, gates, w_sem):
+def moe_kernel(layer, u_ref, router_ref, ids_ref, gains_ref, hidden_hbm, gate_hbm, up_hbm, down_hbm, hidden_ref, normed_ref,
+               ubuf, ag_send, ag_recv, acc, tbuf, rbuf, rs_send, rs_recv, gate_v, up_v, down_v, hidden, gates, hidden_in, w_sem):
     def load(kind, e):
         src, dst = ((gate_hbm, gate_v), (up_hbm, up_v))[kind]
         return pltpu.make_async_copy(src.at[layer, e], dst.at[e], w_sem.at[kind, e])
@@ -489,6 +509,8 @@
         load(0, e).start()
         load(1, e).start()
     down_load.start()
+    residual = pltpu.make_async_copy(hidden_hbm, hidden_in, w_sem.at[2, 1])
+    residual.start()
     at = places()
     entry_barrier(at)
     gather = Gather(at, u_ref, ubuf, ag_send, ag_recv)
@@ -550,6 +572,7 @@
 
     lax.fori_loop(1, N, body, 0)
     gather.finish()
+    residual.wait()
     scatter.finish(acc, hidden_in, gains_ref[2 * layer + 2:2 * layer + 3, :], hidden_ref, normed_ref)
 
 
@@ -558,16 +581,17 @@
     return pl.pallas_call(
         functools.partial(moe_kernel, layer),
         out_shape=RESIDUAL,
-        in_specs=[VM] * 5 + [ANY] * 3, out_specs=(VM, VM),
+        in_specs=[VM] * 4 + [ANY] * 4, out_specs=(VM, VM),
         scratch_shapes=gather_scratch() + scatter_scratch() + [
             pltpu.VMEM((LOCAL_EXPERTS, D, FF), BF16), pltpu.VMEM((LOCAL_EXPERTS, D, FF), BF16),
             pltpu.VMEM((width, D), BF16), pltpu.VMEM((ROWS, width), BF16), pltpu.VMEM((ROWS, EXPERTS), F32),
+            pltpu.VMEM((ROWS, D), F32),
             pltpu.SemaphoreType.DMA((3, LOCAL_EXPERTS))],
         compiler_params=comm_params(ident),
-    )(u, router, ids, hidden, gains, w_gate, w_up, w_down.reshape(LAYERS, width, D))
-
-
-TILE = 1024
+    )(u, router, ids, gains, hidden, w_gate, w_up, w_down.reshape(LAYERS, width, D))
+
+
+TILE = 512
 TILES = VOCAB // TILE
 LAST_TILE = 384
 
@@ -624,14 +648,18 @@
         mine[2, pl.ds(blk, 1), :] = jnp.sum(stat[2], axis=0, keepdims=True)
         last_ref[blk] = ubuf[blk, ROWS - SEQS:ROWS, :]
 
-    def first_tile(c, carry):
-        load(c).wait()
-        even[...] = tile_logits(at["me"], pl.multiple_of(c * TILE, TILE))
-        fold(even[...], c * TILE, group_of(at["me"]), stat)
+    def first_tiles(i, carry):
+        group = group_of(at["me"])
+        bufs = (even, odd)
+        for j in range(2):
+            load(2 * i + j).wait()
+            bufs[j][...] = tile_logits(at["me"], pl.multiple_of((2 * i + j) * TILE, TILE))
+        for j in range(2):
+            fold(bufs[j][...], (2 * i + j) * TILE, group, stat)
         return carry
 
     begin()
-    lax.fori_loop(0, TILES, first_tile, 0)
+    lax.fori_loop(0, TILES // 2, first_tiles, 0)
     end(at["me"])
 
     def body(pos, carry):
@@ -751,11 +779,10 @@
         ids = by_block(tokens[:, :STEPS]).reshape(N, ROWS)
         hidden, normed = embed_tokens(ids, shard, embed, norm_gain)
 
-        pos = by_block(start_pos[:, None] + jnp.arange(STEPS)[None, :]).reshape(N, ROWS)
         inv_freq = ROPE_THETA ** (-2.0 * jnp.arange(HEAD // 2, dtype=F32) / HEAD)
-        angles = pos.astype(F32)[:, :, None] * jnp.tile(inv_freq, 4)
-        cos = jnp.cos(angles)
-        sin = jnp.sin(angles) * jnp.where(jnp.arange(128) % HEAD < HEAD // 2, -1.0, 1.0)
+        angles = jnp.arange(CACHE, dtype=F32)[:, None] * jnp.tile(inv_freq, 4)
+        sign = jnp.where(jnp.arange(128) % HEAD < HEAD // 2, -1.0, 1.0)
+        table = jnp.concatenate([jnp.cos(angles), jnp.sin(angles) * sign], axis=1)
         start_wide = jnp.broadcast_to(start_pos[:, None], (BATCH, 128))
 
         weights = [w.transpose(0, 2, 1) for w in (w_query, w_key, w_value)] + [w_out]
@@ -764,7 +791,7 @@
 
         new_cache = None
         for layer in range(LAYERS):
-            hidden, normed, new_cache = attention(layer, normed, cos, sin, start_wide, hidden, norm_gain, weights, cache, new_cache,
+            hidden, normed, new_cache = attention(layer, normed, table, start_wide, hidden, norm_gain, weights, cache, new_cache,
                                                   1 + 2 * layer)
             hidden, normed = experts(layer, normed, router, routed[layer], hidden, norm_gain, w_gate, w_up, w_down, 2 + 2 * layer)
 

time: 436 us -> 431 us (0.989)
  other arithmetic: 9.38 us -> 4.78 us
    mul x1 -> x0, other arithmetic: 5.51 us -> none  [decode_local(): jnp.sin(angles) * jnp.where(jnp.arange(128) % HEAD < HEAD // 2, -1.0, 1.0)]
where the time goes in v5:
time: 431 us; the launch traced here: 430 us
  Pallas kernels  415 us (96%)
  local copies, waits for them, and re-layouts  8.19 us (2%)
  other arithmetic  4.78 us (1%)
    pallas_call x2, Pallas kernels, experts(): pl.pallas_call(functools.partial(moe_kernel, layer), out_shape=RESIDUAL,...  147 us
    pallas_call x2, Pallas kernels, attention(): pl.pallas_call(functools.partial(attn_kernel, layer), out_shape=RESIDUAL...  126 us
    pallas_call x1, Pallas kernels, head(): pl.pallas_call(head_kernel, out_shape=(jax.ShapeDtypeStruct((N, ROWS), F3...  65.8 us
    pallas_call x1, Pallas kernels, last_step(): pl.pallas_call(last_kernel, out_shape=(jax.ShapeDtypeStruct((BATCH, VOCAB...  35 us
    pallas_call x1, Pallas kernels, exchange_rows(): pl.pallas_call(exchange_kernel, out_shape=RESIDUAL, in_specs=[VM] * 3, ou...  25.6 us
    pallas_call x1, Pallas kernels, pack_rows(): pl.pallas_call(pack_kernel, out_shape=jax.ShapeDtypeStruct((N, CAP, D), B...  15 us

profile of v5, /device:TPU:0, one launch (start us, length us, event | category | flops | bytes accessed | tf_op | source)
XLA Modules:
  0.0 429.9 jit_solution(3366511317102960782)
XLA Ops:
  0.6 0.0 copy-start
  0.7 0.1 mul.50
  0.8 0.8 slice_subtract_fusion
  1.6 0.1 reshape.195
  1.7 0.7 reshape.196.target_ref
  2.3 0.1 reshape.190
  2.4 0.1 reshape.191
  2.6 0.8 convert_reduce_fusion
  3.3 0.6 reduce_max.9
  4.6 0.3 fusion.4
  4.9 0.7 pad_maximum_fusion.table_ref
  5.6 1.5 broadcast_in_dim.65.start_ref
  7.1 1.0 reshape.193
  8.1 0.6 copy.40
  8.7 1.5 fusion.5
  10.2 0.0 copy-done
  10.2 43.4 %conditional.1 = ((f32[256,1536]{1,0:T(8,128)S(1)}, bf16[256,1536]{1,0:T(8,128)(2,1)S(1)})) conditional(s32[]{:T(128)} %convert_element_type.7, (s32[8,256]{1,0:T(8,128)S(1)}, bf16[6144,1536]{1,0:T(8,128)(2,1)}, f32[5,1536]{1,0:T(8,128)S(1)}) %tuple.27, (s32[8,256]{1,0:T(8,128)S(1)}, s32[]{:T(128)}, s32[8,256]{1,0:T(8,128)S(1)}, ...), branch_computations={%region_2.3_spmd, %region_3.0_spmd} | conditional | flops 6322176 | bytes 25255944 | solution.py:306
  10.3 0.2 select_reduce_fusion
  10.5 0.1 reduce_sum.13
  10.6 0.5 negate_select_fusion.2.group_ref
  11.1 0.8 copy.37.slot_ref
  11.9 0.1 copy.34
  12.1 0.8 fusion.1.place_ref
  12.9 15.0 %branch_1_fun.2.packed_ref = bf16[8,64,1536]{2,1,0:T(8,128)(2,1)} custom-call(s32[512]{0:T(512)} %negate_select_fusion.2.group_ref, s32[8,64,1]{2,1,0:T(8,128)} %fusion.1.place_ref, bf16[768,8,1536]{2,1,0:T(8,128)(2,1)} %bitcast.48), custom_call_target="tpu_custom_call" | custom-call | tf_op jit(solution)/shard_map/cond/branch_1_fun/pallas_call | solution.py:234
  27.9 25.6 %branch_1_fun.3 = (f32[256,1536]{1,0:T(8,128)S(1)}, bf16[256,1536]{1,0:T(8,128)(2,1)S(1)}) custom-call(bf16[8,64,1536]{2,1,0:T(8,128)(2,1)} %branch_1_fun.2.packed_ref, s32[256,1]{1,0:T(8,128)} %copy.37.slot_ref, f32[5,1536]{1,0:T(8,128)S(1)} %get-tuple-element.29.gains_ref), custom_call_target="tpu_custom_call" | custom-call | tf_op jit(solution)/shard_map/cond/branch_1_fun/pallas_call | solution.py:278
  53.7 63.7 %shard_map.157 = (f32[256,1536]{1,0:T(8,128)}, bf16[256,1536]{1,0:T(8,128)(2,1)}, bf16[2,2,512,64,128]{4,3,2,1,0:T(8,128)(2,1)}) custom-call(bf16[256,1536]{1,0:T(8,128)(2,1)S(1)} %get-tuple-element.48.u_ref, f32[128,256]{1,0:T(8,128)} %pad_maximum_fusion.table_ref, s32[512,128]{1,0:T(8,128)} %broadcast_in_dim.65.start_ref, f32[5,1536]{1,0:T(8,128)S(1)} %copy-done, ...), custom_call_target="tpu_custom_call" | custom-call | tf_op jit(solution)/shard_map/pallas_call | solution.py:487
  117.3 73.7 %shard_map.158 = (f32[256,1536]{1,0:T(8,128)}, bf16[256,1536]{1,0:T(8,128)(2,1)}) custom-call(bf16[256,1536]{1,0:T(8,128)(2,1)} %get-tuple-element.50.u_ref, bf16[2,40,1536]{2,1,0:T(8,128)(2,1)} %bitcast.65, s32[8,256,8]{2,1,0:T(8,128)} %bitcast.59, f32[5,1536]{1,0:T(8,128)S(1)} %copy-done, f32[256,1536]{1,0:T(8,128)} %get-tuple-element.51.hidden_hbm, ...), custom_call_target="tpu_custom_call" | custom-call | tf_op jit(solution)/shard_map/pallas_call | solution.py:581
  191.1 62.6 %shard_map.159 = (f32[256,1536]{1,0:T(8,128)}, bf16[256,1536]{1,0:T(8,128)(2,1)}, bf16[2,2,512,64,128]{4,3,2,1,0:T(8,128)(2,1)}) custom-call(bf16[256,1536]{1,0:T(8,128)(2,1)} %get-tuple-element.52.u_ref, f32[128,256]{1,0:T(8,128)} %pad_maximum_fusion.table_ref, s32[512,128]{1,0:T(8,128)} %broadcast_in_dim.65.start_ref, ...), custom_call_target="tpu_custom_call", output_to_operand_aliasing={{2}: (10, {})} | custom-call | tf_op jit(solution)/shard_map/pallas_call | solution.py:487
  253.7 73.7 %shard_map.160 = (f32[256,1536]{1,0:T(8,128)}, bf16[256,1536]{1,0:T(8,128)(2,1)}) custom-call(bf16[256,1536]{1,0:T(8,128)(2,1)} %get-tuple-element.55.u_ref, bf16[2,40,1536]{2,1,0:T(8,128)(2,1)} %bitcast.66, s32[8,256,8]{2,1,0:T(8,128)} %bitcast.58, f32[5,1536]{1,0:T(8,128)S(1)} %copy-done, f32[256,1536]{1,0:T(8,128)} %get-tuple-element.56.hidden_hbm, ...), custom_call_target="tpu_custom_call" | custom-call | tf_op jit(solution)/shard_map/pallas_call | solution.py:581
  327.5 65.8 %shard_map.161 = (f32[8,256]{1,0:T(8,128)}, bf16[8,64,1536]{2,1,0:T(8,128)(2,1)}) custom-call(bf16[256,1536]{1,0:T(8,128)(2,1)} %get-tuple-element.57.f_ref, s32[8,1,256]{2,1,0:T(1,128)} %reshape.196.target_ref, bf16[6144,1536]{1,0:T(8,128)(2,1)} %embed_ref.3), custom_call_target="tpu_custom_call" | custom-call | tf_op jit(solution)/shard_map/pallas_call | solution.py:697
  393.2 0.8 reshape.197
  394.0 0.7 reshape.198
  394.7 35.0 %shard_map.162 = (f32[512,6144]{1,0:T(8,128)}, bf16[2048,64,128]{2,1,0:T(8,128)(2,1)}) custom-call(bf16[512,1536]{1,0:T(8,128)(2,1)} %bitcast.60, bf16[6144,1536]{1,0:T(8,128)(2,1)} %embed_ref.3, bf16[2048,64,128]{2,1,0:T(8,128)(2,1)} %bitcast.51), custom_call_target="tpu_custom_call" | custom-call | tf_op jit(solution)/shard_map/pallas_call | solution.py:752
  (11 shorter events, 0.1 us)
Async XLA Ops:
  0.6 9.6 %copy-start = (f32[5,1536]{1,0:T(8,128)S(1)}, f32[5,1536]{1,0:T(8,128)}, u32[]{:S(2)}) copy-start(f32[5,1536]{1,0:T(8,128)} %gains_ref.7) | copy-start | bytes 92164

commit v6 on v5

--- a/solution.py
+++ b/solution.py
@@ -199,48 +199,52 @@
 CAP = 64
 
 
-def pack_kernel(group_ref, place_ref, embed_ref, out_ref, buf, sem):
-    def issue(d):
-        for j in range(CAP):
-            pltpu.make_async_copy(embed_ref.at[group_ref[d * CAP + j]], buf.at[d, j], sem.at[d]).start()
-
-    def place(d):
-        pltpu.make_async_copy(embed_ref.at[0:CAP], buf.at[d], sem.at[d]).wait()
+def pack_kernel(count_ref, group_ref, place_ref, embed_ref, out_ref, buf, sem):
+    def copy(group, d, j):
+        return pltpu.make_async_copy(embed_ref.at[group], buf.at[d, j], sem.at[d])
+
+    def issue(d, carry):
+        def eight(i, carry):
+            for j in range(8):
+                copy(group_ref[d * CAP + 8 * i + j], d, 8 * i + j).start()
+            return carry
+
+        lax.fori_loop(0, count_ref[d], eight, 0)
+        return carry
+
+    def place(d, carry):
+        def eight(i, carry):
+            pltpu.make_async_copy(embed_ref.at[0:8], buf.at[d, pl.ds(8 * i, 8)], sem.at[d]).wait()
+            return carry
+
+        def blank(i, carry):
+            buf[d, pl.ds(8 * i, 8)] = jnp.zeros((8, 8, D), BF16)
+            return carry
+
+        lax.fori_loop(count_ref[d], CAP // 8, blank, 0)
+        lax.fori_loop(0, count_ref[d], eight, 0)
         lane = lax.broadcasted_iota(jnp.int32, (CAP, 8 * CAP), 1)
         one_hot = jnp.where(lane == place_ref[d], 1.0, 0.0).astype(BF16)
         out_ref[d] = jnp.dot(one_hot, buf[d].reshape(8 * CAP, D), preferred_element_type=F32).astype(BF16)
-
-    def body(d, carry):
-        issue(d + 2)
-        place(d)
-        return carry
-
-    def first(d, carry):
-        issue(d)
-        return carry
-
-    def last(d, carry):
-        place(d)
-        return carry
-
-    lax.fori_loop(0, 2, first, 0)
-    lax.fori_loop(0, N - 2, body, 0)
-    lax.fori_loop(N - 2, N, last, 0)
-
-
-def pack_rows(owned, embed):
+        return carry
+
+    lax.fori_loop(0, N, issue, 0)
+    lax.fori_loop(0, N, place, 0)
+
+
+def pack_rows(count, owned, embed):
     group = lax.div(owned, 8).reshape(-1)
     place = (8 * jnp.arange(CAP) + lax.rem(owned, 8)).reshape(N, CAP, 1)
     return pl.pallas_call(
         pack_kernel,
         out_shape=jax.ShapeDtypeStruct((N, CAP, D), BF16),
         grid_spec=pltpu.PrefetchScalarGridSpec(
-            num_scalar_prefetch=1, grid=(1,),
+            num_scalar_prefetch=2, grid=(1,),
             in_specs=[pl.BlockSpec((N, CAP, 1), lambda i, *_: (0, 0, 0)), ANY],
             out_specs=pl.BlockSpec((N, CAP, D), lambda i, *_: (0, 0, 0)),
             scratch_shapes=[pltpu.VMEM((N, CAP, 8, D), BF16), pltpu.SemaphoreType.DMA((N,))]),
         compiler_params=pltpu.CompilerParams(vmem_limit_bytes=VMEM_LIMIT),
-    )(group, place, embed.reshape(VOCAB // 8, 8, D))
+    )(count, group, place, embed.reshape(VOCAB // 8, 8, D))
 
 
 def exchange_kernel(packed_ref, slot_ref, gains_ref, hidden_ref, normed_ref, held, send, recv):
@@ -295,7 +299,8 @@
         hit = mine[:, None, :] == jnp.arange(CAP)[None, :, None]
         owned = jnp.sum(jnp.where(hit, local[:, None, :], 0), axis=2)
         slot = lax.dynamic_index_in_dim(owner * CAP + rank, shard, 0, keepdims=False)
-        return exchange_rows(pack_rows(owned, embed), slot[:, None], gains, 0)
+        count = lax.div(jnp.max(mine, axis=1) + 8, 8)
+        return exchange_rows(pack_rows(count, owned, embed), slot[:, None], gains, 0)
 
     def general(gains):
         flat = local.reshape(-1)
@@ -535,14 +540,14 @@
 
     def activate(e, gate_act, up_act):
         share = jnp.sum(jnp.where(lane == at["me"] * LOCAL_EXPERTS + e, gates[...], 0.0), axis=1, keepdims=True)
-        z = gate_act * jax.nn.sigmoid(gate_act) * up_act * share
+        half = 0.5 * gate_act
+        z = (half * jnp.tanh(half) + half) * up_act * share
         start = e * FF if isinstance(e, int) else pl.multiple_of(e * FF, FF)
         hidden[:, pl.ds(start, FF)] = z.astype(BF16)
 
-    def down():
-        for c in range(D // 512):
-            cols = slice(c * 512, c * 512 + 512)
-            acc[:, cols] = jnp.dot(hidden[...], down_v[:, cols], preferred_element_type=F32)
+    def down(start):
+        cols = pl.ds(start, 512)
+        acc[:, cols] = jnp.dot(hidden[...], down_v[:, cols], preferred_element_type=F32)
 
     def first_expert(e, carry):
         load(0, e).wait()
@@ -554,7 +559,12 @@
     route(at["sib"])
     lax.fori_loop(0, LOCAL_EXPERTS, first_expert, 0)
     down_load.wait()
-    down()
+
+    def first_down(c, carry):
+        down(pl.multiple_of(c * 512, 512))
+        return carry
+
+    lax.fori_loop(0, D // 512, first_down, 0)
     scatter.after(jnp.int32(0), acc)
 
     def body(pos, carry):
@@ -566,7 +576,8 @@
             following = inner(blk, e + 1) if e + 1 < LOCAL_EXPERTS else None
             activate(e, *acts)
             acts = following
-        down()
+        for c in range(D // 512):
+            down(c * 512)
         scatter.after(pos, acc)
         return carry
 
@@ -591,12 +602,9 @@
     )(u, router, ids, gains, hidden, w_gate, w_up, w_down.reshape(LAYERS, width, D))
 
 
-TILE = 512
+TILE = 1024
 TILES = VOCAB // TILE
 LAST_TILE = 384
-
-
-LOG2E = 1.4426950408889634
 
 
 def fold(logits, column, target, stat):
@@ -604,8 +612,8 @@
     peak = stat[0]
     top = jnp.maximum(peak, jnp.max(part, axis=0))
     stat[0] = top
-    stat[1] = stat[1] * jnp.exp2((peak - top) * (LOG2E / LOGIT_DIV)) + jnp.sum(
-        jnp.exp2((part - top) * (LOG2E / LOGIT_DIV)), axis=0)
+    stat[1] = stat[1] * jnp.exp((peak - top) * (1.0 / LOGIT_DIV)) + jnp.sum(
+        jnp.exp((part - top) * (1.0 / LOGIT_DIV)), axis=0)
     here = target - column // 8 if isinstance(column, int) else target - lax.div(column, 8)
     picked = stat[2]
     for g in range(TILE // 8):
@@ -644,22 +652,18 @@
         peak = stat[0]
         top = jnp.max(peak, axis=0, keepdims=True)
         mine[0, pl.ds(blk, 1), :] = top
-        mine[1, pl.ds(blk, 1), :] = jnp.sum(stat[1] * jnp.exp2((peak - top) * (LOG2E / LOGIT_DIV)), axis=0, keepdims=True)
+        mine[1, pl.ds(blk, 1), :] = jnp.sum(stat[1] * jnp.exp((peak - top) * (1.0 / LOGIT_DIV)), axis=0, keepdims=True)
         mine[2, pl.ds(blk, 1), :] = jnp.sum(stat[2], axis=0, keepdims=True)
         last_ref[blk] = ubuf[blk, ROWS - SEQS:ROWS, :]
 
-    def first_tiles(i, carry):
-        group = group_of(at["me"])
-        bufs = (even, odd)
-        for j in range(2):
-            load(2 * i + j).wait()
-            bufs[j][...] = tile_logits(at["me"], pl.multiple_of((2 * i + j) * TILE, TILE))
-        for j in range(2):
-            fold(bufs[j][...], (2 * i + j) * TILE, group, stat)
+    def first_tile(c, carry):
+        load(c).wait()
+        even[...] = tile_logits(at["me"], pl.multiple_of(c * TILE, TILE))
+        fold(even[...], c * TILE, group_of(at["me"]), stat)
         return carry
 
     begin()
-    lax.fori_loop(0, TILES // 2, first_tiles, 0)
+    lax.fori_loop(0, TILES, first_tile, 0)
     end(at["me"])
 
     def body(pos, carry):
@@ -688,7 +692,7 @@
     for item in copies:
         item.wait()
     peak = functools.reduce(jnp.maximum, [theirs[i, 0] for i in range(N)])
-    total = sum(theirs[i, 1] * jnp.exp2((theirs[i, 0] - peak) * (LOG2E / LOGIT_DIV)) for i in range(N))
+    total = sum(theirs[i, 1] * jnp.exp((theirs[i, 0] - peak) * (1.0 / LOGIT_DIV)) for i in range(N))
     picked = sum(theirs[i, 2] for i in range(N))
     probs_ref[...] = (picked - peak) * (1.0 / LOGIT_DIV) - jnp.log(total)
 

time: 431 us -> 425 us (0.986)
  Pallas kernels: 415 us -> 409 us
    pallas_call x1, Pallas kernels: 15 us -> 8.12 us  [pack_rows(): pl.pallas_call(pack_kernel, out_shape=jax.ShapeDtypeStruct((N, CAP, D), B...]
where the time goes in v6:
time: 425 us
  Pallas kernels  409 us (96%)
  local copies, waits for them, and re-layouts  8.17 us (2%)
  other arithmetic  5.43 us (1%)
    pallas_call x2, Pallas kernels, experts(): pl.pallas_call(functools.partial(moe_kernel, layer), out_shape=RESIDUAL,...  150 us
    pallas_call x2, Pallas kernels, attention(): pl.pallas_call(functools.partial(attn_kernel, layer), out_shape=RESIDUAL...  126 us
    pallas_call x1, Pallas kernels, head(): pl.pallas_call(head_kernel, out_shape=(jax.ShapeDtypeStruct((N, ROWS), F3...  64.2 us
    pallas_call x1, Pallas kernels, last_step(): pl.pallas_call(last_kernel, out_shape=(jax.ShapeDtypeStruct((BATCH, VOCAB...  35 us
    pallas_call x1, Pallas kernels, exchange_rows(): pl.pallas_call(exchange_kernel, out_shape=RESIDUAL, in_specs=[VM] * 3, ou...  25.5 us

profile of v6, /device:TPU:0, one launch (start us, length us, event | category | flops | bytes accessed | tf_op | source)
XLA Modules:
  0.0 424.6 jit_solution(10828117730990333525)
XLA Ops:
  0.6 0.0 copy-start
  0.7 0.1 mul.50
  0.8 0.8 slice_subtract_fusion
  1.6 0.1 reshape.195
  1.7 0.7 reshape.196.target_ref
  2.3 0.1 reshape.190
  2.4 0.1 reshape.191
  2.6 0.8 convert_reduce_fusion
  3.3 0.6 reduce_max.18
  4.6 0.3 fusion.5
  4.9 0.7 pad_maximum_fusion.table_ref
  5.5 1.5 broadcast_in_dim.65.start_ref
  7.1 1.0 reshape.193
  8.1 0.6 copy.40
  8.7 1.5 fusion.7
  10.2 0.0 copy-done
  10.2 37.1 %conditional.1 = ((f32[256,1536]{1,0:T(8,128)S(1)}, bf16[256,1536]{1,0:T(8,128)(2,1)S(1)})) conditional(s32[]{:T(128)} %convert_element_type.7, (s32[8,256]{1,0:T(8,128)S(1)}, bf16[6144,1536]{1,0:T(8,128)(2,1)}, f32[5,1536]{1,0:T(8,128)S(1)}) %tuple.28, (s32[8,256]{1,0:T(8,128)S(1)}, s32[]{:T(128)}, s32[8,256]{1,0:T(8,128)S(1)}, ...), branch_computations={%region_2.3_spmd, %region_3.6_spmd} | conditional | flops 6322176 | bytes 25255944 | solution.py:311
  10.2 0.1 fusion.6
  10.4 0.2 select_reduce_fusion
  10.6 0.5 compare_select_fusion.1.count_ref
  11.1 0.1 reduce_sum.13
  11.2 0.6 negate_select_fusion.2.group_ref
  11.8 0.8 copy.37.slot_ref
  12.6 0.1 copy.34
  12.7 0.8 fusion.1.place_ref
  13.5 8.1 %branch_1_fun.2.packed_ref = bf16[8,64,1536]{2,1,0:T(8,128)(2,1)} custom-call(s32[8]{0:T(128)} %compare_select_fusion.1.count_ref, s32[512]{0:T(512)} %negate_select_fusion.2.group_ref, s32[8,64,1]{2,1,0:T(8,128)} %fusion.1.place_ref, bf16[768,8,1536]{2,1,0:T(8,128)(2,1)} %bitcast.48), custom_call_target="tpu_custom_call" | custom-call | tf_op jit(solution)/shard_map/cond/branch_1_fun/pallas_call | solution.py:238
  21.6 25.5 %branch_1_fun.3 = (f32[256,1536]{1,0:T(8,128)S(1)}, bf16[256,1536]{1,0:T(8,128)(2,1)S(1)}) custom-call(bf16[8,64,1536]{2,1,0:T(8,128)(2,1)} %branch_1_fun.2.packed_ref, s32[256,1]{1,0:T(8,128)} %copy.37.slot_ref, f32[5,1536]{1,0:T(8,128)S(1)} %get-tuple-element.29.gains_ref), custom_call_target="tpu_custom_call" | custom-call | tf_op jit(solution)/shard_map/cond/branch_1_fun/pallas_call | solution.py:282
  47.3 63.7 %shard_map.157 = (f32[256,1536]{1,0:T(8,128)}, bf16[256,1536]{1,0:T(8,128)(2,1)}, bf16[2,2,512,64,128]{4,3,2,1,0:T(8,128)(2,1)}) custom-call(bf16[256,1536]{1,0:T(8,128)(2,1)S(1)} %get-tuple-element.48.u_ref, f32[128,256]{1,0:T(8,128)} %pad_maximum_fusion.table_ref, s32[512,128]{1,0:T(8,128)} %broadcast_in_dim.65.start_ref, f32[5,1536]{1,0:T(8,128)S(1)} %copy-done, ...), custom_call_target="tpu_custom_call" | custom-call | tf_op jit(solution)/shard_map/pallas_call | solution.py:492
  111.0 75.0 %shard_map.158 = (f32[256,1536]{1,0:T(8,128)}, bf16[256,1536]{1,0:T(8,128)(2,1)}) custom-call(bf16[256,1536]{1,0:T(8,128)(2,1)} %get-tuple-element.50.u_ref, bf16[2,40,1536]{2,1,0:T(8,128)(2,1)} %bitcast.65, s32[8,256,8]{2,1,0:T(8,128)} %bitcast.59, f32[5,1536]{1,0:T(8,128)S(1)} %copy-done, f32[256,1536]{1,0:T(8,128)} %get-tuple-element.51.hidden_hbm, ...), custom_call_target="tpu_custom_call" | custom-call | tf_op jit(solution)/shard_map/pallas_call | solution.py:592
  186.0 62.6 %shard_map.159 = (f32[256,1536]{1,0:T(8,128)}, bf16[256,1536]{1,0:T(8,128)(2,1)}, bf16[2,2,512,64,128]{4,3,2,1,0:T(8,128)(2,1)}) custom-call(bf16[256,1536]{1,0:T(8,128)(2,1)} %get-tuple-element.52.u_ref, f32[128,256]{1,0:T(8,128)} %pad_maximum_fusion.table_ref, s32[512,128]{1,0:T(8,128)} %broadcast_in_dim.65.start_ref, ...), custom_call_target="tpu_custom_call", output_to_operand_aliasing={{2}: (10, {})} | custom-call | tf_op jit(solution)/shard_map/pallas_call | solution.py:492
  248.7 75.0 %shard_map.160 = (f32[256,1536]{1,0:T(8,128)}, bf16[256,1536]{1,0:T(8,128)(2,1)}) custom-call(bf16[256,1536]{1,0:T(8,128)(2,1)} %get-tuple-element.55.u_ref, bf16[2,40,1536]{2,1,0:T(8,128)(2,1)} %bitcast.66, s32[8,256,8]{2,1,0:T(8,128)} %bitcast.58, f32[5,1536]{1,0:T(8,128)S(1)} %copy-done, f32[256,1536]{1,0:T(8,128)} %get-tuple-element.56.hidden_hbm, ...), custom_call_target="tpu_custom_call" | custom-call | tf_op jit(solution)/shard_map/pallas_call | solution.py:592
  323.7 64.2 %shard_map.161 = (f32[8,256]{1,0:T(8,128)}, bf16[8,64,1536]{2,1,0:T(8,128)(2,1)}) custom-call(bf16[256,1536]{1,0:T(8,128)(2,1)} %get-tuple-element.57.f_ref, s32[8,1,256]{2,1,0:T(1,128)} %reshape.196.target_ref, bf16[6144,1536]{1,0:T(8,128)(2,1)} %embed_ref.3), custom_call_target="tpu_custom_call" | custom-call | tf_op jit(solution)/shard_map/pallas_call | solution.py:701
  387.9 0.8 reshape.197
  388.7 0.7 reshape.198
  389.4 35.0 %shard_map.162 = (f32[512,6144]{1,0:T(8,128)}, bf16[2048,64,128]{2,1,0:T(8,128)(2,1)}) custom-call(bf16[512,1536]{1,0:T(8,128)(2,1)} %bitcast.60, bf16[6144,1536]{1,0:T(8,128)(2,1)} %embed_ref.3, bf16[2048,64,128]{2,1,0:T(8,128)(2,1)} %bitcast.51), custom_call_target="tpu_custom_call" | custom-call | tf_op jit(solution)/shard_map/pallas_call | solution.py:756
  (10 shorter events, 0.1 us)
Async XLA Ops:
  0.6 9.6 %copy-start = (f32[5,1536]{1,0:T(8,128)S(1)}, f32[5,1536]{1,0:T(8,128)}, u32[]{:S(2)}) copy-start(f32[5,1536]{1,0:T(8,128)} %gains_ref.7) | copy-start | bytes 92164

commit v7 on v6

--- a/solution.py
+++ b/solution.py
@@ -540,8 +540,7 @@
 
     def activate(e, gate_act, up_act):
         share = jnp.sum(jnp.where(lane == at["me"] * LOCAL_EXPERTS + e, gates[...], 0.0), axis=1, keepdims=True)
-        half = 0.5 * gate_act
-        z = (half * jnp.tanh(half) + half) * up_act * share
+        z = gate_act * jax.nn.sigmoid(gate_act) * up_act * share
         start = e * FF if isinstance(e, int) else pl.multiple_of(e * FF, FF)
         hidden[:, pl.ds(start, FF)] = z.astype(BF16)
 
@@ -621,7 +620,7 @@
     stat[2] = picked
 
 
-def head_kernel(f_ref, target_ref, embed_ref, probs_ref, last_ref, ubuf, send, recv, table, even, odd, stat, mine, theirs,
+def head_kernel(f_ref, target_ref, embed_ref, probs_ref, last_ref, ubuf, send, recv, table, tile_ref, stat, mine, theirs,
                 share_send, share_recv, sem):
     def load(c):
         rows = pl.ds(pl.multiple_of(c * TILE, TILE), TILE)
@@ -658,8 +657,8 @@
 
     def first_tile(c, carry):
         load(c).wait()
-        even[...] = tile_logits(at["me"], pl.multiple_of(c * TILE, TILE))
-        fold(even[...], c * TILE, group_of(at["me"]), stat)
+        tile_ref[...] = tile_logits(at["me"], pl.multiple_of(c * TILE, TILE))
+        fold(tile_ref[...], c * TILE, group_of(at["me"]), stat)
         return carry
 
     begin()
@@ -671,12 +670,11 @@
         blk = pick(pos, ORDER_AG, at)
         target = group_of(blk)
         begin()
-        bufs = (even, odd)
-        even[...] = tile_logits(blk, 0)
-        for c in range(1, TILES + 1):
-            if c < TILES:
-                bufs[c % 2][...] = tile_logits(blk, c * TILE)
-            fold(bufs[(c - 1) % 2][...], (c - 1) * TILE, target, stat)
+        tile = tile_logits(blk, 0)
+        for c in range(TILES):
+            following = tile_logits(blk, (c + 1) * TILE) if c + 1 < TILES else None
+            fold(tile, c * TILE, target, stat)
+            tile = following
         end(blk)
         return carry
 
@@ -703,7 +701,7 @@
         out_shape=(jax.ShapeDtypeStruct((N, ROWS), F32), jax.ShapeDtypeStruct((N, SEQS, D), BF16)),
         in_specs=[VM, VM, ANY], out_specs=(VM, VM),
         scratch_shapes=gather_scratch() + [
-            pltpu.VMEM((VOCAB, D), BF16), pltpu.VMEM((TILE, ROWS), F32), pltpu.VMEM((TILE, ROWS), F32),
+            pltpu.VMEM((VOCAB, D), BF16), pltpu.VMEM((TILE, ROWS), F32),
             pltpu.VMEM((3, 8, ROWS), F32), pltpu.VMEM((3, N, ROWS), F32), pltpu.VMEM((N, 3, N, ROWS), F32),
             pltpu.SemaphoreType.DMA((N,)), pltpu.SemaphoreType.DMA((N,)), pltpu.SemaphoreType.DMA((TILES,))],
         compiler_params=comm_params(ident),

time: 425 us -> 424 us (level)
  no operation moved by 1% of the time
where the time goes in v7:
time: 424 us
  Pallas kernels  408 us (96%)
  local copies, waits for them, and re-layouts  8.17 us (2%)
  other arithmetic  5.43 us (1%)
    pallas_call x2, Pallas kernels, experts(): pl.pallas_call(functools.partial(moe_kernel, layer), out_shape=RESIDUAL,...  148 us
    pallas_call x2, Pallas kernels, attention(): pl.pallas_call(functools.partial(attn_kernel, layer), out_shape=RESIDUAL...  126 us
    pallas_call x1, Pallas kernels, head(): pl.pallas_call(head_kernel, out_shape=(jax.ShapeDtypeStruct((N, ROWS), F3...  65 us
    pallas_call x1, Pallas kernels, last_step(): pl.pallas_call(last_kernel, out_shape=(jax.ShapeDtypeStruct((BATCH, VOCAB...  35 us
    pallas_call x1, Pallas kernels, exchange_rows(): pl.pallas_call(exchange_kernel, out_shape=RESIDUAL, in_specs=[VM] * 3, ou...  25.6 us

profile of v7, /device:TPU:0, one launch (start us, length us, event | category | flops | bytes accessed | tf_op | source)
XLA Modules:
  0.0 423.6 jit_solution(223612812793849973)
XLA Ops:
  0.6 0.0 copy-start
  0.7 0.1 mul.50
  0.8 0.8 slice_subtract_fusion
  1.6 0.1 reshape.195
  1.7 0.7 reshape.196.target_ref
  2.3 0.1 reshape.190
  2.4 0.1 reshape.191
  2.6 0.8 convert_reduce_fusion
  3.3 0.6 reduce_max.18
  4.6 0.3 fusion.5
  4.9 0.7 pad_maximum_fusion.table_ref
  5.5 1.5 broadcast_in_dim.65.start_ref
  7.1 1.0 reshape.193
  8.1 0.6 copy.40
  8.7 1.5 fusion.7
  10.2 0.0 copy-done
  10.2 37.1 %conditional.1 = ((f32[256,1536]{1,0:T(8,128)S(1)}, bf16[256,1536]{1,0:T(8,128)(2,1)S(1)})) conditional(s32[]{:T(128)} %convert_element_type.7, (s32[8,256]{1,0:T(8,128)S(1)}, bf16[6144,1536]{1,0:T(8,128)(2,1)}, f32[5,1536]{1,0:T(8,128)S(1)}) %tuple.28, (s32[8,256]{1,0:T(8,128)S(1)}, s32[]{:T(128)}, s32[8,256]{1,0:T(8,128)S(1)}, ...), branch_computations={%region_2.3_spmd, %region_3.6_spmd} | conditional | flops 6322176 | bytes 25255944 | solution.py:311
  10.2 0.1 fusion.6
  10.4 0.2 select_reduce_fusion
  10.6 0.5 compare_select_fusion.1.count_ref
  11.1 0.1 reduce_sum.13
  11.2 0.6 negate_select_fusion.2.group_ref
  11.8 0.8 copy.37.slot_ref
  12.6 0.1 copy.34
  12.7 0.8 fusion.1.place_ref
  13.5 8.0 %branch_1_fun.2.packed_ref = bf16[8,64,1536]{2,1,0:T(8,128)(2,1)} custom-call(s32[8]{0:T(128)} %compare_select_fusion.1.count_ref, s32[512]{0:T(512)} %negate_select_fusion.2.group_ref, s32[8,64,1]{2,1,0:T(8,128)} %fusion.1.place_ref, bf16[768,8,1536]{2,1,0:T(8,128)(2,1)} %bitcast.48), custom_call_target="tpu_custom_call" | custom-call | tf_op jit(solution)/shard_map/cond/branch_1_fun/pallas_call | solution.py:238
  21.5 25.6 %branch_1_fun.3 = (f32[256,1536]{1,0:T(8,128)S(1)}, bf16[256,1536]{1,0:T(8,128)(2,1)S(1)}) custom-call(bf16[8,64,1536]{2,1,0:T(8,128)(2,1)} %branch_1_fun.2.packed_ref, s32[256,1]{1,0:T(8,128)} %copy.37.slot_ref, f32[5,1536]{1,0:T(8,128)S(1)} %get-tuple-element.29.gains_ref), custom_call_target="tpu_custom_call" | custom-call | tf_op jit(solution)/shard_map/cond/branch_1_fun/pallas_call | solution.py:282
  47.3 63.7 %shard_map.157 = (f32[256,1536]{1,0:T(8,128)}, bf16[256,1536]{1,0:T(8,128)(2,1)}, bf16[2,2,512,64,128]{4,3,2,1,0:T(8,128)(2,1)}) custom-call(bf16[256,1536]{1,0:T(8,128)(2,1)S(1)} %get-tuple-element.48.u_ref, f32[128,256]{1,0:T(8,128)} %pad_maximum_fusion.table_ref, s32[512,128]{1,0:T(8,128)} %broadcast_in_dim.65.start_ref, f32[5,1536]{1,0:T(8,128)S(1)} %copy-done, ...), custom_call_target="tpu_custom_call" | custom-call | tf_op jit(solution)/shard_map/pallas_call | solution.py:492
  111.0 74.1 %shard_map.158 = (f32[256,1536]{1,0:T(8,128)}, bf16[256,1536]{1,0:T(8,128)(2,1)}) custom-call(bf16[256,1536]{1,0:T(8,128)(2,1)} %get-tuple-element.50.u_ref, bf16[2,40,1536]{2,1,0:T(8,128)(2,1)} %bitcast.65, s32[8,256,8]{2,1,0:T(8,128)} %bitcast.59, f32[5,1536]{1,0:T(8,128)S(1)} %copy-done, f32[256,1536]{1,0:T(8,128)} %get-tuple-element.51.hidden_hbm, ...), custom_call_target="tpu_custom_call" | custom-call | tf_op jit(solution)/shard_map/pallas_call | solution.py:591
  185.2 62.6 %shard_map.159 = (f32[256,1536]{1,0:T(8,128)}, bf16[256,1536]{1,0:T(8,128)(2,1)}, bf16[2,2,512,64,128]{4,3,2,1,0:T(8,128)(2,1)}) custom-call(bf16[256,1536]{1,0:T(8,128)(2,1)} %get-tuple-element.52.u_ref, f32[128,256]{1,0:T(8,128)} %pad_maximum_fusion.table_ref, s32[512,128]{1,0:T(8,128)} %broadcast_in_dim.65.start_ref, ...), custom_call_target="tpu_custom_call", output_to_operand_aliasing={{2}: (10, {})} | custom-call | tf_op jit(solution)/shard_map/pallas_call | solution.py:492
  247.8 74.1 %shard_map.160 = (f32[256,1536]{1,0:T(8,128)}, bf16[256,1536]{1,0:T(8,128)(2,1)}) custom-call(bf16[256,1536]{1,0:T(8,128)(2,1)} %get-tuple-element.55.u_ref, bf16[2,40,1536]{2,1,0:T(8,128)(2,1)} %bitcast.66, s32[8,256,8]{2,1,0:T(8,128)} %bitcast.58, f32[5,1536]{1,0:T(8,128)S(1)} %copy-done, f32[256,1536]{1,0:T(8,128)} %get-tuple-element.56.hidden_hbm, ...), custom_call_target="tpu_custom_call" | custom-call | tf_op jit(solution)/shard_map/pallas_call | solution.py:591
  321.9 65.0 %shard_map.161 = (f32[8,256]{1,0:T(8,128)}, bf16[8,64,1536]{2,1,0:T(8,128)(2,1)}) custom-call(bf16[256,1536]{1,0:T(8,128)(2,1)} %get-tuple-element.57.f_ref, s32[8,1,256]{2,1,0:T(1,128)} %reshape.196.target_ref, bf16[6144,1536]{1,0:T(8,128)(2,1)} %embed_ref.3), custom_call_target="tpu_custom_call" | custom-call | tf_op jit(solution)/shard_map/pallas_call | solution.py:699
  386.9 0.8 reshape.197
  387.7 0.7 reshape.198
  388.4 35.0 %shard_map.162 = (f32[512,6144]{1,0:T(8,128)}, bf16[2048,64,128]{2,1,0:T(8,128)(2,1)}) custom-call(bf16[512,1536]{1,0:T(8,128)(2,1)} %bitcast.60, bf16[6144,1536]{1,0:T(8,128)(2,1)} %embed_ref.3, bf16[2048,64,128]{2,1,0:T(8,128)(2,1)} %bitcast.51), custom_call_target="tpu_custom_call" | custom-call | tf_op jit(solution)/shard_map/pallas_call | solution.py:754
  (10 shorter events, 0.1 us)
Async XLA Ops:
  0.6 9.6 %copy-start = (f32[5,1536]{1,0:T(8,128)S(1)}, f32[5,1536]{1,0:T(8,128)}, u32[]{:S(2)}) copy-start(f32[5,1536]{1,0:T(8,128)} %gains_ref.7) | copy-start | bytes 92164
